TPU v7x, 32 devices: a whole 2x2x4 slice. The times are simulated.
32 devices in a mesh: shard: 16 (over z, y, x), replica: 2 (over core).
Axes of the slice: x: 2, y: 2, z: 4, core: 2. Of those that a mesh axis runs over, the one named last changes fastest.
Arguments:
- request_rows: int32 [2, 16, 128], P('replica', 'shard'), may hold values from 0 to 1023, as said below
- token_slot: int32 [2, 2048], P('replica', 'shard'), may hold values from 0 to 127, as said below
- seq_lengths: int32 [2, 16, 8], P('replica', 'shard'), may hold values from 1 to 48, 128 in all within a row
- cotangent: bfloat16 [2, 2048, 256], P('replica', 'shard'), may hold values from -6 to 6
- table_slab: float32 [16384, 256], P('shard'), may hold values from -6 to 6
- adagrad_state: float32 [16384], P('shard'), may hold values from 0.1 to 1
- w_uvqk: bfloat16 [256, 1024], replicated, may hold values from -0.375 to 0.375
- w_out: bfloat16 [256, 256], replicated, may hold values from -0.375 to 0.375
- norm_gain: float32 [256], replicated, may hold values from 0.1 to 1.9
- out_gain: float32 [256], replicated, may hold values from 0.1 to 1.9
Outputs:
- row_update: float32 [16384, 256], P('shard')
- state_new: float32 [16384], P('shard')
- grad_uvqk: float32 [256, 1024], replicated
- grad_out: float32 [256, 256], replicated
- grad_gains: float32 [2, 256], replicated
Inputs may be any that keep to these rules, and one draw needn't show every extreme that they name: `request_rows`: on each device the rows asked of one owner (slots j with one value of j // 8) are distinct. `token_slot`: each token names one slot of its own device. For each owner the named slots are the first ones of its 8 slots, every such slot is named by some token, and on every device some owner has all 8 slots named. Slots that no token names still ask for a row (each a distinct one); their gradient is zero. `seq_lengths`: the lengths of one device sum to 128; the longest is exactly 48.
All inputs are finite; a program needn't handle non-finite values.
Results may differ from a plain program's by a relative error of at most 0.014.
Values may be sent and summed in bfloat16 or wider, within the bound.
No kernel may reach another device: no remote copies, remote signals or barrier semaphores. Data moves between devices by JAX's collectives and lax.ppermute only.
A program may use at most 64 MiB of HBM per device.

v0:
```python
import jax
import jax.numpy as jnp
from jax import lax
from jax.sharding import PartitionSpec as P

HEADS = 4
MAXLEN = 48


epsilon = 1e-08
learn_rate = 0.5


def normalize(values):
    center = values - jnp.mean(values, axis=1, keepdims=True)
    variance = jnp.mean(center * center, axis=1, keepdims=True)
    return center * lax.rsqrt(variance + 1e-05)


def same_sequence(lengths, count):
    seq_ends = jnp.cumsum(lengths)
    positions = jnp.arange(count, dtype=jnp.int32)
    segment = jnp.sum(positions[:, None] >= seq_ends[None, :], axis=1)
    return (segment[:, None] == segment[None, :]) & (positions[:, None] >= positions[None, :])


def hstu_layer(embedded, w_uvqk, w_out, norm_gain, out_gain, same_seq):
    count = embedded.shape[0]
    model_width = embedded.shape[1]
    head_width = model_width // HEADS
    normed = (normalize(embedded) * norm_gain).astype(jnp.bfloat16)
    projected = jax.nn.silu(jnp.dot(normed, w_uvqk, preferred_element_type=jnp.float32))
    gate_u = projected[:, :model_width]
    packed = projected[:, model_width:].astype(jnp.bfloat16).reshape(count, 3, HEADS, head_width)
    values = packed[:, 0]
    queries = packed[:, 1]
    key_rows = packed[:, 2]
    scores = jnp.einsum(
        "qhd,khd->hqk", queries, key_rows, preferred_element_type=jnp.float32
    ) * head_width ** (-0.5)
    weights = jnp.where(same_seq[None], jax.nn.silu(scores) / MAXLEN, 0.0).astype(jnp.bfloat16)
    attended = jnp.einsum(
        "hqk,khd->qhd", weights, values, preferred_element_type=jnp.float32
    ).reshape(count, model_width)
    gated = (normalize(attended) * out_gain * gate_u).astype(jnp.bfloat16)
    return embedded + jnp.dot(gated, w_out, preferred_element_type=jnp.float32)


def on_device(
    request_rows,
    token_slot,
    seq_lengths,
    cotangent,
    table_slab,
    adagrad_state,
    w_uvqk,
    w_out,
    norm_gain,
    out_gain,
):
    shards = lax.axis_size("shard")
    replicas = lax.axis_size("replica")
    tokens = token_slot.shape[1]
    model_width = table_slab.shape[1]
    rows_dev = table_slab.shape[0]
    capacity = tokens // shards
    asked_rows = request_rows.reshape(shards, capacity)
    wanted = lax.all_to_all(asked_rows, "shard", split_axis=0, concat_axis=0, tiled=True)
    found_rows = jnp.take(table_slab, wanted, axis=0).astype(jnp.bfloat16)
    returned = lax.all_to_all(found_rows, "shard", split_axis=0, concat_axis=0, tiled=True)
    returned, wanted = (returned, wanted)
    slot_rows = returned.reshape(tokens, model_width)
    slot_ids = token_slot[0]
    embedded = jnp.take(slot_rows, slot_ids, axis=0).astype(jnp.float32)
    same_seq = same_sequence(seq_lengths.reshape(-1), tokens)

    def local_layer(first, second, third, fourth, fifth):
        return hstu_layer(first, second, third, fourth, fifth, same_seq)

    unused, pullback = jax.vjp(local_layer, embedded, w_uvqk, w_out, norm_gain, out_gain)
    token_grad, grad_one, grad_two, grad_norm, grad_gate = pullback(
        cotangent[0].astype(jnp.float32)
    )
    slot_grad = jax.ops.segment_sum(token_grad, slot_ids, num_segments=tokens)
    arrived = lax.all_to_all(
        slot_grad.reshape(shards, capacity, model_width).astype(jnp.bfloat16),
        "shard",
        split_axis=0,
        concat_axis=0,
        tiled=True,
    ).astype(jnp.float32)
    row_grads = jax.ops.segment_sum(
        arrived.reshape(-1, model_width), wanted.reshape(-1), num_segments=rows_dev
    )
    mean_square = jnp.mean(row_grads * row_grads, axis=1)
    row_delta = -learn_rate * row_grads / jnp.sqrt(adagrad_state + mean_square + epsilon)[:, None]
    share_rows = rows_dev // replicas
    delta_share, square_share = (
        lax.psum_scatter(
            row_delta.astype(jnp.bfloat16), "replica", scatter_dimension=0, tiled=True
        ).astype(jnp.float32),
        lax.psum_scatter(
            mean_square.astype(jnp.bfloat16), "replica", scatter_dimension=0, tiled=True
        ).astype(jnp.float32),
    )
    state_share = lax.dynamic_slice_in_dim(
        adagrad_state, lax.axis_index("replica") * share_rows, share_rows, 0
    )
    row_update, state_new = (
        lax.all_gather(
            (delta_share / replicas).astype(jnp.bfloat16), "replica", axis=0, tiled=True
        ).astype(jnp.float32),
        lax.all_gather(
            (state_share + square_share / replicas).astype(jnp.bfloat16),
            "replica",
            axis=0,
            tiled=True,
        ).astype(jnp.float32),
    )
    grad_scale = 1.0 / jnp.sqrt(jnp.float32(tokens * shards * replicas))
    dense_terms = (
        grad_one.astype(jnp.float32) * grad_scale,
        grad_two.astype(jnp.float32) * grad_scale,
        jnp.stack([grad_norm, grad_gate]) * grad_scale,
    )
    grad_uvqk, grad_out, grad_gains = lax.psum(
        (dense_terms[0], dense_terms[1], dense_terms[2]), ("shard", "replica")
    )
    return (row_update, state_new, grad_uvqk, grad_out, grad_gains)


def solution(mesh):
    placed = (
        P("replica", "shard", None),
        P("replica", "shard"),
        P("replica", "shard", None),
        P("replica", "shard", None),
        P("shard", None),
        P("shard"),
        P(),
        P(),
        P(),
        P(),
    )
    return jax.shard_map(
        on_device,
        mesh=mesh,
        in_specs=placed,
        out_specs=(P("shard", None), P("shard"), P(), P(), P()),
        check_vma=False,
    )
```

profile of v0, /device:TPU:0, one launch (start us, length us, event | category | flops | bytes accessed | tf_op | source)
XLA Modules:
  0.0 208.5 jit_solution(15645239266758178716)
XLA Ops:
  8.8 0.7 reduce.9
  9.4 0.7 all_to_all.16
  10.1 8.3 %all-to-all-start = ((s32[16,1,8]{2,1,0:T(1,128)}), s32[16,1,8]{2,1,0:T(1,128)S(1)}, u32[]{:S(2)}, u32[]{:S(2)}) async-start(s32[16,1,8]{2,1,0:T(1,128)} %bitcast), calls=%async_computation | async-start | bytes 16384 | tf_op jit(solution)/shard_map/all_to_all | solution.py:68
  18.5 0.6 copy-done.9
  20.1 5.6 %all-to-all-done = s32[16,1,8]{2,1,0:T(1,128)S(1)} async-done(((s32[16,1,8]{2,1,0:T(1,128)}), s32[16,1,8]{2,1,0:T(1,128)S(1)}, u32[]{:S(2)}, u32[]{:S(2)}) %all-to-all-start) | async-done | bytes 544 | tf_op jit(solution)/shard_map/all_to_all | solution.py:68
  26.0 0.8 gather_fusion
  26.8 0.7 fusion.33
  27.5 3.5 %all-to-all-start.1 = ((bf16[16,8,256]{2,1,0:T(8,128)(2,1)}), bf16[16,8,256]{2,1,0:T(8,128)(2,1)S(1)}, u32[]{:S(2)}, u32[]{:S(2)}) async-start(bf16[16,8,256]{2,1,0:T(8,128)(2,1)} %fusion.33), calls=%async_computation.1 | async-start | bytes 131072 | tf_op jit(solution)/shard_map/all_to_all | solution.py:70
  31.1 7.5 %all-to-all-done.1 = bf16[16,8,256]{2,1,0:T(8,128)(2,1)S(1)} async-done(((bf16[16,8,256]{2,1,0:T(8,128)(2,1)}), bf16[16,8,256]{2,1,0:T(8,128)(2,1)S(1)}, u32[]{:S(2)}, u32[]{:S(2)}) %all-to-all-start.1) | async-done | bytes 65568 | tf_op jit(solution)/shard_map/all_to_all | solution.py:70
  38.5 0.8 gather_fusion.1
  39.8 0.7 copy-done.6
  41.0 1.0 select_convert_fusion
  42.5 0.7 copy-done.1
  44.2 0.8 copy-done.14
  46.6 1.4 scatter_custom_fusion
  48.7 3.5 %all-to-all-start.2 = ((bf16[16,8,256]{2,1,0:T(8,128)(2,1)}), bf16[16,8,256]{2,1,0:T(8,128)(2,1)S(1)}, u32[]{:S(2)}, u32[]{:S(2)}) async-start(bf16[16,8,256]{2,1,0:T(8,128)(2,1)} %convert_bitcast_fusion), calls=%async_computation.2 | async-start | bytes 131072 | tf_op jit(solution)/shard_map/all_to_all | solution.py:85
  52.2 0.7 reduce.10
  53.0 6.7 %all-to-all-done.2 = bf16[16,8,256]{2,1,0:T(8,128)(2,1)S(1)} async-done(((bf16[16,8,256]{2,1,0:T(8,128)(2,1)}), bf16[16,8,256]{2,1,0:T(8,128)(2,1)S(1)}, u32[]{:S(2)}, u32[]{:S(2)}) %all-to-all-start.2) | async-done | bytes 65568 | tf_op jit(solution)/shard_map/all_to_all | solution.py:85
  59.7 1.5 scatter_custom_fusion.1
  61.9 1.0 divide_convert_fusion
  63.0 1.0 fusion.3
  64.0 1.5 fusion.1
  65.5 0.6 copy-done.11
  67.4 38.6 %psum.23 = f32[2,256]{1,0:T(2,128)} all-reduce(f32[2,256]{1,0:T(2,128)S(1)} %maximum_multiply_fusion), channel_id=1, replica_groups=mesh['shard'=16,'replica'=2] {'shard','replica'}, use_global_device_ids=true, to_apply=%region_19.20 | all-reduce | flops 512 | bytes 4096 | tf_op jit(solution)/shard_map/psum | solution.py:126
  106.1 2.4 %all-reduce.5 = bf16[1024]{0:T(1024)(128)(2,1)S(1)} all-reduce(bf16[1024]{0:T(1024)(128)(2,1)S(1)} %get-tuple-element.14), channel_id=3, replica_groups=mesh['shard'=16,'replica'=2] {'replica'}, use_global_device_ids=true, to_apply=%region_14.15.clone | all-reduce | flops 1024 | bytes 4096
  108.6 1.8 all-gather
  111.0 1.0 multiply_convert_fusion
  112.0 2.2 %all_gather.6 = bf16[1024,256]{1,0:T(8,128)(2,1)S(1)} all-gather(bf16[512,256]{1,0:T(8,128)(2,1)S(1)} %multiply_convert_fusion), channel_id=1, replica_groups=mesh['shard'=16,'replica'=2] {'replica'}, dimensions={0}, use_global_device_ids=true | all-gather | bytes 786432 | tf_op jit(solution)/shard_map/all_gather | solution.py:110
  114.2 1.0 convert_element_type.129
  115.3 82.7 %all-reduce.9.cloned.1.call-done = (f32[256,1024]{1,0:T(8,128)}, f32[256,256]{1,0:T(8,128)}) async-done(((f32[256,1024]{1,0:T(8,128)}, f32[256,256]{1,0:T(8,128)}), (f32[256,1024]{1,0:T(8,128)}, f32[256,256]{1,0:T(8,128)})) %all-reduce.9.cloned.1.call-update) | async-done | bytes 1310736 | tf_op jit(solution)/shard_map/psum | solution.py:126
  198.0 2.3 %copy.53 = f32[256,1024]{1,0:T(8,128)} copy(f32[256,1024]{1,0:T(8,128)} %get-tuple-element.27) | data formatting | bytes 2097152
  200.3 0.7 copy.54
  (81 shorter events, 8.7 us)
Async XLA Ops:
  8.0 18.0 %copy-start = (f32[1024,256]{1,0:T(8,128)S(1)}, f32[1024,256]{1,0:T(8,128)}, u32[]{:S(2)}) copy-start(f32[1024,256]{1,0:T(8,128)} %param.14) | copy-start | bytes 3145732
  8.0 0.7 copy-start.8
  10.1 15.6 %all-to-all-start = ((s32[16,1,8]{2,1,0:T(1,128)}), s32[16,1,8]{2,1,0:T(1,128)S(1)}, u32[]{:S(2)}, u32[]{:S(2)}) async-start(s32[16,1,8]{2,1,0:T(1,128)} %bitcast), calls=%async_computation | async-start | bytes 16384 | tf_op jit(solution)/shard_map/all_to_all | solution.py:68
  18.5 0.7 copy-start.9
  19.4 0.7 copy-start.10
  26.8 13.0 %copy-start.7 = (bf16[256,1024]{1,0:T(8,128)(2,1)S(1)}, bf16[256,1024]{1,0:T(8,128)(2,1)}, u32[]{:S(2)}) copy-start(bf16[256,1024]{1,0:T(8,128)(2,1)} %param.16) | copy-start | bytes 1572868
  27.5 11.0 %all-to-all-start.1 = ((bf16[16,8,256]{2,1,0:T(8,128)(2,1)}), bf16[16,8,256]{2,1,0:T(8,128)(2,1)S(1)}, u32[]{:S(2)}, u32[]{:S(2)}) async-start(bf16[16,8,256]{2,1,0:T(8,128)(2,1)} %fusion.33), calls=%async_computation.1 | async-start | bytes 131072 | tf_op jit(solution)/shard_map/all_to_all | solution.py:70
  39.8 0.7 copy-start.6
  40.8 5.0 %copy-start.12 = (f32[128,1024]{1,0:T(8,128)}, f32[128,1024]{1,0:T(8,128)S(1)}, u32[]{:S(2)}) copy-start(f32[128,1024]{1,0:T(8,128)S(1)} %get-tuple-element.17) | copy-start | bytes 1572868
  42.3 0.8 copy-start.1
  42.3 0.9 copy-start.3
  42.3 0.9 copy-start.4
  44.0 1.0 copy-start.14
  48.7 11.0 %all-to-all-start.2 = ((bf16[16,8,256]{2,1,0:T(8,128)(2,1)}), bf16[16,8,256]{2,1,0:T(8,128)(2,1)S(1)}, u32[]{:S(2)}, u32[]{:S(2)}) async-start(bf16[16,8,256]{2,1,0:T(8,128)(2,1)} %convert_bitcast_fusion), calls=%async_computation.2 | async-start | bytes 131072 | tf_op jit(solution)/shard_map/all_to_all | solution.py:85
  52.2 58.9 %reduce-scatter.2.cloned.1.call-start = ((), (), s32[]{:S(2)}) async-start(), calls=%async_computation.4 | async-start | bytes 786432 | tf_op jit(solution)/shard_map/reduce_scatter | solution.py:99
  61.2 0.7 copy-start.5
  62.9 1.1 copy-start.13
  62.9 135.0 %all-reduce.9.cloned.1.call-start = ((), (), s32[]{:S(2)}) async-start(), calls=%async_computation.5 | async-start | bytes 2621440 | tf_op jit(solution)/shard_map/psum | solution.py:126
  65.5 0.7 copy-start.11
  198.0 2.4 %copy-start.2 = (f32[256,256]{1,0:T(8,128)S(1)}, f32[256,256]{1,0:T(8,128)}, u32[]{:S(2)}) copy-start(f32[256,256]{1,0:T(8,128)} %get-tuple-element.28) | copy-start | bytes 786436
Sparse Core Ops, SparseCore 0:
  63.1 4.6 reduce-scatter.1
Sparse Core Ops, SparseCore 1:
  69.4 128.5 all-reduce.8
where the time goes:
time: 209 us; the launch traced here: 208 us
  waiting for transfers between devices  103 us (49%)
  blocking collectives  45.1 us (22%)
  between operations  16.5 us (8%)
  starting transfers between devices  15.4 us (7%)
  local copies, waits for them, and re-layouts  12.3 us (6%)
  other arithmetic  11 us (5%)
  matrix products  5.62 us (3%)
    psum x1, waiting for transfers between devices, on_device(): lax.psum((dense_terms[0], dense_terms[1], dense_terms[2]), ('shard', 'rep...  82.7 us
    psum x1, blocking collectives, on_device(): lax.psum((dense_terms[0], dense_terms[1], dense_terms[2]), ('shard', 'rep...  38.6 us
    unnamed x35, local copies, waits for them, and re-layouts  9.02 us
    all_to_all x1, starting transfers between devices, on_device(): lax.all_to_all(asked_rows, 'shard', split_axis=0, concat_axis=0, tiled=True)  8.34 us
    all_to_all x1, waiting for transfers between devices, on_device(): lax.all_to_all(found_rows, 'shard', split_axis=0, concat_axis=0, tiled=True)  7.48 us
    all_to_all x1, waiting for transfers between devices, on_device(): lax.all_to_all(slot_grad.reshape(shards, capacity, model_width).astype(jn...  6.69 us
    all_to_all x1, waiting for transfers between devices, on_device(): lax.all_to_all(asked_rows, 'shard', split_axis=0, concat_axis=0, tiled=True)  5.63 us
  transfers between devices with their start and end apart: 5, of which 4 were waited for; matrix products, arithmetic and copies ran while one was open for 3% of the time, Pallas kernels for 0%

commit v1 on v0

v1 whole, which is shorter than its diff:
```python
import functools
import math

import jax
import jax.numpy as jnp
from jax import lax
from jax.experimental import pallas as pl
from jax.experimental.pallas import tpu as pltpu
from jax.sharding import PartitionSpec as P

HEADS = 4
MAXLEN = 48
EPSILON = 1e-08
LEARN_RATE = 0.5
NORM_EPSILON = 1e-05
GAIN_ROWS = 8

f32 = jnp.float32
bf16 = jnp.bfloat16
VMEM = pl.BlockSpec(memory_space=pltpu.VMEM)


def iota(shape, axis):
    return lax.broadcasted_iota(jnp.int32, shape, axis)


def mm(left, right, contract=(1, 0)):
    return lax.dot_general(
        left.astype(bf16),
        right.astype(bf16),
        (((contract[0],), (contract[1],)), ((), ())),
        preferred_element_type=f32,
    )


def estimate(flops, bytes_accessed):
    return pl.CostEstimate(flops=flops, bytes_accessed=bytes_accessed, transcendentals=0)


def fetch_kernel(capacity, ids_ref, table_ref, found_ref, wanted_ref):
    me = lax.axis_index("shard")
    ids = ids_ref[...].reshape(ids_ref.shape[0], ids_ref.shape[2])
    shards, slots = ids.shape
    rows = table_ref.shape[0]
    high = (ids >> 5).astype(f32)
    low = (ids & 31).astype(f32)
    slot = iota((slots, shards), 0)
    first = iota((slots, shards), 1) * capacity
    expand = ((slot >= first) & (slot < first + capacity)).astype(f32)
    asked = mm(expand, high) * 32.0 + mm(expand, low)
    pick = iota((slots, slots), 1) == me * capacity + lax.rem(iota((slots, slots), 0), capacity)
    column = jnp.sum(jnp.where(pick, asked, 0.0), axis=1, keepdims=True)
    eye = iota((slots, slots), 0) == iota((slots, slots), 1)
    wanted_ref[...] = jnp.sum(jnp.where(eye, column, 0.0), axis=0, keepdims=True)
    chosen = (column.astype(jnp.int32) == iota((slots, rows), 1)).astype(f32)
    found_ref[...] = mm(chosen, table_ref[...]).astype(bf16)


def center(values):
    shifted = values - jnp.mean(values, axis=1, keepdims=True)
    scale = lax.rsqrt(jnp.mean(shifted * shifted, axis=1, keepdims=True) + NORM_EPSILON)
    return shifted * scale, scale


def center_grad(grad, normal, scale):
    along = jnp.mean(grad * normal, axis=1, keepdims=True)
    return scale * (grad - jnp.mean(grad, axis=1, keepdims=True) - normal * along)


def sigmoid(values):
    return 1.0 / (1.0 + jnp.exp(-values))


def segments(lengths):
    count = lengths.shape[1]
    row, col = iota((count, count), 0), iota((count, count), 1)
    column = jnp.sum(jnp.where(row == col, lengths, 0.0), axis=1, keepdims=True)
    ends_column = jnp.sum(jnp.where(col <= row, lengths, 0.0), axis=1, keepdims=True)
    ends_row = jnp.sum(jnp.where(row <= col, column, 0.0), axis=0, keepdims=True)
    return ends_row, ends_column


def layer_kernel(
    slot_ref, rows_ref, length_ref, cot_ref, w_ref, wo_ref, norm_ref, gate_ref, slot_grad_ref, *rest
):
    part_refs, stacked = rest[:-1], rest[-1]
    replicas = len(part_refs)
    tokens, width = rows_ref.shape
    head = width // HEADS
    part_rows = part_refs[0].shape[0] - GAIN_ROWS
    row, col = iota((tokens, tokens), 0), iota((tokens, tokens), 1)

    slot_row = slot_ref[...].astype(f32)
    slot_column = jnp.sum(jnp.where(row == col, slot_row, 0.0), axis=1, keepdims=True)
    embedded = mm((slot_column.astype(jnp.int32) == col).astype(f32), rows_ref[...])

    ends_row, ends_column = segments(length_ref[...].astype(f32))
    count = ends_row.shape[1]
    before_row = iota((count, tokens), 1).astype(f32) >= ends_column
    segment_row = jnp.sum(before_row.astype(f32), axis=0, keepdims=True)
    before_column = iota((tokens, count), 0).astype(f32) >= ends_row
    segment_column = jnp.sum(before_column.astype(f32), axis=1, keepdims=True)
    same = (segment_row == segment_column) & (row >= col)
    same = jnp.concatenate([same.astype(f32)] * HEADS, axis=0)

    lane = iota((1, width), 1)
    heads = [((lane >= h * head) & (lane < (h + 1) * head)).astype(f32) for h in range(HEADS)]

    def by_head(values):
        return jnp.concatenate([values * mask for mask in heads], axis=0).astype(bf16)

    def beside(values):
        return jnp.concatenate(
            [values[h * tokens : (h + 1) * tokens] for h in range(HEADS)], axis=1
        )

    norm_gain, gate_gain = norm_ref[...], gate_ref[...]
    normal, scale = center(embedded)
    normed = (normal * norm_gain).astype(bf16)
    lifted = mm(normed, w_ref[...])
    sig = sigmoid(lifted)
    projected = lifted * sig
    slope = sig * (1.0 + lifted * (1.0 - sig))
    gate_u = projected[:, :width]
    values = projected[:, width : 2 * width].astype(bf16).astype(f32)
    queries = projected[:, 2 * width : 3 * width].astype(bf16).astype(f32)
    keys = projected[:, 3 * width :].astype(bf16).astype(f32)

    queries_by, keys_by, values_by = by_head(queries), by_head(keys), by_head(values)
    scores = mm(queries_by, keys, (1, 1)) * head ** (-0.5)
    score_sig = sigmoid(scores)
    weights = (same * (scores * score_sig / MAXLEN)).astype(bf16)
    attended = mm(beside(weights), values_by)
    normal_two, scale_two = center(attended)
    gated = (normal_two * gate_gain * gate_u).astype(bf16)

    cot = cot_ref[...]
    gated_grad = mm(cot, wo_ref[...], (1, 1)).astype(bf16).astype(f32)
    out_grad = mm(gated, cot, (0, 0))
    normal_u = normal_two * gate_u
    gate_gain_grad = jnp.sum(gated_grad * normal_u, axis=0, keepdims=True)
    gated_gain = gated_grad * gate_gain
    u_grad = gated_gain * normal_two
    attended_grad = center_grad(gated_gain * gate_u, normal_two, scale_two)
    attended_by = by_head(attended_grad)
    weights_grad = mm(attended_by, values, (1, 1)).astype(bf16).astype(f32)
    values_grad = mm(weights, attended_by, (0, 0)).astype(bf16).astype(f32)
    score_slope = score_sig * (1.0 + scores * (1.0 - score_sig))
    scores_grad = (same * weights_grad * score_slope * (head ** (-0.5) / MAXLEN)).astype(bf16)
    queries_grad = mm(beside(scores_grad), keys_by).astype(bf16).astype(f32)
    keys_grad = mm(scores_grad, queries_by, (0, 0)).astype(bf16).astype(f32)
    lifted_grad = (
        jnp.concatenate([u_grad, values_grad, queries_grad, keys_grad], axis=1) * slope
    ).astype(bf16)
    w_grad = mm(normed, lifted_grad, (0, 0)).astype(bf16)
    normed_grad = mm(lifted_grad, w_ref[...], (1, 1)).astype(bf16).astype(f32)
    norm_gain_grad = jnp.sum(normed_grad * normal, axis=0, keepdims=True)
    token_grad = cot.astype(f32) + center_grad(normed_grad * norm_gain, normal, scale)

    to_slot = (slot_row.astype(jnp.int32) == row).astype(f32)
    grad_high = token_grad.astype(bf16).astype(f32)
    slot_grad_ref[...] = mm(
        jnp.concatenate([to_slot, to_slot], axis=1),
        jnp.concatenate([grad_high, token_grad - grad_high], axis=0),
    ).astype(bf16)

    blocks = w_grad.shape[1] // width
    for block in range(blocks):
        stacked[block * width : (block + 1) * width] = w_grad[:, block * width : (block + 1) * width]
    stacked[blocks * width : (blocks + 1) * width] = out_grad.astype(bf16)
    filled = (blocks + 1) * width
    if filled < stacked.shape[0]:
        stacked[filled:] = jnp.zeros((stacked.shape[0] - filled, width), bf16)
    gain_grads = jnp.concatenate([norm_gain_grad, gate_gain_grad], axis=0)
    gain_high = gain_grads.astype(bf16).astype(f32)
    gain_rows = jnp.concatenate(
        [gain_high, gain_grads - gain_high, jnp.zeros((GAIN_ROWS - 4, width), f32)], axis=0
    ).astype(bf16)
    me = lax.axis_index("replica")
    for step, part_ref in enumerate(part_refs):
        start = lax.rem(me + step, replicas) * part_rows
        part_ref[:part_rows] = stacked[pl.ds(pl.multiple_of(start, 16), part_rows)]
        part_ref[part_rows:] = gain_rows


def pack_kernel(shards, slot_grad_ref, *refs):
    part_refs, out_ref = refs[:-1], refs[-1]
    width = slot_grad_ref.shape[1]
    total = part_refs[0][...].astype(f32)
    for part_ref in part_refs[1:]:
        total = total + part_ref[...].astype(f32)
    share = total[:-GAIN_ROWS].reshape(shards, -1, width)
    gains = jnp.broadcast_to(total[-GAIN_ROWS:][None], (shards, GAIN_ROWS, width))
    slots = slot_grad_ref[...].astype(f32).reshape(shards, -1, width)
    out_ref[...] = jnp.concatenate([slots, share, gains], axis=1).astype(bf16)


def unpack_kernel(capacity, grad_scale, in_ref, slots_ref, share_ref, gains_ref):
    shards, rows, width = in_ref.shape
    slots_ref[...] = in_ref[:, :capacity].astype(f32).reshape(-1, width).astype(bf16)
    total = in_ref[0, capacity:].astype(f32)
    for shard in range(1, shards):
        total = total + in_ref[shard, capacity:].astype(f32)
    total = total * grad_scale
    share = total[:-GAIN_ROWS].astype(bf16)
    for shard in range(shards):
        share_ref[shard] = share
    first = total.shape[0] - GAIN_ROWS
    gains_ref[...] = total[first : first + 2] + total[first + 2 : first + 4]


def adagrad_kernel(replicas, *refs):
    wanted_refs, grad_refs = refs[:replicas], refs[replicas : 2 * replicas]
    state_ref, update_ref, state_out_ref = refs[2 * replicas :]
    rows = update_ref.shape[0]
    slots = wanted_refs[0].shape[1]
    first = pl.program_id(0) * rows
    eye = iota((rows, rows), 0) == iota((rows, rows), 1)
    state_row = state_ref[...].reshape(1, rows)
    state = jnp.sum(jnp.where(eye, state_row, 0.0), axis=1, keepdims=True)
    delta = jnp.zeros(update_ref.shape, f32)
    squares = jnp.zeros((rows, 1), f32)
    for wanted_ref, grad_ref in zip(wanted_refs, grad_refs):
        hit = iota((rows, slots), 0) + first == wanted_ref[...].astype(jnp.int32)
        row_grad = mm(hit.astype(f32), grad_ref[...])
        mean_square = jnp.mean(row_grad * row_grad, axis=1, keepdims=True)
        delta = delta + row_grad * lax.rsqrt(state + mean_square + EPSILON)
        squares = squares + mean_square
    update_ref[...] = delta * (-LEARN_RATE / replicas)
    squares_row = jnp.sum(jnp.where(eye, squares, 0.0), axis=0, keepdims=True)
    state_out_ref[...] = (state_row + squares_row / replicas).reshape(state_out_ref.shape)


def spread_kernel(ordered, *refs):
    part_refs, (uvqk_ref, out_ref) = refs[:-2], refs[-2:]
    parts = [part_ref[...] for part_ref in part_refs]
    if not ordered:
        mine, other = parts
        is_first = lax.axis_index("replica") == 0
        parts = [jnp.where(is_first, mine, other), jnp.where(is_first, other, mine)]
    width = parts[0].shape[1]
    rows = jnp.concatenate(parts, axis=0).astype(f32)
    blocks = uvqk_ref.shape[1] // width
    for block in range(blocks):
        uvqk_ref[:, block * width : (block + 1) * width] = rows[block * width : (block + 1) * width]
    out_ref[...] = rows[blocks * width : (blocks + 1) * width]


def from_replicas(parts):
    replicas = len(parts)
    came = [parts[0]]
    for step in range(1, replicas):
        pairs = [(source, (source + step) % replicas) for source in range(replicas)]
        came.append(lax.ppermute(parts[step], "replica", pairs))
    if replicas > 2:
        order = lax.rem(lax.axis_index("replica") - jnp.arange(replicas) + replicas, replicas)
        stacked = jnp.take(jnp.stack(came), order, axis=0)
        came = [stacked[index] for index in range(replicas)]
    return came


def on_device(
    request_rows,
    token_slot,
    seq_lengths,
    cotangent,
    table_slab,
    adagrad_state,
    w_uvqk,
    w_out,
    norm_gain,
    out_gain,
):
    shards = lax.axis_size("shard")
    replicas = lax.axis_size("replica")
    tokens = token_slot.shape[1]
    rows_dev, width = table_slab.shape
    capacity = tokens // shards
    dense_rows = w_uvqk.shape[1] + width
    share_rows = -(-dense_rows // (shards * replicas))
    part_rows = share_rows * shards
    grad_scale = 1.0 / math.sqrt(tokens * shards * replicas)
    shape = jax.ShapeDtypeStruct

    asked = jnp.broadcast_to(request_rows.reshape(1, 1, tokens), (shards, 1, tokens))
    ids = lax.all_to_all(asked, "shard", split_axis=0, concat_axis=0, tiled=True)
    found, wanted = pl.pallas_call(
        functools.partial(fetch_kernel, capacity),
        out_shape=(shape((tokens, width), bf16), shape((1, tokens), f32)),
        in_specs=[VMEM] * 2,
        out_specs=(VMEM, VMEM),
        cost_estimate=estimate(2 * tokens * rows_dev * width, rows_dev * width * 4),
        name="fetch",
    )(ids, table_slab)
    slot_rows = lax.all_to_all(
        found.reshape(shards, capacity, width), "shard", split_axis=0, concat_axis=0, tiled=True
    ).reshape(tokens, width)

    part_shape = shape((part_rows + GAIN_ROWS, width), bf16)
    slot_grad, *parts = pl.pallas_call(
        layer_kernel,
        out_shape=(shape((tokens, width), bf16),) + (part_shape,) * replicas,
        in_specs=[VMEM] * 8,
        out_specs=(VMEM,) * (replicas + 1),
        scratch_shapes=[pltpu.VMEM((part_rows * replicas, width), bf16)],
        cost_estimate=estimate(8 * tokens * width * w_uvqk.shape[1], 4 * dense_rows * width),
        name="layer",
    )(
        token_slot,
        slot_rows,
        seq_lengths.reshape(1, -1),
        cotangent.reshape(tokens, width),
        w_uvqk,
        w_out,
        norm_gain.reshape(1, width),
        out_gain.reshape(1, width),
    )

    came = from_replicas(parts)
    aligned = capacity % 8 == 0 and share_rows % 8 == 0
    message_rows = capacity + share_rows + GAIN_ROWS
    if aligned:
        message = pl.pallas_call(
            functools.partial(pack_kernel, shards),
            out_shape=shape((shards, message_rows, width), bf16),
            in_specs=[VMEM] * (replicas + 1),
            out_specs=VMEM,
            name="pack",
        )(slot_grad, *came)
    else:
        total = sum(part.astype(f32) for part in came).astype(bf16)
        message = jnp.concatenate(
            [
                slot_grad.reshape(shards, capacity, width),
                total[:part_rows].reshape(shards, share_rows, width),
                jnp.broadcast_to(total[part_rows:][None], (shards, GAIN_ROWS, width)),
            ],
            axis=1,
        )
    arrived = lax.all_to_all(message, "shard", split_axis=0, concat_axis=0, tiled=True)
    if aligned:
        owned, share, grad_gains = pl.pallas_call(
            functools.partial(unpack_kernel, capacity, grad_scale),
            out_shape=(
                shape((tokens, width), bf16),
                shape((shards, share_rows, width), bf16),
                shape((2, width), f32),
            ),
            in_specs=[VMEM],
            out_specs=(VMEM,) * 3,
            name="unpack",
        )(arrived)
    else:
        owned = arrived[:, :capacity].reshape(tokens, width)
        total = jnp.sum(arrived[:, capacity:].astype(f32), axis=0) * grad_scale
        share = jnp.broadcast_to(
            total[:share_rows].astype(bf16)[None], (shards, share_rows, width)
        )
        grad_gains = total[share_rows : share_rows + 2] + total[share_rows + 2 : share_rows + 4]

    gathered = lax.all_to_all(share, "shard", split_axis=0, concat_axis=0, tiled=True)

    wanted_all = from_replicas([wanted] * replicas)
    owned_all = from_replicas([owned] * replicas)
    block = 128
    row_update, state_new = pl.pallas_call(
        functools.partial(adagrad_kernel, replicas),
        grid=(rows_dev // block,),
        out_shape=(shape((rows_dev, width), f32), shape((rows_dev // block, 1, block), f32)),
        in_specs=[pl.BlockSpec((1, tokens), lambda step: (0, 0))] * replicas
        + [pl.BlockSpec((tokens, width), lambda step: (0, 0))] * replicas
        + [pl.BlockSpec((1, 1, block), lambda step: (step, 0, 0))],
        out_specs=(
            pl.BlockSpec((block, width), lambda step: (step, 0)),
            pl.BlockSpec((1, 1, block), lambda step: (step, 0, 0)),
        ),
        cost_estimate=estimate(2 * replicas * tokens * rows_dev * width, rows_dev * width * 4),
        name="adagrad",
    )(*wanted_all, *owned_all, adagrad_state.reshape(rows_dev // block, 1, block))

    halves = from_replicas([gathered.reshape(part_rows, width)] * replicas)
    grad_uvqk, grad_out = pl.pallas_call(
        functools.partial(spread_kernel, replicas != 2),
        out_shape=(shape(w_uvqk.shape, f32), shape(w_out.shape, f32)),
        in_specs=[VMEM] * replicas,
        out_specs=(VMEM, VMEM),
        name="spread",
    )(*halves)
    return (row_update, state_new.reshape(rows_dev), grad_uvqk, grad_out, grad_gains)


def solution(mesh):
    placed = (
        P("replica", "shard", None),
        P("replica", "shard"),
        P("replica", "shard", None),
        P("replica", "shard", None),
        P("shard", None),
        P("shard"),
        P(),
        P(),
        P(),
        P(),
    )
    return jax.shard_map(
        on_device,
        mesh=mesh,
        in_specs=placed,
        out_specs=(P("shard", None), P("shard"), P(), P(), P()),
        check_vma=False,
    )
```

time: 209 us -> 86.3 us (0.41)
  waiting for transfers between devices: 103 us -> 2.67 us
  Pallas kernels: 0 us -> 18 us
  between operations: 16.5 us -> 0.68 us
  blocking collectives: 45.1 us -> 60.4 us
  starting transfers between devices: 15.4 us -> 1.01 us
  other arithmetic: 11 us -> 0 us
  local copies, waits for them, and re-layouts: 12.3 us -> 2.84 us
  matrix products: 5.62 us -> 0 us
    psum x1 -> x0, waiting for transfers between devices: 82.7 us -> none  [on_device(): lax.psum((dense_terms[0], dense_terms[1], dense_terms[2]), ('shard', 'rep...]
    all_to_all x0 -> x4, blocking collectives: none -> 60.4 us  [the longest x1 18.6 us: on_device(): lax.all_to_all(message, 'shard', split_axis=0, concat_axis=0, tiled=True)]
    psum x1 -> x0, blocking collectives: 38.6 us -> none  [on_device(): lax.psum((dense_terms[0], dense_terms[1], dense_terms[2]), ('shard', 'rep...]
    all_to_all x3 -> x0, waiting for transfers between devices: 19.8 us -> none  [the longest x1 7.48 us: on_device(): lax.all_to_all(found_rows, 'shard', split_axis=0, concat_axis=0, tiled=True)]
    pallas_call x0 -> x6, Pallas kernels: none -> 18 us  [the longest x1 5.37 us: on_device(): pl.pallas_call(functools.partial(adagrad_kernel, replicas), grid=(rows_de...]
    all_to_all x3 -> x0, starting transfers between devices: 15.3 us -> none  [the longest x1 8.34 us: on_device(): lax.all_to_all(asked_rows, 'shard', split_axis=0, concat_axis=0, tiled=True)]
    unnamed x35 -> x16, local copies, waits for them, and re-layouts: 9.02 us -> 2.83 us
    dot_general x11 -> x0, matrix products: 5.62 us -> none  [the longest x3 2.34 us: hstu_layer(): jnp.dot(normed, w_uvqk, preferred_element_type=jnp.float32)]
  transfers between devices with their start and end apart: 5 -> 4, of which waited for: 4 -> 2; matrix products, arithmetic and copies ran while one was open for 3% -> 0% of each run, Pallas kernels for 0% -> 6%
where the time goes in v1:
time: 86.3 us; the launch traced here: 85.5 us
  blocking collectives  60.4 us (70%)
  Pallas kernels  18 us (21%)
  local copies, waits for them, and re-layouts  2.84 us (3%)
  waiting for transfers between devices  2.67 us (3%)
  starting transfers between devices  1.01 us (1%)
    all_to_all x1, blocking collectives, on_device(): lax.all_to_all(message, 'shard', split_axis=0, concat_axis=0, tiled=True)  18.6 us
    all_to_all x1, blocking collectives, on_device(): lax.all_to_all(asked, 'shard', split_axis=0, concat_axis=0, tiled=True)  15.5 us
    all_to_all x1, blocking collectives, on_device(): lax.all_to_all(share, 'shard', split_axis=0, concat_axis=0, tiled=True)  14.6 us
    all_to_all x1, blocking collectives, on_device(): lax.all_to_all(found.reshape(shards, capacity, width), 'shard', split_axi...  11.7 us
    pallas_call x1, Pallas kernels, on_device(): pl.pallas_call(functools.partial(adagrad_kernel, replicas), grid=(rows_de...  5.37 us
    pallas_call x1, Pallas kernels, on_device(): pl.pallas_call(layer_kernel, out_shape=(shape((tokens, width), bf16),) +...  4.31 us
    unnamed x16, local copies, waits for them, and re-layouts  2.83 us
    ppermute x4, waiting for transfers between devices, from_replicas(): came.append(lax.ppermute(parts[step], 'replica', pairs))  2.67 us
  transfers between devices with their start and end apart: 4, of which 2 were waited for; matrix products, arithmetic and copies ran while one was open for 0% of the time, Pallas kernels for 6%

profile of v1, /device:TPU:0, one launch (start us, length us, event | category | flops | bytes accessed | tf_op | source)
XLA Modules:
  0.0 85.5 jit_solution(13193735333193715012)
XLA Ops:
  0.6 0.0 copy-start.3
  0.6 0.6 copy-done.3
  1.3 15.5 %all_to_all.20.ids_ref = s32[16,1,128]{2,1,0:T(1,128)} all-to-all(s32[16,1,128]{2,1,0:T(1,128)S(1)} %broadcast_in_dim.8), channel_id=1, replica_groups=mesh['shard'=16,'replica'=2] {'shard'}, dimensions={0} | all-to-all | bytes 16384 | tf_op jit(solution)/shard_map/all_to_all | solution.py:286
  16.8 2.3 %fetch.1 = (bf16[128,256]{1,0:T(8,128)(2,1)}, f32[1,128]{1,0:T(1,128)}) custom-call(s32[16,1,128]{2,1,0:T(1,128)} %all_to_all.20.ids_ref, f32[1024,256]{1,0:T(8,128)} %table_ref.1), custom_call_target="tpu_custom_call" | custom-call | flops 67108864 | bytes 1048576 | tf_op jit(solution)/shard_map/fetch/pallas_call | solution.py:287
  19.2 11.7 %all_to_all.21 = bf16[16,8,256]{2,1,0:T(8,128)(2,1)} all-to-all(bf16[16,8,256]{2,1,0:T(8,128)(2,1)} %bitcast.13), channel_id=1, replica_groups=mesh['shard'=16,'replica'=2] {'shard'}, dimensions={0} | all-to-all | bytes 131072 | tf_op jit(solution)/shard_map/all_to_all | solution.py:295
  30.9 4.3 %layer.1 = (bf16[128,256]{1,0:T(8,128)(2,1)}, bf16[648,256]{1,0:T(8,128)(2,1)}, bf16[648,256]{1,0:T(8,128)(2,1)}) custom-call(s32[1,128]{1,0:T(1,128)} %slot_ref.1, bf16[128,256]{1,0:T(8,128)(2,1)} %bitcast.12, s32[1,8]{1,0:T(1,128)} %bitcast.19, bf16[128,256]{1,0:T(8,128)(2,1)} %bitcast.15, bf16[256,1024]{1,0:T(8,128)(2,1)} %w_ref.1, ...), custom_call_target="tpu_custom_call" | custom-call | flops 268435456 | bytes 1310720 | tf_op jit(solution)/shard_map/layer/pallas_call | solution.py:300
  35.2 0.0 collective-permute-start.1
  35.2 1.8 %collective-permute-done.1.refs_1_ = bf16[648,256]{1,0:T(8,128)(2,1)S(1)} collective-permute-done((bf16[648,256]{1,0:T(8,128)(2,1)}, bf16[648,256]{1,0:T(8,128)(2,1)S(1)}, u32[]{:S(2)}, u32[]{:S(2)}) %collective-permute-start.1) | collective-permute-done | bytes 331808 | tf_op jit(solution)/shard_map/ppermute | solution.py:254
  37.0 0.7 copy-done.1
  37.8 1.9 %pack.1 = bf16[16,56,256]{2,1,0:T(8,128)(2,1)} custom-call(bf16[128,256]{1,0:T(8,128)(2,1)} %get-tuple-element.19.slot_grad_ref, bf16[648,256]{1,0:T(8,128)(2,1)} %get-tuple-element.20.refs_0_, bf16[648,256]{1,0:T(8,128)(2,1)} %copy-done.1), custom_call_target="tpu_custom_call" | custom-call | tf_op jit(solution)/shard_map/pack/pallas_call | solution.py:323
  39.7 18.6 %all_to_all.22.in_ref = bf16[16,56,256]{2,1,0:T(8,128)(2,1)} all-to-all(bf16[16,56,256]{2,1,0:T(8,128)(2,1)} %pack.1), channel_id=1, replica_groups=mesh['shard'=16,'replica'=2] {'shard'}, dimensions={0} | all-to-all | bytes 917504 | tf_op jit(solution)/shard_map/all_to_all | solution.py:340
  58.3 1.8 %unpack.1 = (bf16[128,256]{1,0:T(8,128)(2,1)}, bf16[16,40,256]{2,1,0:T(8,128)(2,1)}, f32[2,256]{1,0:T(2,128)}) custom-call(bf16[16,56,256]{2,1,0:T(8,128)(2,1)} %all_to_all.22.in_ref), custom_call_target="tpu_custom_call" | custom-call | tf_op jit(solution)/shard_map/unpack/pallas_call | solution.py:342
  60.1 0.0 copy-start.4
  60.1 14.6 %all_to_all.23 = bf16[16,40,256]{2,1,0:T(8,128)(2,1)S(1)} all-to-all(bf16[16,40,256]{2,1,0:T(8,128)(2,1)} %get-tuple-element.25), channel_id=1, replica_groups=mesh['shard'=16,'replica'=2] {'shard'}, dimensions={0} | all-to-all | bytes 655360 | tf_op jit(solution)/shard_map/all_to_all | solution.py:361
  74.6 0.0 copy-start
  74.6 0.0 collective-permute-start.3
  74.7 0.0 copy-done.4
  74.7 0.0 copy-start.6
  74.7 0.5 collective-permute-start.2
  75.2 0.1 copy-done.6
  75.3 0.5 collective-permute-start
  75.8 0.8 collective-permute-done.refs_1_
  76.6 0.0 copy-start.7
  76.6 0.0 collective-permute-done.2.refs_3_
  76.6 0.6 copy-done.7
  77.2 0.1 copy-done.5
  77.2 5.4 %adagrad.1 = (f32[1024,256]{1,0:T(8,128)}, f32[8,1,128]{2,1,0:T(1,128)}) custom-call(f32[1,128]{1,0:T(1,128)} %get-tuple-element.17.refs_0_, f32[1,128]{1,0:T(1,128)} %copy-done.7, bf16[128,256]{1,0:T(8,128)(2,1)} %get-tuple-element.22.refs_2_, bf16[128,256]{1,0:T(8,128)(2,1)} %copy-done.5, f32[8,1,128]{2,1,0:T(1,128)} %bitcast.16), custom_call_target="tpu_custom_call" | custom-call | flops 134217728 | bytes 1048576 | tf_op jit(solution)/shard_map/adagrad/pallas_call | solution.py:366
  82.6 0.0 collective-permute-done.3.refs_1_
  82.6 0.0 copy-done
  82.6 0.0 copy-start.2
  82.6 0.7 copy-done.2
  83.3 2.2 %spread.1 = (f32[256,1024]{1,0:T(8,128)}, f32[256,256]{1,0:T(8,128)}) custom-call(bf16[640,256]{1,0:T(8,128)(2,1)} %bitcast.11, bf16[640,256]{1,0:T(8,128)(2,1)} %copy-done.2), custom_call_target="tpu_custom_call" | custom-call | tf_op jit(solution)/shard_map/spread/pallas_call | solution.py:382
  (3 shorter events, 0.0 us)
Async XLA Ops:
  0.6 0.7 copy-start.3
  35.2 1.8 %collective-permute-start.1 = (bf16[648,256]{1,0:T(8,128)(2,1)}, bf16[648,256]{1,0:T(8,128)(2,1)S(1)}, u32[]{:S(2)}, u32[]{:S(2)}) collective-permute-start(bf16[648,256]{1,0:T(8,128)(2,1)} %get-tuple-element.21), channel_id=1, source_target_pairs={{0,1},{1,0},{2,3},{3,2},{4,5},{5,4},{6,7},{7,6},{8,9},{9,8},{10,11... | collective-permute-start | bytes 995336 | tf_op jit(solution)/shard_map/ppermute | solution.py:254
  37.0 0.7 copy-start.1
  60.1 14.6 %copy-start.4 = (bf16[128,256]{1,0:T(8,128)(2,1)S(1)}, bf16[128,256]{1,0:T(8,128)(2,1)}, u32[]{:S(2)}) copy-start(bf16[128,256]{1,0:T(8,128)(2,1)} %get-tuple-element.22.refs_2_) | copy-start | bytes 196612
  74.6 8.0 %copy-start = (bf16[16,40,256]{2,1,0:T(8,128)(2,1)}, bf16[16,40,256]{2,1,0:T(8,128)(2,1)S(1)}, u32[]{:S(2)}) copy-start(bf16[16,40,256]{2,1,0:T(8,128)(2,1)S(1)} %all_to_all.23) | copy-start | bytes 983044
  74.6 7.9 %collective-permute-start.3 = (bf16[640,256]{1,0:T(8,128)(2,1)S(1)}, bf16[640,256]{1,0:T(8,128)(2,1)S(1)}, u32[]{:S(2)}, u32[]{:S(2)}) collective-permute-start(bf16[640,256]{1,0:T(8,128)(2,1)S(1)} %bitcast.10), channel_id=1, source_target_pairs={{0,1},{1,0},{2,3},{3,2},{4,5},{5,4},{6,7},{7,6},{8,9},{9,8},{10,11... | collective-permute-start | bytes 983048 | tf_op jit(solution)/shard_map/ppermute | solution.py:254
  74.7 0.6 copy-start.6
  74.7 1.9 %collective-permute-start.2 = (bf16[128,256]{1,0:T(8,128)(2,1)S(1)}, bf16[128,256]{1,0:T(8,128)(2,1)S(1)}, u32[]{:S(2)}, u32[]{:S(2)}) collective-permute-start(bf16[128,256]{1,0:T(8,128)(2,1)S(1)} %copy-done.4), channel_id=1, source_target_pairs={{0,1},{1,0},{2,3},{3,2},{4,5},{5,4},{6,7},{7,6},{8,9},{9,8},{10,11... | collective-permute-start | bytes 196616 | tf_op jit(solution)/shard_map/ppermute | solution.py:254
  75.3 1.3 %collective-permute-start = (f32[1,128]{1,0:T(1,128)S(1)}, f32[1,128]{1,0:T(1,128)S(1)}, u32[]{:S(2)}, u32[]{:S(2)}) collective-permute-start(f32[1,128]{1,0:T(1,128)S(1)} %copy-done.6), channel_id=1, source_target_pairs={{0,1},{1,0},{2,3},{3,2},{4,5},{5,4},{6,7},{7,6},{8,9},{9,8},{10,11... | collective-permute-start | bytes 1544 | tf_op jit(solution)/shard_map/ppermute | solution.py:254
  76.6 0.6 copy-start.7
  76.6 0.6 copy-start.5
  82.6 0.7 copy-start.2

commit v2 on v1

v2 whole, which is shorter than its diff:
```python
import functools
import math

import jax
import jax.numpy as jnp
from jax import lax
from jax.experimental import pallas as pl
from jax.experimental.pallas import tpu as pltpu
from jax.sharding import PartitionSpec as P


HEADS = 4
MAXLEN = 48
EPSILON = 1e-08
LEARN_RATE = 0.5
NORM_EPSILON = 1e-05
GAIN_ROWS = 8

f32 = jnp.float32
bf16 = jnp.bfloat16
VMEM = pl.BlockSpec(memory_space=pltpu.VMEM)


def room(mebibytes):
    return pltpu.CompilerParams(vmem_limit_bytes=mebibytes * 2**20)


def iota(shape, axis):
    return lax.broadcasted_iota(jnp.int32, shape, axis)


def mm(left, right, contract=(1, 0)):
    return lax.dot_general(
        left.astype(bf16),
        right.astype(bf16),
        (((contract[0],), (contract[1],)), ((), ())),
        preferred_element_type=f32,
    )


def estimate(flops, bytes_accessed):
    return pl.CostEstimate(flops=flops, bytes_accessed=bytes_accessed, transcendentals=0)


def ready_kernel(asked_ref, slot_ref, length_ref, norm_ref, gate_ref, ids_ref, small_ref):
    ids_ref[...] = jnp.broadcast_to(asked_ref[...], ids_ref.shape)
    small_ref[0:1, : slot_ref.shape[1]] = slot_ref[...].astype(f32)
    small_ref[1:2, : length_ref.shape[1]] = length_ref[...].astype(f32)
    small_ref[2:3, : norm_ref.shape[1]] = norm_ref[...]
    small_ref[3:4, : gate_ref.shape[1]] = gate_ref[...]


def fetch_kernel(capacity, ids_ref, table_ref, found_ref, wanted_ref):
    me = lax.axis_index("shard")
    ids = ids_ref[...].reshape(ids_ref.shape[0], ids_ref.shape[2])
    shards, slots = ids.shape
    rows = table_ref.shape[0]
    high = (ids >> 5).astype(f32)
    low = (ids & 31).astype(f32)
    slot = iota((slots, shards), 0)
    first = iota((slots, shards), 1) * capacity
    expand = ((slot >= first) & (slot < first + capacity)).astype(f32)
    asked = mm(expand, high) * 32.0 + mm(expand, low)
    pick = iota((slots, slots), 1) == me * capacity + lax.rem(iota((slots, slots), 0), capacity)
    column = jnp.sum(jnp.where(pick, asked, 0.0), axis=1, keepdims=True)
    eye = iota((slots, slots), 0) == iota((slots, slots), 1)
    wanted_ref[...] = jnp.sum(jnp.where(eye, column, 0.0), axis=0, keepdims=True)
    chosen = (column.astype(jnp.int32) == iota((slots, rows), 1)).astype(f32)
    found_ref[...] = mm(chosen, table_ref[...]).astype(bf16)


def center(values):
    shifted = values - jnp.mean(values, axis=1, keepdims=True)
    scale = lax.rsqrt(jnp.mean(shifted * shifted, axis=1, keepdims=True) + NORM_EPSILON)
    return shifted * scale, scale


def center_grad(grad, normal, scale):
    along = jnp.mean(grad * normal, axis=1, keepdims=True)
    return scale * (grad - jnp.mean(grad, axis=1, keepdims=True) - normal * along)


def sigmoid(values):
    return 1.0 / (1.0 + jnp.exp(-values))


def segments(lengths):
    count = lengths.shape[1]
    row, col = iota((count, count), 0), iota((count, count), 1)
    column = jnp.sum(jnp.where(row == col, lengths, 0.0), axis=1, keepdims=True)
    ends_column = jnp.sum(jnp.where(col <= row, lengths, 0.0), axis=1, keepdims=True)
    ends_row = jnp.sum(jnp.where(row <= col, column, 0.0), axis=0, keepdims=True)
    return ends_row, ends_column


def layer_kernel(
    histories, small_ref, rows_ref, cot_ref, w_ref, wo_ref, lifted_ref, normal_ref, gate_ref, *rest
):
    part_refs, stacked = rest[:-1], rest[-1]
    replicas = len(part_refs)
    tokens, width = rows_ref.shape
    head = width // HEADS
    row, col = iota((tokens, tokens), 0), iota((tokens, tokens), 1)

    slot_row = small_ref[0:1, :tokens]
    slot_column = jnp.sum(jnp.where(row == col, slot_row, 0.0), axis=1, keepdims=True)
    embedded = mm((slot_column.astype(jnp.int32) == col).astype(f32), rows_ref[...])

    ends_row, ends_column = segments(small_ref[1:2, :histories])
    before_row = iota((histories, tokens), 1).astype(f32) >= ends_column
    segment_row = jnp.sum(before_row.astype(f32), axis=0, keepdims=True)
    before_column = iota((tokens, histories), 0).astype(f32) >= ends_row
    segment_column = jnp.sum(before_column.astype(f32), axis=1, keepdims=True)
    same = (segment_row == segment_column) & (row >= col)
    same = jnp.concatenate([same.astype(f32)] * HEADS, axis=0)

    lane = iota((1, width), 1)
    heads = [((lane >= h * head) & (lane < (h + 1) * head)).astype(f32) for h in range(HEADS)]

    def by_head(values):
        return jnp.concatenate([values * mask for mask in heads], axis=0).astype(bf16)

    def beside(values):
        return jnp.concatenate(
            [values[h * tokens : (h + 1) * tokens] for h in range(HEADS)], axis=1
        )

    norm_gain, gate_gain = small_ref[2:3, :width], small_ref[3:4, :width]
    normal, scale = center(embedded)
    normed = (normal * norm_gain).astype(bf16)
    lifted = mm(normed, w_ref[...])
    sig = sigmoid(lifted)
    projected = lifted * sig
    slope = sig * (1.0 + lifted * (1.0 - sig))
    gate_u = projected[:, :width]
    values = projected[:, width : 2 * width].astype(bf16).astype(f32)
    queries = projected[:, 2 * width : 3 * width].astype(bf16).astype(f32)
    keys = projected[:, 3 * width :].astype(bf16).astype(f32)

    queries_by, keys_by, values_by = by_head(queries), by_head(keys), by_head(values)
    scores = mm(queries_by, keys, (1, 1)) * head ** (-0.5)
    score_sig = sigmoid(scores)
    weights = (same * (scores * score_sig / MAXLEN)).astype(bf16)
    attended = mm(beside(weights), values_by)
    normal_two, scale_two = center(attended)
    gated = (normal_two * gate_gain * gate_u).astype(bf16)

    cot = cot_ref[...]
    gated_grad = mm(cot, wo_ref[...], (1, 1)).astype(bf16).astype(f32)
    out_grad = mm(gated, cot, (0, 0))
    normal_u = normal_two * gate_u
    gate_ref[...] = jnp.sum(gated_grad * normal_u, axis=0, keepdims=True)
    gated_gain = gated_grad * gate_gain
    u_grad = gated_gain * normal_two
    attended_grad = center_grad(gated_gain * gate_u, normal_two, scale_two)
    attended_by = by_head(attended_grad)
    weights_grad = mm(attended_by, values, (1, 1)).astype(bf16).astype(f32)
    values_grad = mm(weights, attended_by, (0, 0)).astype(bf16).astype(f32)
    score_slope = score_sig * (1.0 + scores * (1.0 - score_sig))
    scores_grad = (same * weights_grad * score_slope * (head ** (-0.5) / MAXLEN)).astype(bf16)
    queries_grad = mm(beside(scores_grad), keys_by).astype(bf16).astype(f32)
    keys_grad = mm(scores_grad, queries_by, (0, 0)).astype(bf16).astype(f32)
    lifted_grad = (
        jnp.concatenate([u_grad, values_grad, queries_grad, keys_grad], axis=1) * slope
    ).astype(bf16)
    lifted_ref[...] = lifted_grad
    normal_ref[:, :width] = normal
    normal_ref[:, width:] = jnp.broadcast_to(scale, (tokens, normal_ref.shape[1] - width))
    w_grad = mm(normed, lifted_grad, (0, 0)).astype(bf16)

    blocks = w_grad.shape[1] // width
    for block in range(blocks):
        stacked[block * width : (block + 1) * width] = w_grad[:, block * width : (block + 1) * width]
    stacked[blocks * width :] = out_grad.astype(bf16)
    me = lax.axis_index("replica")
    height = width // replicas
    for step, part_ref in enumerate(part_refs):
        start = lax.rem(me + step, replicas) * height
        for block in range(blocks + 1):
            part_ref[block * height : (block + 1) * height] = stacked[
                pl.ds(pl.multiple_of(block * width + start, 16), height)
            ]
        filled = (blocks + 1) * height
        if filled < part_ref.shape[0]:
            part_ref[filled:] = jnp.zeros((part_ref.shape[0] - filled, width), bf16)


def finish_kernel(small_ref, cot_ref, w_ref, lifted_ref, normal_ref, gate_ref, slot_grad_ref, gain_ref):
    tokens, width = cot_ref.shape
    normal = normal_ref[:, :width]
    scale = normal_ref[:, width : width + 1]
    normed_grad = mm(lifted_ref[...], w_ref[...], (1, 1)).astype(bf16).astype(f32)
    norm_gain_grad = jnp.sum(normed_grad * normal, axis=0, keepdims=True)
    token_grad = cot_ref[...].astype(f32) + center_grad(
        normed_grad * small_ref[2:3, :width], normal, scale
    )
    slot_row = small_ref[0:1, :tokens].astype(jnp.int32)
    to_slot = (slot_row == iota((tokens, tokens), 0)).astype(f32)
    grad_high = token_grad.astype(bf16).astype(f32)
    slot_grad_ref[...] = mm(
        jnp.concatenate([to_slot, to_slot], axis=1),
        jnp.concatenate([grad_high, token_grad - grad_high], axis=0),
    ).astype(bf16)
    gains = jnp.concatenate([norm_gain_grad, gate_ref[...]], axis=0)
    high = gains.astype(bf16).astype(f32)
    gain_ref[...] = jnp.concatenate([high, gains - high], axis=0)


def halves_down(values):
    lanes = values.shape[-1] // 2
    return jnp.concatenate([values[..., :lanes], values[..., lanes:]], axis=-2)


def halves_across(values):
    rows = values.shape[-2] // 2
    return jnp.concatenate([values[..., :rows, :], values[..., rows:, :]], axis=-1)


def pack_kernel(shards, slot_grad_ref, gain_ref, *refs):
    part_refs, out_ref = refs[:-1], refs[-1]
    width = slot_grad_ref.shape[1]
    total = part_refs[0][...].astype(f32)
    for part_ref in part_refs[1:]:
        total = total + part_ref[...].astype(f32)
    share = total.reshape(shards, -1, width)
    gains = halves_down(gain_ref[...])
    gains = jnp.broadcast_to(gains[None], (shards,) + gains.shape)
    slots = slot_grad_ref[...].astype(f32).reshape(shards, -1, width)
    out_ref[...] = jnp.concatenate(
        [halves_down(slots), halves_down(share), gains], axis=1
    ).astype(bf16)


def unpack_kernel(capacity, grad_scale, in_ref, share_ref):
    shards, rows, _ = in_ref.shape
    wanted = slice(2 * capacity, rows - GAIN_ROWS)
    total = in_ref[0, wanted].astype(f32)
    for shard in range(1, shards):
        total = total + in_ref[shard, wanted].astype(f32)
    share = halves_across(total * grad_scale).astype(bf16)
    for shard in range(shards):
        share_ref[shard] = share


def slots_kernel(capacity, grad_scale, in_ref, slots_ref):
    shards, rows, lanes = in_ref.shape
    tokens = shards * capacity
    slots = halves_across(in_ref[:, : 2 * capacity].astype(f32))
    gains = halves_across(jnp.sum(in_ref[:, rows - GAIN_ROWS :].astype(f32), axis=0))
    gains = (gains[:2] + gains[2:]) * grad_scale
    high = gains.astype(bf16).astype(f32)
    padding = jnp.zeros((slots_ref.shape[0] - tokens - 4, 2 * lanes), f32)
    slots_ref[...] = jnp.concatenate(
        [slots.reshape(tokens, 2 * lanes), high, gains - high, padding], axis=0
    ).astype(bf16)


def adagrad_kernel(replicas, *refs):
    wanted_refs, grad_refs = refs[:replicas], refs[replicas : 2 * replicas]
    state_ref, update_ref, state_out_ref, gains_ref = refs[2 * replicas :]
    rows = update_ref.shape[0]
    slots = wanted_refs[0].shape[1]
    first = pl.program_id(0) * rows
    eye = iota((rows, rows), 0) == iota((rows, rows), 1)
    state_row = state_ref[...].reshape(1, rows)
    state = jnp.sum(jnp.where(eye, state_row, 0.0), axis=1, keepdims=True)
    delta = jnp.zeros(update_ref.shape, f32)
    squares = jnp.zeros((rows, 1), f32)
    gains = jnp.zeros((grad_refs[0].shape[0] - slots, update_ref.shape[1]), f32)
    for wanted_ref, grad_ref in zip(wanted_refs, grad_refs):
        hit = iota((rows, slots), 0) + first == wanted_ref[...].astype(jnp.int32)
        row_grad = mm(hit.astype(f32), grad_ref[:slots])
        mean_square = jnp.mean(row_grad * row_grad, axis=1, keepdims=True)
        delta = delta + row_grad * lax.rsqrt(state + mean_square + EPSILON)
        squares = squares + mean_square
        gains = gains + grad_ref[slots:].astype(f32)
    update_ref[...] = delta * (-LEARN_RATE / replicas)
    squares_row = jnp.sum(jnp.where(eye, squares, 0.0), axis=0, keepdims=True)
    gains_ref[...] = gains[:2] + gains[2:4]
    state_out_ref[...] = (state_row + squares_row / replicas).reshape(state_out_ref.shape)


def spread_kernel(step, replicas, part_ref, *refs):
    uvqk_ref, out_ref, uvqk_rows, out_rows, sems = refs[-5:]
    height, columns = uvqk_rows.shape
    width = out_rows.shape[1]
    part = lax.rem(lax.axis_index("replica") + (replicas - step), replicas)
    rows = pl.ds(pl.multiple_of(part * height, 8), height)
    blocks = columns // width
    for block in range(blocks):
        uvqk_rows[:, block * width : (block + 1) * width] = part_ref[
            block * height : (block + 1) * height
        ].astype(f32)
    first = pltpu.make_async_copy(uvqk_rows, uvqk_ref.at[rows], sems.at[0])
    first.start()
    out_rows[...] = part_ref[blocks * height : (blocks + 1) * height].astype(f32)
    second = pltpu.make_async_copy(out_rows, out_ref.at[rows], sems.at[1])
    second.start()
    first.wait()
    second.wait()


def hand_on(parts):
    replicas = len(parts)
    came = [parts[0]]
    for step in range(1, replicas):
        pairs = [(source, (source + step) % replicas) for source in range(replicas)]
        came.append(lax.ppermute(parts[step], "replica", pairs))
    return came


def from_all(value, replicas):
    came = hand_on([value] * replicas)
    if replicas > 2:
        order = lax.rem(lax.axis_index("replica") - jnp.arange(replicas) + replicas, replicas)
        stacked = jnp.take(jnp.stack(came), order, axis=0)
        came = [stacked[index] for index in range(replicas)]
    return came


def on_device(
    request_rows,
    token_slot,
    seq_lengths,
    cotangent,
    table_slab,
    adagrad_state,
    w_uvqk,
    w_out,
    norm_gain,
    out_gain,
):
    shards = lax.axis_size("shard")
    replicas = lax.axis_size("replica")
    tokens = token_slot.shape[1]
    rows_dev, width = table_slab.shape
    capacity = tokens // shards
    blocks = w_uvqk.shape[1] // width + 1
    share_rows = -(-blocks * width // (replicas * shards))
    part_rows = share_rows * shards
    grad_scale = 1.0 / math.sqrt(tokens * shards * replicas)
    shape = jax.ShapeDtypeStruct

    asked, small = pl.pallas_call(
        ready_kernel,
        out_shape=(
            shape((shards, 1, tokens), jnp.int32),
            shape((8, max(width, tokens)), f32),
        ),
        in_specs=[VMEM] * 5,
        out_specs=(VMEM, VMEM),
        cost_estimate=estimate(rows_dev * width * 8192, rows_dev * width * 128),
        compiler_params=room(4),
        name="ready",
    )(
        request_rows,
        token_slot,
        seq_lengths.reshape(1, -1),
        norm_gain.reshape(1, width),
        out_gain.reshape(1, width),
    )
    ids = lax.all_to_all(asked, "shard", split_axis=0, concat_axis=0, tiled=True)
    found, wanted = pl.pallas_call(
        functools.partial(fetch_kernel, capacity),
        out_shape=(shape((tokens, width), bf16), shape((1, tokens), f32)),
        in_specs=[VMEM] * 2,
        out_specs=(VMEM, VMEM),
        cost_estimate=estimate(2 * tokens * rows_dev * width, rows_dev * width * 4),
        compiler_params=room(8),
        name="fetch",
    )(ids, table_slab)
    slot_rows = lax.all_to_all(
        found.reshape(shards, capacity, width), "shard", split_axis=0, concat_axis=0, tiled=True
    ).reshape(tokens, width)

    cot = cotangent.reshape(tokens, width)
    lifted_grad, normal, gate_grad, *parts = pl.pallas_call(
        functools.partial(layer_kernel, seq_lengths.shape[-1]),
        out_shape=(
            shape((tokens, w_uvqk.shape[1]), bf16),
            shape((tokens, width + 128), f32),
            shape((1, width), f32),
        )
        + (shape((part_rows, width), bf16),) * replicas,
        in_specs=[VMEM] * 5,
        out_specs=(VMEM,) * (replicas + 3),
        scratch_shapes=[pltpu.VMEM((blocks * width, width), bf16)],
        cost_estimate=estimate(8 * tokens * width * w_uvqk.shape[1], 4 * blocks * width * width),
        compiler_params=room(20),
        name="layer",
    )(small, slot_rows, cot, w_uvqk, w_out)
    came = hand_on(parts)
    slot_grad, gain_rows = pl.pallas_call(
        finish_kernel,
        out_shape=(shape((tokens, width), bf16), shape((4, width), f32)),
        in_specs=[VMEM] * 6,
        out_specs=(VMEM, VMEM),
        cost_estimate=estimate(2 * tokens * width * w_uvqk.shape[1], 2 * blocks * width * width),
        compiler_params=room(10),
        name="finish",
    )(small, cot, w_uvqk, lifted_grad, normal, gate_grad)

    aligned = capacity % 8 == 0 and share_rows % 8 == 0
    message_rows = 2 * (capacity + share_rows) + GAIN_ROWS
    if aligned:
        message = pl.pallas_call(
            functools.partial(pack_kernel, shards),
            out_shape=shape((shards, message_rows, width // 2), bf16),
            in_specs=[VMEM] * (replicas + 2),
            out_specs=VMEM,
            compiler_params=room(10),
            name="pack",
        )(slot_grad, gain_rows, *came)
    else:
        total = sum(part.astype(f32) for part in came).astype(bf16)
        gains = jnp.broadcast_to(gain_rows.astype(bf16)[None], (shards, 4, width))
        message = jnp.concatenate(
            [
                slot_grad.reshape(shards, capacity, width),
                total.reshape(shards, share_rows, width),
                gains,
            ],
            axis=1,
        )
    arrived = lax.all_to_all(message, "shard", split_axis=0, concat_axis=0, tiled=True)
    if aligned:
        share = pl.pallas_call(
            functools.partial(unpack_kernel, capacity, grad_scale),
            out_shape=shape((shards, share_rows, width), bf16),
            in_specs=[VMEM],
            out_specs=VMEM,
            compiler_params=room(8),
            name="unpack",
        )(arrived)
        owned = pl.pallas_call(
            functools.partial(slots_kernel, capacity, grad_scale),
            out_shape=shape((tokens + GAIN_ROWS, width), bf16),
            in_specs=[VMEM],
            out_specs=VMEM,
            cost_estimate=estimate(tokens * width, 4 * tokens * width),
            compiler_params=room(6),
            name="slots",
        )(arrived)
    else:
        total = jnp.sum(arrived[:, capacity:].astype(f32), axis=0) * grad_scale
        share = jnp.broadcast_to(
            total[:share_rows].astype(bf16)[None], (shards, share_rows, width)
        )
        gains = total[share_rows : share_rows + 2] + total[share_rows + 2 :]
        high = gains.astype(bf16)
        owned = jnp.concatenate(
            [
                arrived[:, :capacity].reshape(tokens, width),
                high,
                (gains - high.astype(f32)).astype(bf16),
                jnp.zeros((GAIN_ROWS - 4, width), bf16),
            ],
            axis=0,
        )

    gathered = lax.all_to_all(share, "shard", split_axis=0, concat_axis=0, tiled=True)

    wanted_all = from_all(wanted, replicas)
    owned_all = from_all(owned, replicas)
    block = 128
    row_update, state_new, grad_gains = pl.pallas_call(
        functools.partial(adagrad_kernel, replicas),
        grid=(rows_dev // block,),
        out_shape=(
            shape((rows_dev, width), f32),
            shape((rows_dev // block, 1, block), f32),
            shape((2, width), f32),
        ),
        in_specs=[pl.BlockSpec((1, tokens), lambda step: (0, 0))] * replicas
        + [pl.BlockSpec((tokens + GAIN_ROWS, width), lambda step: (0, 0))] * replicas
        + [pl.BlockSpec((1, 1, block), lambda step: (step, 0, 0))],
        out_specs=(
            pl.BlockSpec((block, width), lambda step: (step, 0)),
            pl.BlockSpec((1, 1, block), lambda step: (step, 0, 0)),
            pl.BlockSpec((2, width), lambda step: (0, 0)),
        ),
        cost_estimate=estimate(2 * replicas * tokens * rows_dev * width, rows_dev * width * 4),
        compiler_params=room(10),
        name="adagrad",
    )(*wanted_all, *owned_all, adagrad_state.reshape(rows_dev // block, 1, block))

    halves = hand_on([gathered.reshape(part_rows, width)] * replicas)
    grads = ()
    for step, half in enumerate(halves):
        grads = pl.pallas_call(
            functools.partial(spread_kernel, step, replicas),
            out_shape=(shape(w_uvqk.shape, f32), shape(w_out.shape, f32)),
            in_specs=[VMEM] + [pl.BlockSpec(memory_space=pl.ANY)] * len(grads),
            out_specs=(pl.BlockSpec(memory_space=pl.ANY),) * 2,
            scratch_shapes=[
                pltpu.VMEM((width // replicas, w_uvqk.shape[1]), f32),
                pltpu.VMEM((width // replicas, width), f32),
                pltpu.SemaphoreType.DMA((2,)),
            ],
            input_output_aliases={1: 0, 2: 1} if grads else {},
            cost_estimate=estimate(blocks * width * width, 3 * blocks * width * width),
            compiler_params=room(6),
        )(half, *grads)
    return (row_update, state_new.reshape(rows_dev), *grads, grad_gains)


def solution(mesh):
    placed = (
        P("replica", "shard", None),
        P("replica", "shard"),
        P("replica", "shard", None),
        P("replica", "shard", None),
        P("shard", None),
        P("shard"),
        P(),
        P(),
        P(),
        P(),
    )

    return jax.shard_map(
        on_device,
        mesh=mesh,
        in_specs=placed,
        out_specs=(P("shard", None), P("shard"), P(), P(), P()),
        check_vma=False,
    )
```

time: 86.3 us -> 69.8 us (0.81)
  Pallas kernels: 18 us -> 8.96 us
  blocking collectives: 60.4 us -> 56.2 us
  local copies, waits for them, and re-layouts: 2.84 us -> 0.71 us
    all_to_all x1, blocking collectives: 18.6 us -> 16.4 us  [on_device(): lax.all_to_all(message, 'shard', split_axis=0, concat_axis=0, tiled=True)]
    pallas_call x2 -> x6, Pallas kernels: 6.51 us -> 4.34 us  [the longest x1 1.98 us: on_device(): pl.pallas_call(functools.partial(layer_kernel, seq_lengths.shape[-1]), ou...]
    unnamed x16 -> x20, local copies, waits for them, and re-layouts: 2.83 us -> 0.71 us
    pallas_call x1, Pallas kernels: 2.35 us -> 0.47 us  [on_device(): pl.pallas_call(functools.partial(fetch_kernel, capacity), out_shape=(shap...]
    pallas_call x1, Pallas kernels: 1.95 us -> 0.09 us  [on_device(): pl.pallas_call(functools.partial(pack_kernel, shards), out_shape=shape((s...]
    pallas_call x1, Pallas kernels: 1.8 us -> 0.05 us  [on_device(): pl.pallas_call(functools.partial(unpack_kernel, capacity, grad_scale), ou...]
    all_to_all x1, blocking collectives: 11.7 us -> 10.1 us  [on_device(): lax.all_to_all(found.reshape(shards, capacity, width), 'shard', split_axi...]
    pallas_call x1, Pallas kernels: 5.37 us -> 4.02 us  [on_device(): pl.pallas_call(functools.partial(adagrad_kernel, replicas), grid=(rows_de...]
  transfers between devices with their start and end apart: 4 -> 4, of which waited for: 2 -> 2; matrix products, arithmetic and copies ran while one was open for 0% -> 0% of each run, Pallas kernels for 6% -> 8%
where the time goes in v2:
time: 69.8 us; the launch traced here: 69.5 us
  blocking collectives  56.2 us (81%)
  Pallas kernels  8.96 us (13%)
  waiting for transfers between devices  2.14 us (3%)
  between operations  0.75 us (1%)
  starting transfers between devices  0.72 us (1%)
  local copies, waits for them, and re-layouts  0.71 us (1%)
    all_to_all x1, blocking collectives, on_device(): lax.all_to_all(message, 'shard', split_axis=0, concat_axis=0, tiled=True)  16.4 us
    all_to_all x1, blocking collectives, on_device(): lax.all_to_all(asked, 'shard', split_axis=0, concat_axis=0, tiled=True)  15.6 us
    all_to_all x1, blocking collectives, on_device(): lax.all_to_all(share, 'shard', split_axis=0, concat_axis=0, tiled=True)  14.2 us
    all_to_all x1, blocking collectives, on_device(): lax.all_to_all(found.reshape(shards, capacity, width), 'shard', split_axi...  10.1 us
    pallas_call x1, Pallas kernels, on_device(): pl.pallas_call(functools.partial(adagrad_kernel, replicas), grid=(rows_de...  4.02 us
    ppermute x4, waiting for transfers between devices, hand_on(): came.append(lax.ppermute(parts[step], 'replica', pairs))  2.14 us
    pallas_call x1, Pallas kernels, on_device(): pl.pallas_call(functools.partial(layer_kernel, seq_lengths.shape[-1]), ou...  1.98 us
    pallas_call x2, Pallas kernels, on_device(): pl.pallas_call(functools.partial(spread_kernel, step, replicas), out_shap...  1.76 us
  transfers between devices with their start and end apart: 4, of which 2 were waited for; matrix products, arithmetic and copies ran while one was open for 0% of the time, Pallas kernels for 8%

profile of v2, /device:TPU:0, one launch (start us, length us, event | category | flops | bytes accessed | tf_op | source)
XLA Modules:
  0.0 69.5 jit_solution(10409069347709533260)
XLA Ops:
  0.6 0.0 copy-start.6
  0.6 0.0 copy-start.8
  0.7 0.0 copy-start.9
  0.7 0.0 copy-start.5
  0.7 0.0 copy-start.7
  0.7 0.6 copy-done.6
  1.3 0.0 copy-done.8
  1.3 0.0 copy-done.9
  1.3 0.0 copy-done.5
  1.4 0.0 copy-done.7
  1.4 15.6 %all_to_all.20.ids_ref = s32[16,1,128]{2,1,0:T(1,128)S(1)} all-to-all(s32[16,1,128]{2,1,0:T(1,128)S(1)} %get-tuple-element.23), channel_id=1, replica_groups=mesh['shard'=16,'replica'=2] {'shard'}, dimensions={0} | all-to-all | bytes 16384 | tf_op jit(solution)/shard_map/all_to_all | solution.py:362
  17.0 0.0 copy-done
  17.0 0.5 fetch.1
  17.4 0.0 copy-start.2
  17.4 10.1 %all_to_all.21 = bf16[16,8,256]{2,1,0:T(8,128)(2,1)S(1)} all-to-all(bf16[16,8,256]{2,1,0:T(8,128)(2,1)S(1)} %bitcast.14), channel_id=1, replica_groups=mesh['shard'=16,'replica'=2] {'shard'}, dimensions={0} | all-to-all | bytes 131072 | tf_op jit(solution)/shard_map/all_to_all | solution.py:372
  27.6 2.0 %layer.1 = (bf16[128,1024]{1,0:T(8,128)(2,1)S(1)}, f32[128,384]{1,0:T(8,128)S(1)}, f32[1,256]{1,0:T(1,128)S(1)}, bf16[640,256]{1,0:T(8,128)(2,1)S(1)}, bf16[640,256]{1,0:T(8,128)(2,1)S(1)}) custom-call(f32[8,256]{1,0:T(8,128)S(1)} %get-tuple-element.25.small_ref, bf16[128,256]{1,0:T(8,128)(2,1)S(1)} %bitcast.13, bf16[128,256]{1,0:T(8,128)(2,1)S(1)} %bitcast.11, ...), custom_call_target="tpu_custom_call" | custom-call | flops 268435456 | bytes 1310720 | tf_op jit(solution)/shard_map/layer/pallas_call | solution.py:377
  29.6 0.1 collective-permute-start.1
  29.6 0.6 finish.1
  30.2 1.1 %collective-permute-done.1.refs_1_ = bf16[640,256]{1,0:T(8,128)(2,1)S(1)} collective-permute-done((bf16[640,256]{1,0:T(8,128)(2,1)S(1)}, bf16[640,256]{1,0:T(8,128)(2,1)S(1)}, u32[]{:S(2)}, u32[]{:S(2)}) %collective-permute-start.1) | collective-permute-done | bytes 327712 | tf_op jit(solution)/shard_map/ppermute | solution.py:308
  31.3 0.1 pack.1
  31.4 16.4 %all_to_all.22.in_ref = bf16[16,104,128]{2,1,0:T(8,128)(2,1)S(1)} all-to-all(bf16[16,104,128]{2,1,0:T(8,128)(2,1)S(1)} %pack.1), channel_id=1, replica_groups=mesh['shard'=16,'replica'=2] {'shard'}, dimensions={0} | all-to-all | bytes 851968 | tf_op jit(solution)/shard_map/all_to_all | solution.py:425
  47.7 0.1 unpack.1
  47.8 14.2 %all_to_all.23 = bf16[16,40,256]{2,1,0:T(8,128)(2,1)S(1)} all-to-all(bf16[16,40,256]{2,1,0:T(8,128)(2,1)S(1)} %unpack.1), channel_id=1, replica_groups=mesh['shard'=16,'replica'=2] {'shard'}, dimensions={0} | all-to-all | bytes 655360 | tf_op jit(solution)/shard_map/all_to_all | solution.py:461
  61.9 0.0 collective-permute-start.3
  62.0 0.6 collective-permute-start.2
  62.6 0.1 collective-permute-start
  62.6 1.1 %collective-permute-done.refs_1_ = f32[1,128]{1,0:T(1,128)S(1)} collective-permute-done((f32[1,128]{1,0:T(1,128)S(1)}, f32[1,128]{1,0:T(1,128)S(1)}, u32[]{:S(2)}, u32[]{:S(2)}) %collective-permute-start) | collective-permute-done | bytes 544 | tf_op jit(solution)/shard_map/ppermute | solution.py:308
  63.7 0.0 collective-permute-done.2.refs_3_
  63.7 4.0 %adagrad.1 = (f32[1024,256]{1,0:T(8,128)}, f32[8,1,128]{2,1,0:T(1,128)}, f32[2,256]{1,0:T(2,128)}) custom-call(f32[1,128]{1,0:T(1,128)S(1)} %get-tuple-element.24.refs_0_, f32[1,128]{1,0:T(1,128)S(1)} %collective-permute-done.refs_1_, bf16[136,256]{1,0:T(8,128)(2,1)S(1)} %slots.1.refs_2_, bf16[136,256]{1,0:T(8,128)(2,1)S(1)} %collective-permute-done.2.refs_3_, ...), custom_call_target="tpu_custom_call" | custom-call | flops 134217728 | bytes 1048576 | tf_op jit(solution)/shard_map/adagrad/pallas_call | solution.py:466
  67.7 0.9 %shard_map.137 = (f32[256,1024]{1,0:T(8,128)}, f32[256,256]{1,0:T(8,128)}) custom-call(bf16[640,256]{1,0:T(8,128)(2,1)S(1)} %bitcast.10), custom_call_target="tpu_custom_call" | custom-call | flops 327680 | bytes 983040 | tf_op jit(solution)/shard_map/pallas_call | solution.py:490
  68.6 0.0 collective-permute-done.3.part_ref
  68.6 0.9 %shard_map.138 = (f32[256,1024]{1,0:T(8,128)}, f32[256,256]{1,0:T(8,128)}) custom-call(bf16[640,256]{1,0:T(8,128)(2,1)S(1)} %collective-permute-done.3.part_ref, f32[256,1024]{1,0:T(8,128)} %get-tuple-element.36.refs_0_, f32[256,256]{1,0:T(8,128)} %get-tuple-element.37.refs_1_), custom_call_target="tpu_custom_call", output_to_operand_aliasing={{0}: (1, {}), {1}: (2, {})} | custom-call | flops 327680 | bytes 983040 | tf_op jit(solution)/shard_map/pallas_call | solution.py:490
  (10 shorter events, 0.1 us)
Async XLA Ops:
  0.6 0.7 copy-start.6
  0.6 0.7 copy-start.8
  0.7 0.7 copy-start.9
  0.7 0.7 %copy-start.5 = (f32[256]{0:T(256)S(1)}, f32[256]{0:T(256)}, u32[]{:S(2)}) copy-start(f32[256]{0:T(256)} %param.18) | copy-start | bytes 3076
  0.7 0.7 copy-start.7
  1.4 15.6 %copy-start = (f32[1024,256]{1,0:T(8,128)S(1)}, f32[1024,256]{1,0:T(8,128)}, u32[]{:S(2)}) copy-start(f32[1024,256]{1,0:T(8,128)} %table_ref.1) | copy-start | bytes 3145732
  17.0 10.6 %copy-start.1 = (bf16[256,1024]{1,0:T(8,128)(2,1)S(1)}, bf16[256,1024]{1,0:T(8,128)(2,1)}, u32[]{:S(2)}) copy-start(bf16[256,1024]{1,0:T(8,128)(2,1)} %w_ref.3) | copy-start | bytes 1572868
  17.0 10.6 %copy-start.3 = (bf16[256,256]{1,0:T(8,128)(2,1)S(1)}, bf16[256,256]{1,0:T(8,128)(2,1)}, u32[]{:S(2)}) copy-start(bf16[256,256]{1,0:T(8,128)(2,1)} %wo_ref.1) | copy-start | bytes 393220
  17.4 10.1 %copy-start.2 = (bf16[1,128,256]{2,1,0:T(8,128)(2,1)S(1)}, bf16[1,128,256]{2,1,0:T(8,128)(2,1)}, u32[]{:S(2)}) copy-start(bf16[1,128,256]{2,1,0:T(8,128)(2,1)} %param.13) | copy-start | bytes 196612
  29.6 1.7 %collective-permute-start.1 = (bf16[640,256]{1,0:T(8,128)(2,1)S(1)}, bf16[640,256]{1,0:T(8,128)(2,1)S(1)}, u32[]{:S(2)}, u32[]{:S(2)}) collective-permute-start(bf16[640,256]{1,0:T(8,128)(2,1)S(1)} %get-tuple-element.33), channel_id=1, source_target_pairs={{0,1},{1,0},{2,3},{3,2},{4,5},{5,4},{6,7},{7,6},{8,9},{9,8},{10,11... | collective-permute-start | bytes 983048 | tf_op jit(solution)/shard_map/ppermute | solution.py:308
  61.9 1.8 %copy-start.4 = (f32[1024]{0:T(1024)S(1)}, f32[1024]{0:T(1024)}, u32[]{:S(2)}) copy-start(f32[1024]{0:T(1024)} %param.15) | copy-start | bytes 12292
  61.9 6.7 %collective-permute-start.3 = (bf16[640,256]{1,0:T(8,128)(2,1)S(1)}, bf16[640,256]{1,0:T(8,128)(2,1)S(1)}, u32[]{:S(2)}, u32[]{:S(2)}) collective-permute-start(bf16[640,256]{1,0:T(8,128)(2,1)S(1)} %bitcast.9), channel_id=1, source_target_pairs={{0,1},{1,0},{2,3},{3,2},{4,5},{5,4},{6,7},{7,6},{8,9},{9,8},{10,11... | collective-permute-start | bytes 983048 | tf_op jit(solution)/shard_map/ppermute | solution.py:308
  62.0 1.7 %collective-permute-start.2 = (bf16[136,256]{1,0:T(8,128)(2,1)S(1)}, bf16[136,256]{1,0:T(8,128)(2,1)S(1)}, u32[]{:S(2)}, u32[]{:S(2)}) collective-permute-start(bf16[136,256]{1,0:T(8,128)(2,1)S(1)} %slots.1.refs_2_), channel_id=1, source_target_pairs={{0,1},{1,0},{2,3},{3,2},{4,5},{5,4},{6,7},{7,6},{8,9},{9,8},{10,11... | collective-permute-start | bytes 208904 | tf_op jit(solution)/shard_map/ppermute | solution.py:308
  62.6 1.2 %collective-permute-start = (f32[1,128]{1,0:T(1,128)S(1)}, f32[1,128]{1,0:T(1,128)S(1)}, u32[]{:S(2)}, u32[]{:S(2)}) collective-permute-start(f32[1,128]{1,0:T(1,128)S(1)} %get-tuple-element.24.refs_0_), channel_id=1, source_target_pairs={{0,1},{1,0},{2,3},{3,2},{4,5},{5,4},{6,7},{7,6},{8,9},{9,8},{10,11... | collective-permute-start | bytes 1544 | tf_op jit(solution)/shard_map/ppermute | solution.py:308

commit v3 on v2

--- a/solution.py
+++ b/solution.py
@@ -216,43 +216,68 @@
     return jnp.concatenate([values[..., :rows, :], values[..., rows:, :]], axis=-1)
 
 
-def pack_kernel(shards, slot_grad_ref, gain_ref, *refs):
+def pack_kernel(group, slot_grad_ref, gain_ref, *refs):
     part_refs, out_ref = refs[:-1], refs[-1]
-    width = slot_grad_ref.shape[1]
+    half_slots, width = slot_grad_ref.shape[0] // 2, slot_grad_ref.shape[1]
     total = part_refs[0][...].astype(f32)
     for part_ref in part_refs[1:]:
         total = total + part_ref[...].astype(f32)
-    share = total.reshape(shards, -1, width)
+    half = lax.axis_index("shard") // group
+
+    def slots_of(which):
+        rows = pl.ds(pl.multiple_of(which * half_slots, 16), half_slots)
+        return halves_down(slot_grad_ref[rows].astype(f32).reshape(group, -1, width))
+
     gains = halves_down(gain_ref[...])
-    gains = jnp.broadcast_to(gains[None], (shards,) + gains.shape)
-    slots = slot_grad_ref[...].astype(f32).reshape(shards, -1, width)
     out_ref[...] = jnp.concatenate(
-        [halves_down(slots), halves_down(share), gains], axis=1
+        [
+            slots_of(half),
+            slots_of(1 - half),
+            halves_down(total.reshape(group, -1, width)),
+            jnp.broadcast_to(gains[None], (group,) + gains.shape),
+        ],
+        axis=1,
     ).astype(bf16)
 
 
-def unpack_kernel(capacity, grad_scale, in_ref, share_ref):
-    shards, rows, _ = in_ref.shape
-    wanted = slice(2 * capacity, rows - GAIN_ROWS)
-    total = in_ref[0, wanted].astype(f32)
-    for shard in range(1, shards):
-        total = total + in_ref[shard, wanted].astype(f32)
-    share = halves_across(total * grad_scale).astype(bf16)
-    for shard in range(shards):
-        share_ref[shard] = share
-
-
-def slots_kernel(capacity, grad_scale, in_ref, slots_ref):
-    shards, rows, lanes = in_ref.shape
-    tokens = shards * capacity
-    slots = halves_across(in_ref[:, : 2 * capacity].astype(f32))
-    gains = halves_across(jnp.sum(in_ref[:, rows - GAIN_ROWS :].astype(f32), axis=0))
-    gains = (gains[:2] + gains[2:]) * grad_scale
-    high = gains.astype(bf16).astype(f32)
-    padding = jnp.zeros((slots_ref.shape[0] - tokens - 4, 2 * lanes), f32)
-    slots_ref[...] = jnp.concatenate(
-        [slots.reshape(tokens, 2 * lanes), high, gains - high, padding], axis=0
-    ).astype(bf16)
+def as_two(values):
+    high = values.astype(bf16).astype(f32)
+    return jnp.concatenate([high, values - high], axis=0)
+
+
+def cross_kernel(capacity, in_ref, cross_ref, mine_ref):
+    group, _, lanes = in_ref.shape
+    slots = 2 * capacity
+    mine_ref[...] = halves_across(in_ref[:, :slots].astype(f32)).reshape(mine_ref.shape).astype(bf16)
+    theirs = halves_across(in_ref[:, slots : 2 * slots].astype(f32)).reshape(mine_ref.shape)
+    total = in_ref[0, 2 * slots :].astype(f32)
+    for peer in range(1, group):
+        total = total + in_ref[peer, 2 * slots :].astype(f32)
+    gains = halves_across(total[-GAIN_ROWS:])
+    gains = as_two(gains[:2] + gains[2:])
+    padding = jnp.zeros((GAIN_ROWS - gains.shape[0], 2 * lanes), f32)
+    share = halves_across(total[:-GAIN_ROWS])
+    cross_ref[...] = jnp.concatenate([theirs, share, gains, padding], axis=0).astype(bf16)
+
+
+def share_kernel(grad_scale, mine_ref, other_ref, share_ref):
+    group, rows, _ = share_ref.shape
+    first = mine_ref.shape[0] - GAIN_ROWS - rows
+    total = mine_ref[first : first + rows].astype(f32) + other_ref[first : first + rows].astype(f32)
+    share = (total * grad_scale).astype(bf16)
+    for peer in range(group):
+        share_ref[peer] = share
+
+
+def slots_kernel(group, grad_scale, slots_ref, mine_ref, other_ref, owned_ref):
+    rows = slots_ref.shape[0]
+    half = lax.axis_index("shard") // group
+    owned_ref[pl.ds(pl.multiple_of(half * rows, 16), rows)] = slots_ref[...]
+    owned_ref[pl.ds(pl.multiple_of((1 - half) * rows, 16), rows)] = other_ref[:rows]
+    gains = mine_ref[-GAIN_ROWS:].astype(f32) + other_ref[-GAIN_ROWS:].astype(f32)
+    gains = as_two((gains[:2] + gains[2:4]) * grad_scale)
+    padding = jnp.zeros((GAIN_ROWS - gains.shape[0], gains.shape[1]), f32)
+    owned_ref[2 * rows :] = jnp.concatenate([gains, padding], axis=0).astype(bf16)
 
 
 def adagrad_kernel(replicas, *refs):
@@ -336,8 +361,11 @@
     rows_dev, width = table_slab.shape
     capacity = tokens // shards
     blocks = w_uvqk.shape[1] // width + 1
-    share_rows = -(-blocks * width // (replicas * shards))
-    part_rows = share_rows * shards
+    group = shards // 2
+    share_rows = -(-blocks * width // (replicas * group))
+    part_rows = share_rows * group
+    in_half = [list(range(group)), list(range(group, shards))]
+    half_slots = group * capacity
     grad_scale = 1.0 / math.sqrt(tokens * shards * replicas)
     shape = jax.ShapeDtypeStruct
 
@@ -401,64 +429,82 @@
     )(small, cot, w_uvqk, lifted_grad, normal, gate_grad)
 
     aligned = capacity % 8 == 0 and share_rows % 8 == 0
-    message_rows = 2 * (capacity + share_rows) + GAIN_ROWS
+    message_rows = 2 * (2 * capacity + share_rows) + GAIN_ROWS
     if aligned:
         message = pl.pallas_call(
-            functools.partial(pack_kernel, shards),
-            out_shape=shape((shards, message_rows, width // 2), bf16),
+            functools.partial(pack_kernel, group),
+            out_shape=shape((group, message_rows, width // 2), bf16),
             in_specs=[VMEM] * (replicas + 2),
             out_specs=VMEM,
             compiler_params=room(10),
             name="pack",
         )(slot_grad, gain_rows, *came)
     else:
+        half = lax.axis_index("shard") // group
+        by_half = slot_grad.reshape(2, group, capacity, width)
         total = sum(part.astype(f32) for part in came).astype(bf16)
-        gains = jnp.broadcast_to(gain_rows.astype(bf16)[None], (shards, 4, width))
         message = jnp.concatenate(
             [
-                slot_grad.reshape(shards, capacity, width),
-                total.reshape(shards, share_rows, width),
-                gains,
+                jnp.take(by_half, half, axis=0),
+                jnp.take(by_half, 1 - half, axis=0),
+                total.reshape(group, share_rows, width),
+                jnp.broadcast_to(gain_rows.astype(bf16)[None], (group, 4, width)),
             ],
             axis=1,
         )
-    arrived = lax.all_to_all(message, "shard", split_axis=0, concat_axis=0, tiled=True)
+    arrived = lax.all_to_all(
+        message, "shard", split_axis=0, concat_axis=0, tiled=True, axis_index_groups=in_half
+    )
+    cross_rows = half_slots + share_rows + GAIN_ROWS
+    if aligned:
+        cross, mine = pl.pallas_call(
+            functools.partial(cross_kernel, capacity),
+            out_shape=(shape((cross_rows, width), bf16), shape((half_slots, width), bf16)),
+            in_specs=[VMEM],
+            out_specs=(VMEM, VMEM),
+            compiler_params=room(8),
+            name="cross",
+        )(arrived)
+    else:
+        mine = arrived[:, :capacity].reshape(half_slots, width)
+        theirs = arrived[:, capacity : 2 * capacity].reshape(half_slots, width)
+        total = jnp.sum(arrived[:, 2 * capacity :].astype(f32), axis=0)
+        gains = as_two(total[share_rows : share_rows + 2] + total[share_rows + 2 :]).astype(bf16)
+        padding = jnp.zeros((GAIN_ROWS - 4, width), bf16)
+        cross = jnp.concatenate([theirs, total[:share_rows].astype(bf16), gains, padding], axis=0)
+    mirror = [(source, (source + group) % shards) for source in range(shards)]
+    other = lax.ppermute(cross, "shard", mirror)
     if aligned:
         share = pl.pallas_call(
-            functools.partial(unpack_kernel, capacity, grad_scale),
-            out_shape=shape((shards, share_rows, width), bf16),
-            in_specs=[VMEM],
+            functools.partial(share_kernel, grad_scale),
+            out_shape=shape((group, share_rows, width), bf16),
+            in_specs=[VMEM] * 2,
             out_specs=VMEM,
-            compiler_params=room(8),
-            name="unpack",
-        )(arrived)
+            compiler_params=room(4),
+            name="share",
+        )(cross, other)
         owned = pl.pallas_call(
-            functools.partial(slots_kernel, capacity, grad_scale),
+            functools.partial(slots_kernel, group, grad_scale),
             out_shape=shape((tokens + GAIN_ROWS, width), bf16),
-            in_specs=[VMEM],
+            in_specs=[VMEM] * 3,
             out_specs=VMEM,
             cost_estimate=estimate(tokens * width, 4 * tokens * width),
-            compiler_params=room(6),
+            compiler_params=room(4),
             name="slots",
-        )(arrived)
+        )(mine, cross, other)
     else:
-        total = jnp.sum(arrived[:, capacity:].astype(f32), axis=0) * grad_scale
+        total = (cross[half_slots:].astype(f32) + other[half_slots:].astype(f32)) * grad_scale
         share = jnp.broadcast_to(
-            total[:share_rows].astype(bf16)[None], (shards, share_rows, width)
+            total[:share_rows].astype(bf16)[None], (group, share_rows, width)
         )
-        gains = total[share_rows : share_rows + 2] + total[share_rows + 2 :]
-        high = gains.astype(bf16)
-        owned = jnp.concatenate(
-            [
-                arrived[:, :capacity].reshape(tokens, width),
-                high,
-                (gains - high.astype(f32)).astype(bf16),
-                jnp.zeros((GAIN_ROWS - 4, width), bf16),
-            ],
-            axis=0,
-        )
-
-    gathered = lax.all_to_all(share, "shard", split_axis=0, concat_axis=0, tiled=True)
+        gains = as_two(total[share_rows : share_rows + 2] + total[share_rows + 2 : share_rows + 4])
+        by_half = jnp.stack([mine, other[:half_slots]])
+        by_half = jnp.where(half == 0, by_half, by_half[::-1]).reshape(tokens, width)
+        owned = jnp.concatenate([by_half, gains.astype(bf16), padding], axis=0)
+
+    gathered = lax.all_to_all(
+        share, "shard", split_axis=0, concat_axis=0, tiled=True, axis_index_groups=in_half
+    )
 
     wanted_all = from_all(wanted, replicas)
     owned_all = from_all(owned, replicas)

time: 69.8 us -> 66.5 us (0.953)
  blocking collectives: 56.2 us -> 46.6 us
  waiting for transfers between devices: 2.14 us -> 7.53 us
  starting transfers between devices: 0.72 us -> 1.52 us
    all_to_all x2, blocking collectives: 30.5 us -> 20.9 us  [the longest x1 11.3 us: on_device(): lax.all_to_all(message, 'shard', split_axis=0, concat_axis=0, tiled=True,...]
    ppermute x0 -> x1, waiting for transfers between devices: none -> 5.39 us  [on_device(): other = lax.ppermute(cross, 'shard', mirror)]
    ppermute x0 -> x1, starting transfers between devices: none -> 0.8 us  [on_device(): other = lax.ppermute(cross, 'shard', mirror)]
  transfers between devices with their start and end apart: 4 -> 5, of which waited for: 2 -> 3; matrix products, arithmetic and copies ran while one was open for 0% -> 0% of each run, Pallas kernels for 8% -> 8%
where the time goes in v3:
time: 66.5 us; the launch traced here: 66.1 us
  blocking collectives  46.6 us (70%)
  Pallas kernels  8.99 us (14%)
  waiting for transfers between devices  7.53 us (11%)
  starting transfers between devices  1.52 us (2%)
  between operations  0.76 us (1%)
  local copies, waits for them, and re-layouts  0.71 us (1%)
    all_to_all x1, blocking collectives, on_device(): lax.all_to_all(asked, 'shard', split_axis=0, concat_axis=0, tiled=True)  15.6 us
    all_to_all x1, blocking collectives, on_device(): lax.all_to_all(message, 'shard', split_axis=0, concat_axis=0, tiled=True,...  11.3 us
    all_to_all x1, blocking collectives, on_device(): lax.all_to_all(found.reshape(shards, capacity, width), 'shard', split_axi...  10.1 us
    all_to_all x1, blocking collectives, on_device(): lax.all_to_all(share, 'shard', split_axis=0, concat_axis=0, tiled=True, a...  9.62 us
    ppermute x1, waiting for transfers between devices, on_device(): other = lax.ppermute(cross, 'shard', mirror)  5.39 us
    pallas_call x1, Pallas kernels, on_device(): pl.pallas_call(functools.partial(adagrad_kernel, replicas), grid=(rows_de...  4.02 us
    ppermute x4, waiting for transfers between devices, hand_on(): came.append(lax.ppermute(parts[step], 'replica', pairs))  2.14 us
    pallas_call x1, Pallas kernels, on_device(): pl.pallas_call(functools.partial(layer_kernel, seq_lengths.shape[-1]), ou...  1.98 us
  transfers between devices with their start and end apart: 5, of which 3 were waited for; matrix products, arithmetic and copies ran while one was open for 0% of the time, Pallas kernels for 8%

profile of v3, /device:TPU:0, one launch (start us, length us, event | category | flops | bytes accessed | tf_op | source)
XLA Modules:
  0.0 66.1 jit_solution(8584306617934030179)
XLA Ops:
  0.6 0.0 copy-start.6
  0.6 0.0 copy-start.8
  0.7 0.0 copy-start.9
  0.7 0.6 copy-done.6
  1.3 0.0 copy-done.9
  1.3 0.0 copy-done.5
  1.4 0.0 copy-done.7
  1.4 15.6 %all_to_all.20.ids_ref = s32[16,1,128]{2,1,0:T(1,128)S(1)} all-to-all(s32[16,1,128]{2,1,0:T(1,128)S(1)} %get-tuple-element.25), channel_id=1, replica_groups=mesh['shard'=16,'replica'=2] {'shard'}, dimensions={0} | all-to-all | bytes 16384 | tf_op jit(solution)/shard_map/all_to_all | solution.py:390
  17.0 0.0 copy-done
  17.0 0.5 fetch.1
  17.4 0.0 copy-start.2
  17.4 10.1 %all_to_all.21 = bf16[16,8,256]{2,1,0:T(8,128)(2,1)S(1)} all-to-all(bf16[16,8,256]{2,1,0:T(8,128)(2,1)S(1)} %bitcast.14), channel_id=1, replica_groups=mesh['shard'=16,'replica'=2] {'shard'}, dimensions={0} | all-to-all | bytes 131072 | tf_op jit(solution)/shard_map/all_to_all | solution.py:400
  27.6 2.0 %layer.1 = (bf16[128,1024]{1,0:T(8,128)(2,1)S(1)}, f32[128,384]{1,0:T(8,128)S(1)}, f32[1,256]{1,0:T(1,128)S(1)}, bf16[640,256]{1,0:T(8,128)(2,1)S(1)}, bf16[640,256]{1,0:T(8,128)(2,1)S(1)}) custom-call(f32[8,256]{1,0:T(8,128)S(1)} %get-tuple-element.27.small_ref, bf16[128,256]{1,0:T(8,128)(2,1)S(1)} %bitcast.13, bf16[128,256]{1,0:T(8,128)(2,1)S(1)} %bitcast.11, ...), custom_call_target="tpu_custom_call" | custom-call | flops 268435456 | bytes 1310720 | tf_op jit(solution)/shard_map/layer/pallas_call | solution.py:405
  29.6 0.1 collective-permute-start.1
  29.6 0.6 finish.1
  30.2 1.1 %collective-permute-done.1.refs_1_ = bf16[640,256]{1,0:T(8,128)(2,1)S(1)} collective-permute-done((bf16[640,256]{1,0:T(8,128)(2,1)S(1)}, bf16[640,256]{1,0:T(8,128)(2,1)S(1)}, u32[]{:S(2)}, u32[]{:S(2)}) %collective-permute-start.1) | collective-permute-done | bytes 327712 | tf_op jit(solution)/shard_map/ppermute | solution.py:333
  31.3 0.1 pack.1
  31.4 11.3 %all_to_all.22.in_ref = bf16[8,200,128]{2,1,0:T(8,128)(2,1)S(1)} all-to-all(bf16[8,200,128]{2,1,0:T(8,128)(2,1)S(1)} %pack.1), channel_id=1, replica_groups={{0,2,4,6,8,10,12,14},{16,18,20,22,24,26,28,30},{1,3,5,7,9,11,13,15},{17..., dimensions={0} | all-to-all | bytes 819200 | tf_op jit(solution)/shard_map/all_to_all | solution.py:455
  42.7 0.1 cross.1
  42.7 0.8 %collective-permute-start.2 = (bf16[152,256]{1,0:T(8,128)(2,1)S(1)}, bf16[152,256]{1,0:T(8,128)(2,1)S(1)}, u32[]{:S(2)}, u32[]{:S(2)}) collective-permute-start(bf16[152,256]{1,0:T(8,128)(2,1)S(1)} %get-tuple-element.37.mine_ref), channel_id=1, source_target_pairs={{0,16},{2,18},{4,20},{6,22},{8,24},{10,26},{12,28},{14,30},{16,0},... | collective-permute-start | bytes 233480 | tf_op jit(solution)/shard_map/ppermute | solution.py:476
  43.5 5.4 %collective-permute-done.2.other_ref = bf16[152,256]{1,0:T(8,128)(2,1)S(1)} collective-permute-done((bf16[152,256]{1,0:T(8,128)(2,1)S(1)}, bf16[152,256]{1,0:T(8,128)(2,1)S(1)}, u32[]{:S(2)}, u32[]{:S(2)}) %collective-permute-start.2) | collective-permute-done | bytes 77856 | tf_op jit(solution)/shard_map/ppermute | solution.py:476
  49.0 9.6 %all_to_all.23 = bf16[8,80,256]{2,1,0:T(8,128)(2,1)S(1)} all-to-all(bf16[8,80,256]{2,1,0:T(8,128)(2,1)S(1)} %share.1), channel_id=1, replica_groups={{0,2,4,6,8,10,12,14},{16,18,20,22,24,26,28,30},{1,3,5,7,9,11,13,15},{17..., dimensions={0} | all-to-all | bytes 655360 | tf_op jit(solution)/shard_map/all_to_all | solution.py:505
  58.6 0.0 collective-permute-start.4
  58.6 0.6 collective-permute-start.3
  59.2 0.1 collective-permute-start
  59.3 1.1 %collective-permute-done.refs_1_ = f32[1,128]{1,0:T(1,128)S(1)} collective-permute-done((f32[1,128]{1,0:T(1,128)S(1)}, f32[1,128]{1,0:T(1,128)S(1)}, u32[]{:S(2)}, u32[]{:S(2)}) %collective-permute-start) | collective-permute-done | bytes 544 | tf_op jit(solution)/shard_map/ppermute | solution.py:333
  60.3 0.0 collective-permute-done.3.refs_3_
  60.3 0.0 copy-done.4
  60.3 4.0 %adagrad.1 = (f32[1024,256]{1,0:T(8,128)}, f32[8,1,128]{2,1,0:T(1,128)}, f32[2,256]{1,0:T(2,128)}) custom-call(f32[1,128]{1,0:T(1,128)S(1)} %get-tuple-element.26.refs_0_, f32[1,128]{1,0:T(1,128)S(1)} %collective-permute-done.refs_1_, bf16[136,256]{1,0:T(8,128)(2,1)S(1)} %slots.1.refs_2_, bf16[136,256]{1,0:T(8,128)(2,1)S(1)} %collective-permute-done.3.refs_3_, ...), custom_call_target="tpu_custom_call" | custom-call | flops 134217728 | bytes 1048576 | tf_op jit(solution)/shard_map/adagrad/pallas_call | solution.py:512
  64.4 0.9 %shard_map.137 = (f32[256,1024]{1,0:T(8,128)}, f32[256,256]{1,0:T(8,128)}) custom-call(bf16[640,256]{1,0:T(8,128)(2,1)S(1)} %bitcast.10), custom_call_target="tpu_custom_call" | custom-call | flops 327680 | bytes 983040 | tf_op jit(solution)/shard_map/pallas_call | solution.py:536
  65.3 0.0 collective-permute-done.4.part_ref
  65.3 0.9 %shard_map.138 = (f32[256,1024]{1,0:T(8,128)}, f32[256,256]{1,0:T(8,128)}) custom-call(bf16[640,256]{1,0:T(8,128)(2,1)S(1)} %collective-permute-done.4.part_ref, f32[256,1024]{1,0:T(8,128)} %get-tuple-element.40.refs_0_, f32[256,256]{1,0:T(8,128)} %get-tuple-element.41.refs_1_), custom_call_target="tpu_custom_call", output_to_operand_aliasing={{0}: (1, {}), {1}: (2, {})} | custom-call | flops 327680 | bytes 983040 | tf_op jit(solution)/shard_map/pallas_call | solution.py:536
  (13 shorter events, 0.1 us)
Async XLA Ops:
  0.6 0.7 %copy-start.6 = (f32[256]{0:T(256)S(1)}, f32[256]{0:T(256)}, u32[]{:S(2)}) copy-start(f32[256]{0:T(256)} %param.19) | copy-start | bytes 3076
  0.6 0.7 %copy-start.8 = (s32[1,128]{1,0:T(1,128)S(1)}, s32[1,128]{1,0:T(1,128)}, u32[]{:S(2)}) copy-start(s32[1,128]{1,0:T(1,128)} %slot_ref.1) | copy-start | bytes 1540
  0.7 0.7 %copy-start.9 = (s32[1,1,8]{2,1,0:T(1,128)S(1)}, s32[1,1,8]{2,1,0:T(1,128)}, u32[]{:S(2)}) copy-start(s32[1,1,8]{2,1,0:T(1,128)} %param.12) | copy-start | bytes 100
  0.7 0.7 %copy-start.5 = (f32[256]{0:T(256)S(1)}, f32[256]{0:T(256)}, u32[]{:S(2)}) copy-start(f32[256]{0:T(256)} %param.18) | copy-start | bytes 3076
  0.7 0.7 %copy-start.7 = (s32[1,1,128]{2,1,0:T(1,128)S(1)}, s32[1,1,128]{2,1,0:T(1,128)}, u32[]{:S(2)}) copy-start(s32[1,1,128]{2,1,0:T(1,128)} %asked_ref.1) | copy-start | bytes 1540
  1.4 15.6 %copy-start = (f32[1024,256]{1,0:T(8,128)S(1)}, f32[1024,256]{1,0:T(8,128)}, u32[]{:S(2)}) copy-start(f32[1024,256]{1,0:T(8,128)} %table_ref.1) | copy-start | bytes 3145732
  17.0 10.6 %copy-start.1 = (bf16[256,1024]{1,0:T(8,128)(2,1)S(1)}, bf16[256,1024]{1,0:T(8,128)(2,1)}, u32[]{:S(2)}) copy-start(bf16[256,1024]{1,0:T(8,128)(2,1)} %w_ref.3) | copy-start | bytes 1572868
  17.0 10.6 %copy-start.3 = (bf16[256,256]{1,0:T(8,128)(2,1)S(1)}, bf16[256,256]{1,0:T(8,128)(2,1)}, u32[]{:S(2)}) copy-start(bf16[256,256]{1,0:T(8,128)(2,1)} %wo_ref.1) | copy-start | bytes 393220
  17.4 10.1 %copy-start.2 = (bf16[1,128,256]{2,1,0:T(8,128)(2,1)S(1)}, bf16[1,128,256]{2,1,0:T(8,128)(2,1)}, u32[]{:S(2)}) copy-start(bf16[1,128,256]{2,1,0:T(8,128)(2,1)} %param.13) | copy-start | bytes 196612
  29.6 1.7 %collective-permute-start.1 = (bf16[640,256]{1,0:T(8,128)(2,1)S(1)}, bf16[640,256]{1,0:T(8,128)(2,1)S(1)}, u32[]{:S(2)}, u32[]{:S(2)}) collective-permute-start(bf16[640,256]{1,0:T(8,128)(2,1)S(1)} %get-tuple-element.35), channel_id=1, source_target_pairs={{0,1},{1,0},{2,3},{3,2},{4,5},{5,4},{6,7},{7,6},{8,9},{9,8},{10,11... | collective-permute-start | bytes 983048 | tf_op jit(solution)/shard_map/ppermute | solution.py:333
  42.7 6.2 %collective-permute-start.2 = (bf16[152,256]{1,0:T(8,128)(2,1)S(1)}, bf16[152,256]{1,0:T(8,128)(2,1)S(1)}, u32[]{:S(2)}, u32[]{:S(2)}) collective-permute-start(bf16[152,256]{1,0:T(8,128)(2,1)S(1)} %get-tuple-element.37.mine_ref), channel_id=1, source_target_pairs={{0,16},{2,18},{4,20},{6,22},{8,24},{10,26},{12,28},{14,30},{16,0},... | collective-permute-start | bytes 233480 | tf_op jit(solution)/shard_map/ppermute | solution.py:476
  58.6 6.7 %collective-permute-start.4 = (bf16[640,256]{1,0:T(8,128)(2,1)S(1)}, bf16[640,256]{1,0:T(8,128)(2,1)S(1)}, u32[]{:S(2)}, u32[]{:S(2)}) collective-permute-start(bf16[640,256]{1,0:T(8,128)(2,1)S(1)} %bitcast.9), channel_id=1, source_target_pairs={{0,1},{1,0},{2,3},{3,2},{4,5},{5,4},{6,7},{7,6},{8,9},{9,8},{10,11... | collective-permute-start | bytes 983048 | tf_op jit(solution)/shard_map/ppermute | solution.py:333
  58.6 1.8 %copy-start.4 = (f32[1024]{0:T(1024)S(1)}, f32[1024]{0:T(1024)}, u32[]{:S(2)}) copy-start(f32[1024]{0:T(1024)} %param.15) | copy-start | bytes 12292
  58.6 1.7 %collective-permute-start.3 = (bf16[136,256]{1,0:T(8,128)(2,1)S(1)}, bf16[136,256]{1,0:T(8,128)(2,1)S(1)}, u32[]{:S(2)}, u32[]{:S(2)}) collective-permute-start(bf16[136,256]{1,0:T(8,128)(2,1)S(1)} %slots.1.refs_2_), channel_id=1, source_target_pairs={{0,1},{1,0},{2,3},{3,2},{4,5},{5,4},{6,7},{7,6},{8,9},{9,8},{10,11... | collective-permute-start | bytes 208904 | tf_op jit(solution)/shard_map/ppermute | solution.py:333
  59.2 1.2 %collective-permute-start = (f32[1,128]{1,0:T(1,128)S(1)}, f32[1,128]{1,0:T(1,128)S(1)}, u32[]{:S(2)}, u32[]{:S(2)}) collective-permute-start(f32[1,128]{1,0:T(1,128)S(1)} %get-tuple-element.26.refs_0_), channel_id=1, source_target_pairs={{0,1},{1,0},{2,3},{3,2},{4,5},{5,4},{6,7},{7,6},{8,9},{9,8},{10,11... | collective-permute-start | bytes 1544 | tf_op jit(solution)/shard_map/ppermute | solution.py:333

commit v4 on v3

--- a/solution.py
+++ b/solution.py
@@ -81,7 +81,7 @@
 
 
 def sigmoid(values):
-    return 1.0 / (1.0 + jnp.exp(-values))
+    return 0.5 + 0.5 * jnp.tanh(0.5 * values)
 
 
 def segments(lengths):
@@ -93,11 +93,35 @@
     return ends_row, ends_column
 
 
+def part_of_grads(part, height, left_ref, lifted_grad, cot, part_ref):
+    width = cot.shape[1]
+    blocks = lifted_grad.shape[1] // width
+    features = left_ref.shape[0] // 2
+    start = pl.multiple_of(part * height, 16)
+    w_grad = mm(left_ref[pl.ds(start, height)], lifted_grad).astype(bf16)
+    for block in range(blocks):
+        part_ref[block * height : (block + 1) * height] = w_grad[:, block * width : (block + 1) * width]
+    out_grad = mm(left_ref[pl.ds(pl.multiple_of(features + start, 16), height)], cot).astype(bf16)
+    part_ref[blocks * height : (blocks + 1) * height] = out_grad
+    filled = (blocks + 1) * height
+    if filled < part_ref.shape[0]:
+        part_ref[filled:] = jnp.zeros((part_ref.shape[0] - filled, width), bf16)
+
+
 def layer_kernel(
-    histories, small_ref, rows_ref, cot_ref, w_ref, wo_ref, lifted_ref, normal_ref, gate_ref, *rest
+    histories,
+    small_ref,
+    rows_ref,
+    cot_ref,
+    w_ref,
+    wo_ref,
+    lifted_ref,
+    normal_ref,
+    gate_ref,
+    left_ref,
+    *part_refs,
 ):
-    part_refs, stacked = rest[:-1], rest[-1]
-    replicas = len(part_refs)
+    replicas = len(part_refs) + 1
     tokens, width = rows_ref.shape
     head = width // HEADS
     row, col = iota((tokens, tokens), 0), iota((tokens, tokens), 1)
@@ -127,7 +151,9 @@
 
     norm_gain, gate_gain = small_ref[2:3, :width], small_ref[3:4, :width]
     normal, scale = center(embedded)
-    normed = (normal * norm_gain).astype(bf16)
+    scaled = normal * norm_gain
+    normed = scaled.astype(bf16)
+    left_ref[:width] = scaled.T.astype(bf16)
     lifted = mm(normed, w_ref[...])
     sig = sigmoid(lifted)
     projected = lifted * sig
@@ -143,11 +169,10 @@
     weights = (same * (scores * score_sig / MAXLEN)).astype(bf16)
     attended = mm(beside(weights), values_by)
     normal_two, scale_two = center(attended)
-    gated = (normal_two * gate_gain * gate_u).astype(bf16)
+    left_ref[width:] = (normal_two * gate_gain * gate_u).T.astype(bf16)
 
     cot = cot_ref[...]
     gated_grad = mm(cot, wo_ref[...], (1, 1)).astype(bf16).astype(f32)
-    out_grad = mm(gated, cot, (0, 0))
     normal_u = normal_two * gate_u
     gate_ref[...] = jnp.sum(gated_grad * normal_u, axis=0, keepdims=True)
     gated_gain = gated_grad * gate_gain
@@ -166,27 +191,28 @@
     lifted_ref[...] = lifted_grad
     normal_ref[:, :width] = normal
     normal_ref[:, width:] = jnp.broadcast_to(scale, (tokens, normal_ref.shape[1] - width))
-    w_grad = mm(normed, lifted_grad, (0, 0)).astype(bf16)
-
-    blocks = w_grad.shape[1] // width
-    for block in range(blocks):
-        stacked[block * width : (block + 1) * width] = w_grad[:, block * width : (block + 1) * width]
-    stacked[blocks * width :] = out_grad.astype(bf16)
     me = lax.axis_index("replica")
-    height = width // replicas
-    for step, part_ref in enumerate(part_refs):
-        start = lax.rem(me + step, replicas) * height
-        for block in range(blocks + 1):
-            part_ref[block * height : (block + 1) * height] = stacked[
-                pl.ds(pl.multiple_of(block * width + start, 16), height)
-            ]
-        filled = (blocks + 1) * height
-        if filled < part_ref.shape[0]:
-            part_ref[filled:] = jnp.zeros((part_ref.shape[0] - filled, width), bf16)
-
-
-def finish_kernel(small_ref, cot_ref, w_ref, lifted_ref, normal_ref, gate_ref, slot_grad_ref, gain_ref):
+    for step, part_ref in enumerate(part_refs, 1):
+        part = lax.rem(me + step, replicas)
+        part_of_grads(part, width // replicas, left_ref, lifted_grad, cot, part_ref)
+
+
+def finish_kernel(
+    replicas,
+    small_ref,
+    cot_ref,
+    w_ref,
+    lifted_ref,
+    normal_ref,
+    gate_ref,
+    left_ref,
+    slot_grad_ref,
+    gain_ref,
+    part_ref,
+):
     tokens, width = cot_ref.shape
+    me = lax.axis_index("replica")
+    part_of_grads(me, width // replicas, left_ref, lifted_ref[...], cot_ref[...], part_ref)
     normal = normal_ref[:, :width]
     scale = normal_ref[:, width : width + 1]
     normed_grad = mm(lifted_ref[...], w_ref[...], (1, 1)).astype(bf16).astype(f32)
@@ -245,7 +271,7 @@
     return jnp.concatenate([high, values - high], axis=0)
 
 
-def cross_kernel(capacity, in_ref, cross_ref, mine_ref):
+def cross_kernel(capacity, in_ref, cross_ref, theirs_ref, mine_ref):
     group, _, lanes = in_ref.shape
     slots = 2 * capacity
     mine_ref[...] = halves_across(in_ref[:, :slots].astype(f32)).reshape(mine_ref.shape).astype(bf16)
@@ -256,25 +282,24 @@
     gains = halves_across(total[-GAIN_ROWS:])
     gains = as_two(gains[:2] + gains[2:])
     padding = jnp.zeros((GAIN_ROWS - gains.shape[0], 2 * lanes), f32)
-    share = halves_across(total[:-GAIN_ROWS])
-    cross_ref[...] = jnp.concatenate([theirs, share, gains, padding], axis=0).astype(bf16)
+    cross_ref[...] = halves_across(total[:-GAIN_ROWS]).astype(bf16)
+    theirs_ref[...] = jnp.concatenate([theirs, gains, padding], axis=0).astype(bf16)
 
 
 def share_kernel(grad_scale, mine_ref, other_ref, share_ref):
-    group, rows, _ = share_ref.shape
-    first = mine_ref.shape[0] - GAIN_ROWS - rows
-    total = mine_ref[first : first + rows].astype(f32) + other_ref[first : first + rows].astype(f32)
+    group, _, _ = share_ref.shape
+    total = mine_ref[...].astype(f32) + other_ref[...].astype(f32)
     share = (total * grad_scale).astype(bf16)
     for peer in range(group):
         share_ref[peer] = share
 
 
-def slots_kernel(group, grad_scale, slots_ref, mine_ref, other_ref, owned_ref):
+def slots_kernel(group, grad_scale, slots_ref, theirs_ref, other_ref, owned_ref):
     rows = slots_ref.shape[0]
     half = lax.axis_index("shard") // group
     owned_ref[pl.ds(pl.multiple_of(half * rows, 16), rows)] = slots_ref[...]
     owned_ref[pl.ds(pl.multiple_of((1 - half) * rows, 16), rows)] = other_ref[:rows]
-    gains = mine_ref[-GAIN_ROWS:].astype(f32) + other_ref[-GAIN_ROWS:].astype(f32)
+    gains = theirs_ref[-GAIN_ROWS:].astype(f32) + other_ref[-GAIN_ROWS:].astype(f32)
     gains = as_two((gains[:2] + gains[2:4]) * grad_scale)
     padding = jnp.zeros((GAIN_ROWS - gains.shape[0], gains.shape[1]), f32)
     owned_ref[2 * rows :] = jnp.concatenate([gains, padding], axis=0).astype(bf16)
@@ -284,11 +309,17 @@
     wanted_refs, grad_refs = refs[:replicas], refs[replicas : 2 * replicas]
     state_ref, update_ref, state_out_ref, gains_ref = refs[2 * replicas :]
     rows = update_ref.shape[0]
+    chunks, _, lanes = state_ref.shape
     slots = wanted_refs[0].shape[1]
     first = pl.program_id(0) * rows
-    eye = iota((rows, rows), 0) == iota((rows, rows), 1)
-    state_row = state_ref[...].reshape(1, rows)
-    state = jnp.sum(jnp.where(eye, state_row, 0.0), axis=1, keepdims=True)
+    eye = iota((lanes, lanes), 0) == iota((lanes, lanes), 1)
+    state = jnp.concatenate(
+        [
+            jnp.sum(jnp.where(eye, state_ref[chunk], 0.0), axis=1, keepdims=True)
+            for chunk in range(chunks)
+        ],
+        axis=0,
+    )
     delta = jnp.zeros(update_ref.shape, f32)
     squares = jnp.zeros((rows, 1), f32)
     gains = jnp.zeros((grad_refs[0].shape[0] - slots, update_ref.shape[1]), f32)
@@ -300,9 +331,11 @@
         squares = squares + mean_square
         gains = gains + grad_ref[slots:].astype(f32)
     update_ref[...] = delta * (-LEARN_RATE / replicas)
-    squares_row = jnp.sum(jnp.where(eye, squares, 0.0), axis=0, keepdims=True)
+    for chunk in range(chunks):
+        column = squares[chunk * lanes : (chunk + 1) * lanes]
+        square_row = jnp.sum(jnp.where(eye, column, 0.0), axis=0, keepdims=True)
+        state_out_ref[chunk] = state_ref[chunk] + square_row / replicas
     gains_ref[...] = gains[:2] + gains[2:4]
-    state_out_ref[...] = (state_row + squares_row / replicas).reshape(state_out_ref.shape)
 
 
 def spread_kernel(step, replicas, part_ref, *refs):
@@ -402,31 +435,36 @@
     ).reshape(tokens, width)
 
     cot = cotangent.reshape(tokens, width)
-    lifted_grad, normal, gate_grad, *parts = pl.pallas_call(
+    lifted_grad, normal, gate_grad, left, *parts = pl.pallas_call(
         functools.partial(layer_kernel, seq_lengths.shape[-1]),
         out_shape=(
             shape((tokens, w_uvqk.shape[1]), bf16),
             shape((tokens, width + 128), f32),
             shape((1, width), f32),
+            shape((2 * width, tokens), bf16),
         )
-        + (shape((part_rows, width), bf16),) * replicas,
+        + (shape((part_rows, width), bf16),) * (replicas - 1),
         in_specs=[VMEM] * 5,
         out_specs=(VMEM,) * (replicas + 3),
-        scratch_shapes=[pltpu.VMEM((blocks * width, width), bf16)],
         cost_estimate=estimate(8 * tokens * width * w_uvqk.shape[1], 4 * blocks * width * width),
         compiler_params=room(20),
         name="layer",
     )(small, slot_rows, cot, w_uvqk, w_out)
-    came = hand_on(parts)
-    slot_grad, gain_rows = pl.pallas_call(
-        finish_kernel,
-        out_shape=(shape((tokens, width), bf16), shape((4, width), f32)),
-        in_specs=[VMEM] * 6,
-        out_specs=(VMEM, VMEM),
-        cost_estimate=estimate(2 * tokens * width * w_uvqk.shape[1], 2 * blocks * width * width),
+    came = hand_on([None] + parts)[1:]
+    slot_grad, gain_rows, kept = pl.pallas_call(
+        functools.partial(finish_kernel, replicas),
+        out_shape=(
+            shape((tokens, width), bf16),
+            shape((4, width), f32),
+            shape((part_rows, width), bf16),
+        ),
+        in_specs=[VMEM] * 7,
+        out_specs=(VMEM,) * 3,
+        cost_estimate=estimate(3 * tokens * width * w_uvqk.shape[1], 3 * blocks * width * width),
         compiler_params=room(10),
         name="finish",
-    )(small, cot, w_uvqk, lifted_grad, normal, gate_grad)
+    )(small, cot, w_uvqk, lifted_grad, normal, gate_grad, left)
+    came = [kept] + came
 
     aligned = capacity % 8 == 0 and share_rows % 8 == 0
     message_rows = 2 * (2 * capacity + share_rows) + GAIN_ROWS
@@ -455,13 +493,16 @@
     arrived = lax.all_to_all(
         message, "shard", split_axis=0, concat_axis=0, tiled=True, axis_index_groups=in_half
     )
-    cross_rows = half_slots + share_rows + GAIN_ROWS
     if aligned:
-        cross, mine = pl.pallas_call(
+        cross, theirs, mine = pl.pallas_call(
             functools.partial(cross_kernel, capacity),
-            out_shape=(shape((cross_rows, width), bf16), shape((half_slots, width), bf16)),
+            out_shape=(
+                shape((share_rows, width), bf16),
+                shape((half_slots + GAIN_ROWS, width), bf16),
+                shape((half_slots, width), bf16),
+            ),
             in_specs=[VMEM],
-            out_specs=(VMEM, VMEM),
+            out_specs=(VMEM,) * 3,
             compiler_params=room(8),
             name="cross",
         )(arrived)
@@ -471,9 +512,11 @@
         total = jnp.sum(arrived[:, 2 * capacity :].astype(f32), axis=0)
         gains = as_two(total[share_rows : share_rows + 2] + total[share_rows + 2 :]).astype(bf16)
         padding = jnp.zeros((GAIN_ROWS - 4, width), bf16)
-        cross = jnp.concatenate([theirs, total[:share_rows].astype(bf16), gains, padding], axis=0)
+        cross = total[:share_rows].astype(bf16)
+        theirs = jnp.concatenate([theirs, gains, padding], axis=0)
     mirror = [(source, (source + group) % shards) for source in range(shards)]
     other = lax.ppermute(cross, "shard", mirror)
+    other_slots = lax.ppermute(theirs, "shard", mirror)
     if aligned:
         share = pl.pallas_call(
             functools.partial(share_kernel, grad_scale),
@@ -491,14 +534,13 @@
             cost_estimate=estimate(tokens * width, 4 * tokens * width),
             compiler_params=room(4),
             name="slots",
-        )(mine, cross, other)
+        )(mine, theirs, other_slots)
     else:
-        total = (cross[half_slots:].astype(f32) + other[half_slots:].astype(f32)) * grad_scale
-        share = jnp.broadcast_to(
-            total[:share_rows].astype(bf16)[None], (group, share_rows, width)
-        )
-        gains = as_two(total[share_rows : share_rows + 2] + total[share_rows + 2 : share_rows + 4])
-        by_half = jnp.stack([mine, other[:half_slots]])
+        total = (cross.astype(f32) + other.astype(f32)) * grad_scale
+        share = jnp.broadcast_to(total.astype(bf16)[None], (group, share_rows, width))
+        gains = theirs[half_slots:].astype(f32) + other_slots[half_slots:].astype(f32)
+        gains = as_two((gains[:2] + gains[2:4]) * grad_scale)
+        by_half = jnp.stack([mine, other_slots[:half_slots]])
         by_half = jnp.where(half == 0, by_half, by_half[::-1]).reshape(tokens, width)
         owned = jnp.concatenate([by_half, gains.astype(bf16), padding], axis=0)
 
@@ -508,27 +550,28 @@
 
     wanted_all = from_all(wanted, replicas)
     owned_all = from_all(owned, replicas)
-    block = 128
+    lanes = 128
+    block = min(rows_dev, 2048 // replicas)
     row_update, state_new, grad_gains = pl.pallas_call(
         functools.partial(adagrad_kernel, replicas),
         grid=(rows_dev // block,),
         out_shape=(
             shape((rows_dev, width), f32),
-            shape((rows_dev // block, 1, block), f32),
+            shape((rows_dev // lanes, 1, lanes), f32),
             shape((2, width), f32),
         ),
         in_specs=[pl.BlockSpec((1, tokens), lambda step: (0, 0))] * replicas
         + [pl.BlockSpec((tokens + GAIN_ROWS, width), lambda step: (0, 0))] * replicas
-        + [pl.BlockSpec((1, 1, block), lambda step: (step, 0, 0))],
+        + [pl.BlockSpec((block // lanes, 1, lanes), lambda step: (step, 0, 0))],
         out_specs=(
             pl.BlockSpec((block, width), lambda step: (step, 0)),
-            pl.BlockSpec((1, 1, block), lambda step: (step, 0, 0)),
+            pl.BlockSpec((block // lanes, 1, lanes), lambda step: (step, 0, 0)),
             pl.BlockSpec((2, width), lambda step: (0, 0)),
         ),
         cost_estimate=estimate(2 * replicas * tokens * rows_dev * width, rows_dev * width * 4),
-        compiler_params=room(10),
+        compiler_params=room(12),
         name="adagrad",
-    )(*wanted_all, *owned_all, adagrad_state.reshape(rows_dev // block, 1, block))
+    )(*wanted_all, *owned_all, adagrad_state.reshape(rows_dev // lanes, 1, lanes))
 
     halves = hand_on([gathered.reshape(part_rows, width)] * replicas)
     grads = ()

time: 66.5 us -> 68.6 us (1.032)
  waiting for transfers between devices: 7.53 us -> 11.7 us
  Pallas kernels: 8.99 us -> 6.78 us
    ppermute x0 -> x1, waiting for transfers between devices: none -> 5.28 us  [on_device(): other_slots = lax.ppermute(theirs, 'shard', mirror)]
    pallas_call x1, Pallas kernels: 4.02 us -> 1.81 us  [on_device(): pl.pallas_call(functools.partial(adagrad_kernel, replicas), grid=(rows_de...]
    ppermute x1, waiting for transfers between devices: 5.39 us -> 4.6 us  [on_device(): other = lax.ppermute(cross, 'shard', mirror)]
  transfers between devices with their start and end apart: 5 -> 6, of which waited for: 3 -> 4; matrix products, arithmetic and copies ran while one was open for 0% -> 0% of each run, Pallas kernels for 8% -> 5%
where the time goes in v4:
time: 68.6 us; the launch traced here: 68.3 us
  blocking collectives  46.6 us (68%)
  waiting for transfers between devices  11.7 us (17%)
  Pallas kernels  6.78 us (10%)
  starting transfers between devices  1.74 us (3%)
  between operations  0.77 us (1%)
  local copies, waits for them, and re-layouts  0.71 us (1%)
    all_to_all x1, blocking collectives, on_device(): lax.all_to_all(asked, 'shard', split_axis=0, concat_axis=0, tiled=True)  15.6 us
    all_to_all x1, blocking collectives, on_device(): lax.all_to_all(message, 'shard', split_axis=0, concat_axis=0, tiled=True,...  11.3 us
    all_to_all x1, blocking collectives, on_device(): lax.all_to_all(found.reshape(shards, capacity, width), 'shard', split_axi...  10.1 us
    all_to_all x1, blocking collectives, on_device(): lax.all_to_all(share, 'shard', split_axis=0, concat_axis=0, tiled=True, a...  9.62 us
    ppermute x1, waiting for transfers between devices, on_device(): other_slots = lax.ppermute(theirs, 'shard', mirror)  5.28 us
    ppermute x1, waiting for transfers between devices, on_device(): other = lax.ppermute(cross, 'shard', mirror)  4.6 us
    pallas_call x1, Pallas kernels, on_device(): pl.pallas_call(functools.partial(layer_kernel, seq_lengths.shape[-1]), ou...  1.9 us
    pallas_call x1, Pallas kernels, on_device(): pl.pallas_call(functools.partial(adagrad_kernel, replicas), grid=(rows_de...  1.81 us
  transfers between devices with their start and end apart: 6, of which 4 were waited for; matrix products, arithmetic and copies ran while one was open for 0% of the time, Pallas kernels for 5%

profile of v4, /device:TPU:0, one launch (start us, length us, event | category | flops | bytes accessed | tf_op | source)
XLA Modules:
  0.0 68.3 jit_solution(17407035649235546319)
XLA Ops:
  0.6 0.0 copy-start.6
  0.6 0.0 copy-start.8
  0.7 0.6 copy-done.6
  1.3 0.0 copy-done.9
  1.3 0.0 copy-done.5
  1.4 0.0 copy-done.7
  1.4 15.6 %all_to_all.20.ids_ref = s32[16,1,128]{2,1,0:T(1,128)S(1)} all-to-all(s32[16,1,128]{2,1,0:T(1,128)S(1)} %get-tuple-element.27), channel_id=1, replica_groups=mesh['shard'=16,'replica'=2] {'shard'}, dimensions={0} | all-to-all | bytes 16384 | tf_op jit(solution)/shard_map/all_to_all | solution.py:423
  17.0 0.0 copy-done
  17.0 0.5 fetch.1
  17.4 0.0 copy-start.2
  17.4 10.1 %all_to_all.21 = bf16[16,8,256]{2,1,0:T(8,128)(2,1)S(1)} all-to-all(bf16[16,8,256]{2,1,0:T(8,128)(2,1)S(1)} %bitcast.12), channel_id=1, replica_groups=mesh['shard'=16,'replica'=2] {'shard'}, dimensions={0} | all-to-all | bytes 131072 | tf_op jit(solution)/shard_map/all_to_all | solution.py:433
  27.6 1.9 %layer.1 = (bf16[128,1024]{1,0:T(8,128)(2,1)S(1)}, f32[128,384]{1,0:T(8,128)S(1)}, f32[1,256]{1,0:T(1,128)S(1)}, bf16[512,128]{1,0:T(8,128)(2,1)S(1)}, bf16[640,256]{1,0:T(8,128)(2,1)S(1)}) custom-call(f32[8,256]{1,0:T(8,128)S(1)} %get-tuple-element.29.small_ref, bf16[128,256]{1,0:T(8,128)(2,1)S(1)} %bitcast.11, bf16[128,256]{1,0:T(8,128)(2,1)S(1)} %bitcast.13, ...), custom_call_target="tpu_custom_call" | custom-call | flops 268435456 | bytes 1310720 | tf_op jit(solution)/shard_map/layer/pallas_call | solution.py:438
  29.5 0.1 collective-permute-start.1
  29.6 0.6 finish.1
  30.2 1.0 %collective-permute-done.1.refs_1_ = bf16[640,256]{1,0:T(8,128)(2,1)S(1)} collective-permute-done((bf16[640,256]{1,0:T(8,128)(2,1)S(1)}, bf16[640,256]{1,0:T(8,128)(2,1)S(1)}, u32[]{:S(2)}, u32[]{:S(2)}) %collective-permute-start.1) | collective-permute-done | bytes 327712 | tf_op jit(solution)/shard_map/ppermute | solution.py:366
  31.2 0.1 pack.1
  31.3 11.3 %all_to_all.22.in_ref = bf16[8,200,128]{2,1,0:T(8,128)(2,1)S(1)} all-to-all(bf16[8,200,128]{2,1,0:T(8,128)(2,1)S(1)} %pack.1), channel_id=1, replica_groups={{0,2,4,6,8,10,12,14},{16,18,20,22,24,26,28,30},{1,3,5,7,9,11,13,15},{17..., dimensions={0} | all-to-all | bytes 819200 | tf_op jit(solution)/shard_map/all_to_all | solution.py:493
  42.6 0.1 cross.1
  42.6 0.8 %collective-permute-start.4 = (bf16[80,256]{1,0:T(8,128)(2,1)S(1)}, bf16[80,256]{1,0:T(8,128)(2,1)S(1)}, u32[]{:S(2)}, u32[]{:S(2)}) collective-permute-start(bf16[80,256]{1,0:T(8,128)(2,1)S(1)} %get-tuple-element.43.mine_ref), channel_id=1, source_target_pairs={{0,16},{2,18},{4,20},{6,22},{8,24},{10,26},{12,28},{14,30},{16,0},... | collective-permute-start | bytes 122888 | tf_op jit(solution)/shard_map/ppermute | solution.py:518
  43.4 4.6 %collective-permute-done.4.other_ref = bf16[80,256]{1,0:T(8,128)(2,1)S(1)} collective-permute-done((bf16[80,256]{1,0:T(8,128)(2,1)S(1)}, bf16[80,256]{1,0:T(8,128)(2,1)S(1)}, u32[]{:S(2)}, u32[]{:S(2)}) %collective-permute-start.4) | collective-permute-done | bytes 40992 | tf_op jit(solution)/shard_map/ppermute | solution.py:518
  48.1 9.6 %all_to_all.23 = bf16[8,80,256]{2,1,0:T(8,128)(2,1)S(1)} all-to-all(bf16[8,80,256]{2,1,0:T(8,128)(2,1)S(1)} %share.1), channel_id=1, replica_groups={{0,2,4,6,8,10,12,14},{16,18,20,22,24,26,28,30},{1,3,5,7,9,11,13,15},{17..., dimensions={0} | all-to-all | bytes 655360 | tf_op jit(solution)/shard_map/all_to_all | solution.py:547
  57.7 0.0 collective-permute-start.5
  57.7 0.3 collective-permute-start.2
  58.0 5.3 %collective-permute-done.2.other_ref = bf16[72,256]{1,0:T(8,128)(2,1)S(1)} collective-permute-done((bf16[72,256]{1,0:T(8,128)(2,1)S(1)}, bf16[72,256]{1,0:T(8,128)(2,1)S(1)}, u32[]{:S(2)}, u32[]{:S(2)}) %collective-permute-start.2) | collective-permute-done | bytes 36896 | tf_op jit(solution)/shard_map/ppermute | solution.py:519
  63.3 0.1 collective-permute-start.3
  63.4 0.5 collective-permute-start
  63.9 0.8 %collective-permute-done.refs_1_ = f32[1,128]{1,0:T(1,128)S(1)} collective-permute-done((f32[1,128]{1,0:T(1,128)S(1)}, f32[1,128]{1,0:T(1,128)S(1)}, u32[]{:S(2)}, u32[]{:S(2)}) %collective-permute-start) | collective-permute-done | bytes 544 | tf_op jit(solution)/shard_map/ppermute | solution.py:366
  64.7 0.0 collective-permute-done.3.refs_3_
  64.7 1.8 %adagrad.1 = (f32[1024,256]{1,0:T(8,128)}, f32[8,1,128]{2,1,0:T(1,128)}, f32[2,256]{1,0:T(2,128)}) custom-call(f32[1,128]{1,0:T(1,128)S(1)} %get-tuple-element.28.refs_0_, f32[1,128]{1,0:T(1,128)S(1)} %collective-permute-done.refs_1_, bf16[136,256]{1,0:T(8,128)(2,1)S(1)} %slots.1.refs_2_, bf16[136,256]{1,0:T(8,128)(2,1)S(1)} %collective-permute-done.3.refs_3_, ...), custom_call_target="tpu_custom_call" | custom-call | flops 134217728 | bytes 1048576 | tf_op jit(solution)/shard_map/adagrad/pallas_call | solution.py:555
  66.5 0.9 %shard_map.137 = (f32[256,1024]{1,0:T(8,128)}, f32[256,256]{1,0:T(8,128)}) custom-call(bf16[640,256]{1,0:T(8,128)(2,1)S(1)} %bitcast.10), custom_call_target="tpu_custom_call" | custom-call | flops 327680 | bytes 983040 | tf_op jit(solution)/shard_map/pallas_call | solution.py:579
  67.4 0.0 collective-permute-done.5.part_ref
  67.4 0.9 %shard_map.138 = (f32[256,1024]{1,0:T(8,128)}, f32[256,256]{1,0:T(8,128)}) custom-call(bf16[640,256]{1,0:T(8,128)(2,1)S(1)} %collective-permute-done.5.part_ref, f32[256,1024]{1,0:T(8,128)} %get-tuple-element.44.refs_0_, f32[256,256]{1,0:T(8,128)} %get-tuple-element.45.refs_1_), custom_call_target="tpu_custom_call", output_to_operand_aliasing={{0}: (1, {}), {1}: (2, {})} | custom-call | flops 327680 | bytes 983040 | tf_op jit(solution)/shard_map/pallas_call | solution.py:579
  (15 shorter events, 0.1 us)
Async XLA Ops:
  0.6 0.7 copy-start.6
  0.6 0.7 copy-start.8
  0.7 0.7 copy-start.9
  0.7 0.7 %copy-start.5 = (f32[256]{0:T(256)S(1)}, f32[256]{0:T(256)}, u32[]{:S(2)}) copy-start(f32[256]{0:T(256)} %param.18) | copy-start | bytes 3076
  0.7 0.7 %copy-start.7 = (s32[1,1,128]{2,1,0:T(1,128)S(1)}, s32[1,1,128]{2,1,0:T(1,128)}, u32[]{:S(2)}) copy-start(s32[1,1,128]{2,1,0:T(1,128)} %asked_ref.1) | copy-start | bytes 1540
  1.4 15.6 %copy-start = (f32[1024,256]{1,0:T(8,128)S(1)}, f32[1024,256]{1,0:T(8,128)}, u32[]{:S(2)}) copy-start(f32[1024,256]{1,0:T(8,128)} %table_ref.1) | copy-start | bytes 3145732
  17.0 10.6 %copy-start.1 = (bf16[256,1024]{1,0:T(8,128)(2,1)S(1)}, bf16[256,1024]{1,0:T(8,128)(2,1)}, u32[]{:S(2)}) copy-start(bf16[256,1024]{1,0:T(8,128)(2,1)} %w_ref.3) | copy-start | bytes 1572868
  17.0 10.6 %copy-start.3 = (bf16[256,256]{1,0:T(8,128)(2,1)S(1)}, bf16[256,256]{1,0:T(8,128)(2,1)}, u32[]{:S(2)}) copy-start(bf16[256,256]{1,0:T(8,128)(2,1)} %wo_ref.1) | copy-start | bytes 393220
  17.4 10.1 %copy-start.2 = (bf16[1,128,256]{2,1,0:T(8,128)(2,1)S(1)}, bf16[1,128,256]{2,1,0:T(8,128)(2,1)}, u32[]{:S(2)}) copy-start(bf16[1,128,256]{2,1,0:T(8,128)(2,1)} %param.13) | copy-start | bytes 196612
  29.5 1.7 %collective-permute-start.1 = (bf16[640,256]{1,0:T(8,128)(2,1)S(1)}, bf16[640,256]{1,0:T(8,128)(2,1)S(1)}, u32[]{:S(2)}, u32[]{:S(2)}) collective-permute-start(bf16[640,256]{1,0:T(8,128)(2,1)S(1)} %get-tuple-element.38), channel_id=1, source_target_pairs={{0,1},{1,0},{2,3},{3,2},{4,5},{5,4},{6,7},{7,6},{8,9},{9,8},{10,11... | collective-permute-start | bytes 983048 | tf_op jit(solution)/shard_map/ppermute | solution.py:366
  42.6 5.4 %collective-permute-start.4 = (bf16[80,256]{1,0:T(8,128)(2,1)S(1)}, bf16[80,256]{1,0:T(8,128)(2,1)S(1)}, u32[]{:S(2)}, u32[]{:S(2)}) collective-permute-start(bf16[80,256]{1,0:T(8,128)(2,1)S(1)} %get-tuple-element.43.mine_ref), channel_id=1, source_target_pairs={{0,16},{2,18},{4,20},{6,22},{8,24},{10,26},{12,28},{14,30},{16,0},... | collective-permute-start | bytes 122888 | tf_op jit(solution)/shard_map/ppermute | solution.py:518
  57.7 9.7 %collective-permute-start.5 = (bf16[640,256]{1,0:T(8,128)(2,1)S(1)}, bf16[640,256]{1,0:T(8,128)(2,1)S(1)}, u32[]{:S(2)}, u32[]{:S(2)}) collective-permute-start(bf16[640,256]{1,0:T(8,128)(2,1)S(1)} %bitcast.9), channel_id=1, source_target_pairs={{0,1},{1,0},{2,3},{3,2},{4,5},{5,4},{6,7},{7,6},{8,9},{9,8},{10,11... | collective-permute-start | bytes 983048 | tf_op jit(solution)/shard_map/ppermute | solution.py:366
  57.7 5.6 %collective-permute-start.2 = (bf16[72,256]{1,0:T(8,128)(2,1)S(1)}, bf16[72,256]{1,0:T(8,128)(2,1)S(1)}, u32[]{:S(2)}, u32[]{:S(2)}) collective-permute-start(bf16[72,256]{1,0:T(8,128)(2,1)S(1)} %get-tuple-element.40.theirs_ref), channel_id=1, source_target_pairs={{0,16},{2,18},{4,20},{6,22},{8,24},{10,26},{12,28},{14,30},{16,0},... | collective-permute-start | bytes 110600 | tf_op jit(solution)/shard_map/ppermute | solution.py:519
  63.3 1.4 %copy-start.4 = (f32[1024]{0:T(1024)S(1)}, f32[1024]{0:T(1024)}, u32[]{:S(2)}) copy-start(f32[1024]{0:T(1024)} %param.15) | copy-start | bytes 12292
  63.3 1.4 %collective-permute-start.3 = (bf16[136,256]{1,0:T(8,128)(2,1)S(1)}, bf16[136,256]{1,0:T(8,128)(2,1)S(1)}, u32[]{:S(2)}, u32[]{:S(2)}) collective-permute-start(bf16[136,256]{1,0:T(8,128)(2,1)S(1)} %slots.1.refs_2_), channel_id=1, source_target_pairs={{0,1},{1,0},{2,3},{3,2},{4,5},{5,4},{6,7},{7,6},{8,9},{9,8},{10,11... | collective-permute-start | bytes 208904 | tf_op jit(solution)/shard_map/ppermute | solution.py:366
  63.4 1.3 %collective-permute-start = (f32[1,128]{1,0:T(1,128)S(1)}, f32[1,128]{1,0:T(1,128)S(1)}, u32[]{:S(2)}, u32[]{:S(2)}) collective-permute-start(f32[1,128]{1,0:T(1,128)S(1)} %get-tuple-element.28.refs_0_), channel_id=1, source_target_pairs={{0,1},{1,0},{2,3},{3,2},{4,5},{5,4},{6,7},{7,6},{8,9},{9,8},{10,11... | collective-permute-start | bytes 1544 | tf_op jit(solution)/shard_map/ppermute | solution.py:366

commit v5 on v4

--- a/solution.py
+++ b/solution.py
@@ -50,7 +50,33 @@
     small_ref[3:4, : gate_ref.shape[1]] = gate_ref[...]
 
 
-def fetch_kernel(capacity, ids_ref, table_ref, found_ref, wanted_ref):
+def segments(lengths):
+    count = lengths.shape[1]
+    row, col = iota((count, count), 0), iota((count, count), 1)
+    column = jnp.sum(jnp.where(row == col, lengths, 0.0), axis=1, keepdims=True)
+    ends_column = jnp.sum(jnp.where(col <= row, lengths, 0.0), axis=1, keepdims=True)
+    ends_row = jnp.sum(jnp.where(row <= col, column, 0.0), axis=0, keepdims=True)
+    return ends_row, ends_column
+
+
+def token_kernel(histories, small_ref, token_ref, same_ref):
+    tokens = token_ref.shape[0]
+    row, col = iota((tokens, tokens), 0), iota((tokens, tokens), 1)
+    slot_row = small_ref[0:1, :tokens]
+    slot_column = jnp.sum(jnp.where(row == col, slot_row, 0.0), axis=1, keepdims=True)
+    token_ref[...] = (slot_column.astype(jnp.int32) == col).astype(f32).astype(bf16)
+    ends_row, ends_column = segments(small_ref[1:2, :histories])
+    before_row = iota((histories, tokens), 1).astype(f32) >= ends_column
+    segment_row = jnp.sum(before_row.astype(f32), axis=0, keepdims=True)
+    before_column = iota((tokens, histories), 0).astype(f32) >= ends_row
+    segment_column = jnp.sum(before_column.astype(f32), axis=1, keepdims=True)
+    same_ref[...] = ((segment_row == segment_column) & (row >= col)).astype(f32)
+
+
+def fetch_kernel(
+    capacity, histories, ids_ref, table_ref, small_ref, found_ref, wanted_ref, token_ref, same_ref
+):
+    token_kernel(histories, small_ref, token_ref, same_ref)
     me = lax.axis_index("shard")
     ids = ids_ref[...].reshape(ids_ref.shape[0], ids_ref.shape[2])
     shards, slots = ids.shape
@@ -84,15 +110,6 @@
     return 0.5 + 0.5 * jnp.tanh(0.5 * values)
 
 
-def segments(lengths):
-    count = lengths.shape[1]
-    row, col = iota((count, count), 0), iota((count, count), 1)
-    column = jnp.sum(jnp.where(row == col, lengths, 0.0), axis=1, keepdims=True)
-    ends_column = jnp.sum(jnp.where(col <= row, lengths, 0.0), axis=1, keepdims=True)
-    ends_row = jnp.sum(jnp.where(row <= col, column, 0.0), axis=0, keepdims=True)
-    return ends_row, ends_column
-
-
 def part_of_grads(part, height, left_ref, lifted_grad, cot, part_ref):
     width = cot.shape[1]
     blocks = lifted_grad.shape[1] // width
@@ -108,9 +125,17 @@
         part_ref[filled:] = jnp.zeros((part_ref.shape[0] - filled, width), bf16)
 
 
+def part_held(twist, group, replicas, back=0):
+    half = lax.axis_index("shard") // group
+    return lax.rem(lax.axis_index("replica") + half * twist + (replicas - back), replicas)
+
+
 def layer_kernel(
-    histories,
+    twist,
+    group,
     small_ref,
+    token_ref,
+    same_ref,
     rows_ref,
     cot_ref,
     w_ref,
@@ -124,19 +149,8 @@
     replicas = len(part_refs) + 1
     tokens, width = rows_ref.shape
     head = width // HEADS
-    row, col = iota((tokens, tokens), 0), iota((tokens, tokens), 1)
-
-    slot_row = small_ref[0:1, :tokens]
-    slot_column = jnp.sum(jnp.where(row == col, slot_row, 0.0), axis=1, keepdims=True)
-    embedded = mm((slot_column.astype(jnp.int32) == col).astype(f32), rows_ref[...])
-
-    ends_row, ends_column = segments(small_ref[1:2, :histories])
-    before_row = iota((histories, tokens), 1).astype(f32) >= ends_column
-    segment_row = jnp.sum(before_row.astype(f32), axis=0, keepdims=True)
-    before_column = iota((tokens, histories), 0).astype(f32) >= ends_row
-    segment_column = jnp.sum(before_column.astype(f32), axis=1, keepdims=True)
-    same = (segment_row == segment_column) & (row >= col)
-    same = jnp.concatenate([same.astype(f32)] * HEADS, axis=0)
+    embedded = mm(token_ref[...], rows_ref[...])
+    same = jnp.concatenate([same_ref[...]] * HEADS, axis=0)
 
     lane = iota((1, width), 1)
     heads = [((lane >= h * head) & (lane < (h + 1) * head)).astype(f32) for h in range(HEADS)]
@@ -191,13 +205,14 @@
     lifted_ref[...] = lifted_grad
     normal_ref[:, :width] = normal
     normal_ref[:, width:] = jnp.broadcast_to(scale, (tokens, normal_ref.shape[1] - width))
-    me = lax.axis_index("replica")
     for step, part_ref in enumerate(part_refs, 1):
-        part = lax.rem(me + step, replicas)
+        part = part_held(twist, group, replicas, replicas - step)
         part_of_grads(part, width // replicas, left_ref, lifted_grad, cot, part_ref)
 
 
 def finish_kernel(
+    twist,
+    group,
     replicas,
     small_ref,
     cot_ref,
@@ -211,8 +226,8 @@
     part_ref,
 ):
     tokens, width = cot_ref.shape
-    me = lax.axis_index("replica")
-    part_of_grads(me, width // replicas, left_ref, lifted_ref[...], cot_ref[...], part_ref)
+    part = part_held(twist, group, replicas)
+    part_of_grads(part, width // replicas, left_ref, lifted_ref[...], cot_ref[...], part_ref)
     normal = normal_ref[:, :width]
     scale = normal_ref[:, width : width + 1]
     normed_grad = mm(lifted_ref[...], w_ref[...], (1, 1)).astype(bf16).astype(f32)
@@ -305,7 +320,7 @@
     owned_ref[2 * rows :] = jnp.concatenate([gains, padding], axis=0).astype(bf16)
 
 
-def adagrad_kernel(replicas, *refs):
+def adagrad_kernel(twist, group, replicas, *refs):
     wanted_refs, grad_refs = refs[:replicas], refs[replicas : 2 * replicas]
     state_ref, update_ref, state_out_ref, gains_ref = refs[2 * replicas :]
     rows = update_ref.shape[0]
@@ -323,9 +338,18 @@
     delta = jnp.zeros(update_ref.shape, f32)
     squares = jnp.zeros((rows, 1), f32)
     gains = jnp.zeros((grad_refs[0].shape[0] - slots, update_ref.shape[1]), f32)
-    for wanted_ref, grad_ref in zip(wanted_refs, grad_refs):
-        hit = iota((rows, slots), 0) + first == wanted_ref[...].astype(jnp.int32)
-        row_grad = mm(hit.astype(f32), grad_ref[:slots])
+    wanted = [wanted_ref[...] for wanted_ref in wanted_refs]
+    grads = [grad_ref[:slots].astype(f32) for grad_ref in grad_refs]
+    if twist:
+        start = lax.axis_index("shard") // group * (slots // 2)
+        lane, row = iota((1, slots), 1), iota((slots, 1), 0)
+        here = (lane >= start) & (lane < start + slots // 2)
+        wanted = [jnp.where(here, *wanted), jnp.where(here, *wanted[::-1])]
+        here = (row >= start) & (row < start + slots // 2)
+        grads = [jnp.where(here, *grads), jnp.where(here, *grads[::-1])]
+    for asked, grad, grad_ref in zip(wanted, grads, grad_refs):
+        hit = iota((rows, slots), 0) + first == asked.astype(jnp.int32)
+        row_grad = mm(hit.astype(f32), grad)
         mean_square = jnp.mean(row_grad * row_grad, axis=1, keepdims=True)
         delta = delta + row_grad * lax.rsqrt(state + mean_square + EPSILON)
         squares = squares + mean_square
@@ -338,11 +362,11 @@
     gains_ref[...] = gains[:2] + gains[2:4]
 
 
-def spread_kernel(step, replicas, part_ref, *refs):
+def spread_kernel(twist, group, step, replicas, part_ref, *refs):
     uvqk_ref, out_ref, uvqk_rows, out_rows, sems = refs[-5:]
     height, columns = uvqk_rows.shape
     width = out_rows.shape[1]
-    part = lax.rem(lax.axis_index("replica") + (replicas - step), replicas)
+    part = part_held(twist, group, replicas, step)
     rows = pl.ds(pl.multiple_of(part * height, 8), height)
     blocks = columns // width
     for block in range(blocks):
@@ -398,6 +422,13 @@
     share_rows = -(-blocks * width // (replicas * group))
     part_rows = share_rows * group
     in_half = [list(range(group)), list(range(group, shards))]
+    twist = 1 if replicas == 2 else 0
+    both = ("shard", "replica")
+    place = lambda replica, shard: shard * replicas + replica % replicas
+    lookup_groups = [
+        [place(replica + shard // group * twist, shard) for shard in range(shards)]
+        for replica in range(replicas)
+    ]
     half_slots = group * capacity
     grad_scale = 1.0 / math.sqrt(tokens * shards * replicas)
     shape = jax.ShapeDtypeStruct
@@ -420,23 +451,35 @@
         norm_gain.reshape(1, width),
         out_gain.reshape(1, width),
     )
-    ids = lax.all_to_all(asked, "shard", split_axis=0, concat_axis=0, tiled=True)
-    found, wanted = pl.pallas_call(
-        functools.partial(fetch_kernel, capacity),
-        out_shape=(shape((tokens, width), bf16), shape((1, tokens), f32)),
-        in_specs=[VMEM] * 2,
-        out_specs=(VMEM, VMEM),
+    ids = lax.all_to_all(
+        asked, both, split_axis=0, concat_axis=0, tiled=True, axis_index_groups=lookup_groups
+    )
+    found, wanted, token_hot, same = pl.pallas_call(
+        functools.partial(fetch_kernel, capacity, seq_lengths.shape[-1]),
+        out_shape=(
+            shape((tokens, width), bf16),
+            shape((1, tokens), f32),
+            shape((tokens, tokens), bf16),
+            shape((tokens, tokens), f32),
+        ),
+        in_specs=[VMEM] * 3,
+        out_specs=(VMEM,) * 4,
         cost_estimate=estimate(2 * tokens * rows_dev * width, rows_dev * width * 4),
         compiler_params=room(8),
         name="fetch",
-    )(ids, table_slab)
+    )(ids, table_slab, small)
     slot_rows = lax.all_to_all(
-        found.reshape(shards, capacity, width), "shard", split_axis=0, concat_axis=0, tiled=True
+        found.reshape(shards, capacity, width),
+        both,
+        split_axis=0,
+        concat_axis=0,
+        tiled=True,
+        axis_index_groups=lookup_groups,
     ).reshape(tokens, width)
 
     cot = cotangent.reshape(tokens, width)
     lifted_grad, normal, gate_grad, left, *parts = pl.pallas_call(
-        functools.partial(layer_kernel, seq_lengths.shape[-1]),
+        functools.partial(layer_kernel, 0, group),
         out_shape=(
             shape((tokens, w_uvqk.shape[1]), bf16),
             shape((tokens, width + 128), f32),
@@ -444,15 +487,15 @@
             shape((2 * width, tokens), bf16),
         )
         + (shape((part_rows, width), bf16),) * (replicas - 1),
-        in_specs=[VMEM] * 5,
+        in_specs=[VMEM] * 7,
         out_specs=(VMEM,) * (replicas + 3),
         cost_estimate=estimate(8 * tokens * width * w_uvqk.shape[1], 4 * blocks * width * width),
         compiler_params=room(20),
         name="layer",
-    )(small, slot_rows, cot, w_uvqk, w_out)
+    )(small, token_hot, same, slot_rows, cot, w_uvqk, w_out)
     came = hand_on([None] + parts)[1:]
     slot_grad, gain_rows, kept = pl.pallas_call(
-        functools.partial(finish_kernel, replicas),
+        functools.partial(finish_kernel, 0, group, replicas),
         out_shape=(
             shape((tokens, width), bf16),
             shape((4, width), f32),
@@ -514,9 +557,14 @@
         padding = jnp.zeros((GAIN_ROWS - 4, width), bf16)
         cross = total[:share_rows].astype(bf16)
         theirs = jnp.concatenate([theirs, gains, padding], axis=0)
-    mirror = [(source, (source + group) % shards) for source in range(shards)]
+    mirror = [(shard, (shard + group) % shards) for shard in range(shards)]
+    turned_mirror = [
+        (place(replica, shard), place(replica + twist, (shard + group) % shards))
+        for replica in range(replicas)
+        for shard in range(shards)
+    ]
     other = lax.ppermute(cross, "shard", mirror)
-    other_slots = lax.ppermute(theirs, "shard", mirror)
+    other_slots = lax.ppermute(theirs, both, turned_mirror)
     if aligned:
         share = pl.pallas_call(
             functools.partial(share_kernel, grad_scale),
@@ -553,7 +601,7 @@
     lanes = 128
     block = min(rows_dev, 2048 // replicas)
     row_update, state_new, grad_gains = pl.pallas_call(
-        functools.partial(adagrad_kernel, replicas),
+        functools.partial(adagrad_kernel, twist, group, replicas),
         grid=(rows_dev // block,),
         out_shape=(
             shape((rows_dev, width), f32),
@@ -577,7 +625,7 @@
     grads = ()
     for step, half in enumerate(halves):
         grads = pl.pallas_call(
-            functools.partial(spread_kernel, step, replicas),
+            functools.partial(spread_kernel, 0, group, step, replicas),
             out_shape=(shape(w_uvqk.shape, f32), shape(w_out.shape, f32)),
             in_specs=[VMEM] + [pl.BlockSpec(memory_space=pl.ANY)] * len(grads),
             out_specs=(pl.BlockSpec(memory_space=pl.ANY),) * 2,

time: 68.6 us -> 67 us (0.977)
  waiting for transfers between devices: 11.7 us -> 10.2 us
  starting transfers between devices: 1.74 us -> 3.15 us
  blocking collectives: 46.6 us -> 45.2 us
    all_to_all x2, blocking collectives: 25.7 us -> 24 us  [the longest x1 14.4 us: on_device(): lax.all_to_all(asked, both, split_axis=0, concat_axis=0, tiled=True, axis...]
    ppermute x1, waiting for transfers between devices: 5.28 us -> 4.45 us  [on_device(): other_slots = lax.ppermute(theirs, both, turned_mirror)]
where the time goes in v5:
time: 67 us; the launch traced here: 66.7 us
  blocking collectives  45.2 us (67%)
  waiting for transfers between devices  10.2 us (15%)
  Pallas kernels  6.76 us (10%)
  starting transfers between devices  3.15 us (5%)
  between operations  0.75 us (1%)
  local copies, waits for them, and re-layouts  0.71 us (1%)
    all_to_all x1, blocking collectives, on_device(): lax.all_to_all(asked, both, split_axis=0, concat_axis=0, tiled=True, axis...  14.4 us
    all_to_all x1, blocking collectives, on_device(): lax.all_to_all(message, 'shard', split_axis=0, concat_axis=0, tiled=True,...  11.6 us
    all_to_all x1, blocking collectives, on_device(): lax.all_to_all(share, 'shard', split_axis=0, concat_axis=0, tiled=True, a...  9.62 us
    all_to_all x1, blocking collectives, on_device(): lax.all_to_all(found.reshape(shards, capacity, width), both, split_axis=0...  9.56 us
    ppermute x1, waiting for transfers between devices, on_device(): other_slots = lax.ppermute(theirs, both, turned_mirror)  4.45 us
    ppermute x1, waiting for transfers between devices, on_device(): other = lax.ppermute(cross, 'shard', mirror)  4.29 us
    pallas_call x1, Pallas kernels, on_device(): pl.pallas_call(functools.partial(adagrad_kernel, twist, group, replicas),...  1.85 us
    pallas_call x1, Pallas kernels, on_device(): pl.pallas_call(functools.partial(layer_kernel, 0, group), out_shape=(shap...  1.83 us
  transfers between devices with their start and end apart: 6, of which 4 were waited for; matrix products, arithmetic and copies ran while one was open for 0% of the time, Pallas kernels for 5%

profile of v5, /device:TPU:0, one launch (start us, length us, event | category | flops | bytes accessed | tf_op | source)
XLA Modules:
  0.0 66.7 jit_solution(3193072429254917169)
XLA Ops:
  0.7 0.6 copy-done.6
  1.3 0.0 copy-done.9
  1.3 0.0 copy-done.5
  1.4 0.0 copy-done.7
  1.4 14.4 %all_to_all.20.ids_ref = s32[16,1,128]{2,1,0:T(1,128)S(1)} all-to-all(s32[16,1,128]{2,1,0:T(1,128)S(1)} %get-tuple-element.29), channel_id=1, replica_groups={{0,2,4,6,8,10,12,14,17,19,21,23,25,27,29,31},{1,3,5,7,9,11,13,15,16,18,..., dimensions={0} | all-to-all | bytes 16384 | tf_op jit(solution)/shard_map/all_to_all | solution.py:454
  15.8 0.0 copy-done
  15.8 0.5 fetch.1
  16.3 0.0 copy-start.2
  16.3 9.6 %all_to_all.21 = bf16[16,8,256]{2,1,0:T(8,128)(2,1)S(1)} all-to-all(bf16[16,8,256]{2,1,0:T(8,128)(2,1)S(1)} %bitcast.12), channel_id=1, replica_groups={{0,2,4,6,8,10,12,14,17,19,21,23,25,27,29,31},{1,3,5,7,9,11,13,15,16,18,..., dimensions={0} | all-to-all | bytes 131072 | tf_op jit(solution)/shard_map/all_to_all | solution.py:471
  25.9 0.0 copy-done.3
  25.9 1.8 %layer.1 = (bf16[128,1024]{1,0:T(8,128)(2,1)S(1)}, f32[128,384]{1,0:T(8,128)S(1)}, f32[1,256]{1,0:T(1,128)S(1)}, bf16[512,128]{1,0:T(8,128)(2,1)S(1)}, bf16[640,256]{1,0:T(8,128)(2,1)S(1)}) custom-call(f32[8,256]{1,0:T(8,128)S(1)} %get-tuple-element.30.small_ref, bf16[128,128]{1,0:T(8,128)(2,1)S(1)} %get-tuple-element.32.token_ref, ...), custom_call_target="tpu_custom_call" | custom-call | flops 268435456 | bytes 1310720 | tf_op jit(solution)/shard_map/layer/pallas_call | solution.py:481
  27.7 0.7 %collective-permute-start.1 = (bf16[640,256]{1,0:T(8,128)(2,1)S(1)}, bf16[640,256]{1,0:T(8,128)(2,1)S(1)}, u32[]{:S(2)}, u32[]{:S(2)}) collective-permute-start(bf16[640,256]{1,0:T(8,128)(2,1)S(1)} %get-tuple-element.42), channel_id=1, source_target_pairs={{0,1},{1,0},{2,3},{3,2},{4,5},{5,4},{6,7},{7,6},{8,9},{9,8},{10,11... | collective-permute-start | bytes 983048 | tf_op jit(solution)/shard_map/ppermute | solution.py:390
  28.5 0.6 finish.1
  29.1 0.6 collective-permute-done.1.refs_1_
  29.7 0.1 pack.1
  29.8 11.6 %all_to_all.22.in_ref = bf16[8,200,128]{2,1,0:T(8,128)(2,1)S(1)} all-to-all(bf16[8,200,128]{2,1,0:T(8,128)(2,1)S(1)} %pack.1), channel_id=1, replica_groups={{0,2,4,6,8,10,12,14},{16,18,20,22,24,26,28,30},{1,3,5,7,9,11,13,15},{17..., dimensions={0} | all-to-all | bytes 819200 | tf_op jit(solution)/shard_map/all_to_all | solution.py:536
  41.4 0.1 cross.1
  41.4 1.1 %collective-permute-start.4 = (bf16[80,256]{1,0:T(8,128)(2,1)S(1)}, bf16[80,256]{1,0:T(8,128)(2,1)S(1)}, u32[]{:S(2)}, u32[]{:S(2)}) collective-permute-start(bf16[80,256]{1,0:T(8,128)(2,1)S(1)} %get-tuple-element.47.mine_ref), channel_id=1, source_target_pairs={{0,16},{2,18},{4,20},{6,22},{8,24},{10,26},{12,28},{14,30},{16,0},... | collective-permute-start | bytes 122888 | tf_op jit(solution)/shard_map/ppermute | solution.py:566
  42.5 4.3 %collective-permute-done.4.other_ref = bf16[80,256]{1,0:T(8,128)(2,1)S(1)} collective-permute-done((bf16[80,256]{1,0:T(8,128)(2,1)S(1)}, bf16[80,256]{1,0:T(8,128)(2,1)S(1)}, u32[]{:S(2)}, u32[]{:S(2)}) %collective-permute-start.4) | collective-permute-done | bytes 40992 | tf_op jit(solution)/shard_map/ppermute | solution.py:566
  46.9 9.6 %all_to_all.23 = bf16[8,80,256]{2,1,0:T(8,128)(2,1)S(1)} all-to-all(bf16[8,80,256]{2,1,0:T(8,128)(2,1)S(1)} %share.1), channel_id=1, replica_groups={{0,2,4,6,8,10,12,14},{16,18,20,22,24,26,28,30},{1,3,5,7,9,11,13,15},{17..., dimensions={0} | all-to-all | bytes 655360 | tf_op jit(solution)/shard_map/all_to_all | solution.py:595
  56.5 0.0 collective-permute-start.5
  56.5 0.7 %collective-permute-start.2 = (bf16[72,256]{1,0:T(8,128)(2,1)S(1)}, bf16[72,256]{1,0:T(8,128)(2,1)S(1)}, u32[]{:S(2)}, u32[]{:S(2)}) collective-permute-start(bf16[72,256]{1,0:T(8,128)(2,1)S(1)} %get-tuple-element.44.theirs_ref), channel_id=1, source_target_pairs={{0,17},{2,19},{4,21},{6,23},{8,25},{10,27},{12,29},{14,31},{16,1},... | collective-permute-start | bytes 110600 | tf_op jit(solution)/shard_map/ppermute | solution.py:567
  57.2 4.5 %collective-permute-done.2.other_ref = bf16[72,256]{1,0:T(8,128)(2,1)S(1)} collective-permute-done((bf16[72,256]{1,0:T(8,128)(2,1)S(1)}, bf16[72,256]{1,0:T(8,128)(2,1)S(1)}, u32[]{:S(2)}, u32[]{:S(2)}) %collective-permute-start.2) | collective-permute-done | bytes 36896 | tf_op jit(solution)/shard_map/ppermute | solution.py:567
  61.7 0.2 collective-permute-start.3
  61.9 0.4 collective-permute-start
  62.3 0.8 %collective-permute-done.refs_1_ = f32[1,128]{1,0:T(1,128)S(1)} collective-permute-done((f32[1,128]{1,0:T(1,128)S(1)}, f32[1,128]{1,0:T(1,128)S(1)}, u32[]{:S(2)}, u32[]{:S(2)}) %collective-permute-start) | collective-permute-done | bytes 544 | tf_op jit(solution)/shard_map/ppermute | solution.py:390
  63.1 0.0 collective-permute-done.3.refs_3_
  63.1 0.0 copy-done.4
  63.1 1.8 %adagrad.1 = (f32[1024,256]{1,0:T(8,128)}, f32[8,1,128]{2,1,0:T(1,128)}, f32[2,256]{1,0:T(2,128)}) custom-call(f32[1,128]{1,0:T(1,128)S(1)} %get-tuple-element.31.refs_0_, f32[1,128]{1,0:T(1,128)S(1)} %collective-permute-done.refs_1_, bf16[136,256]{1,0:T(8,128)(2,1)S(1)} %slots.1.refs_2_, bf16[136,256]{1,0:T(8,128)(2,1)S(1)} %collective-permute-done.3.refs_3_, ...), custom_call_target="tpu_custom_call" | custom-call | flops 134217728 | bytes 1048576 | tf_op jit(solution)/shard_map/adagrad/pallas_call | solution.py:603
  64.9 0.9 %shard_map.137 = (f32[256,1024]{1,0:T(8,128)}, f32[256,256]{1,0:T(8,128)}) custom-call(bf16[640,256]{1,0:T(8,128)(2,1)S(1)} %bitcast.10), custom_call_target="tpu_custom_call" | custom-call | flops 327680 | bytes 983040 | tf_op jit(solution)/shard_map/pallas_call | solution.py:627
  65.8 0.0 collective-permute-done.5.part_ref
  65.8 0.9 %shard_map.138 = (f32[256,1024]{1,0:T(8,128)}, f32[256,256]{1,0:T(8,128)}) custom-call(bf16[640,256]{1,0:T(8,128)(2,1)S(1)} %collective-permute-done.5.part_ref, f32[256,1024]{1,0:T(8,128)} %get-tuple-element.48.refs_0_, f32[256,256]{1,0:T(8,128)} %get-tuple-element.49.refs_1_), custom_call_target="tpu_custom_call", output_to_operand_aliasing={{0}: (1, {}), {1}: (2, {})} | custom-call | flops 327680 | bytes 983040 | tf_op jit(solution)/shard_map/pallas_call | solution.py:627
  (15 shorter events, 0.1 us)
Async XLA Ops:
  0.6 0.7 %copy-start.6 = (f32[256]{0:T(256)S(1)}, f32[256]{0:T(256)}, u32[]{:S(2)}) copy-start(f32[256]{0:T(256)} %param.19) | copy-start | bytes 3076
  0.6 0.7 %copy-start.8 = (s32[1,128]{1,0:T(1,128)S(1)}, s32[1,128]{1,0:T(1,128)}, u32[]{:S(2)}) copy-start(s32[1,128]{1,0:T(1,128)} %slot_ref.1) | copy-start | bytes 1540
  0.7 0.7 %copy-start.9 = (s32[1,1,8]{2,1,0:T(1,128)S(1)}, s32[1,1,8]{2,1,0:T(1,128)}, u32[]{:S(2)}) copy-start(s32[1,1,8]{2,1,0:T(1,128)} %param.12) | copy-start | bytes 100
  0.7 0.7 %copy-start.5 = (f32[256]{0:T(256)S(1)}, f32[256]{0:T(256)}, u32[]{:S(2)}) copy-start(f32[256]{0:T(256)} %param.18) | copy-start | bytes 3076
  0.7 0.7 %copy-start.7 = (s32[1,1,128]{2,1,0:T(1,128)S(1)}, s32[1,1,128]{2,1,0:T(1,128)}, u32[]{:S(2)}) copy-start(s32[1,1,128]{2,1,0:T(1,128)} %asked_ref.1) | copy-start | bytes 1540
  1.4 14.5 %copy-start = (f32[1024,256]{1,0:T(8,128)S(1)}, f32[1024,256]{1,0:T(8,128)}, u32[]{:S(2)}) copy-start(f32[1024,256]{1,0:T(8,128)} %table_ref.1) | copy-start | bytes 3145732
  15.8 10.1 %copy-start.1 = (bf16[256,1024]{1,0:T(8,128)(2,1)S(1)}, bf16[256,1024]{1,0:T(8,128)(2,1)}, u32[]{:S(2)}) copy-start(bf16[256,1024]{1,0:T(8,128)(2,1)} %w_ref.3) | copy-start | bytes 1572868
  15.8 10.1 %copy-start.3 = (bf16[256,256]{1,0:T(8,128)(2,1)S(1)}, bf16[256,256]{1,0:T(8,128)(2,1)}, u32[]{:S(2)}) copy-start(bf16[256,256]{1,0:T(8,128)(2,1)} %wo_ref.1) | copy-start | bytes 393220
  16.3 9.6 %copy-start.2 = (bf16[1,128,256]{2,1,0:T(8,128)(2,1)S(1)}, bf16[1,128,256]{2,1,0:T(8,128)(2,1)}, u32[]{:S(2)}) copy-start(bf16[1,128,256]{2,1,0:T(8,128)(2,1)} %param.13) | copy-start | bytes 196612
  27.7 2.0 %collective-permute-start.1 = (bf16[640,256]{1,0:T(8,128)(2,1)S(1)}, bf16[640,256]{1,0:T(8,128)(2,1)S(1)}, u32[]{:S(2)}, u32[]{:S(2)}) collective-permute-start(bf16[640,256]{1,0:T(8,128)(2,1)S(1)} %get-tuple-element.42), channel_id=1, source_target_pairs={{0,1},{1,0},{2,3},{3,2},{4,5},{5,4},{6,7},{7,6},{8,9},{9,8},{10,11... | collective-permute-start | bytes 983048 | tf_op jit(solution)/shard_map/ppermute | solution.py:390
  41.4 5.4 %collective-permute-start.4 = (bf16[80,256]{1,0:T(8,128)(2,1)S(1)}, bf16[80,256]{1,0:T(8,128)(2,1)S(1)}, u32[]{:S(2)}, u32[]{:S(2)}) collective-permute-start(bf16[80,256]{1,0:T(8,128)(2,1)S(1)} %get-tuple-element.47.mine_ref), channel_id=1, source_target_pairs={{0,16},{2,18},{4,20},{6,22},{8,24},{10,26},{12,28},{14,30},{16,0},... | collective-permute-start | bytes 122888 | tf_op jit(solution)/shard_map/ppermute | solution.py:566
  56.5 9.3 %collective-permute-start.5 = (bf16[640,256]{1,0:T(8,128)(2,1)S(1)}, bf16[640,256]{1,0:T(8,128)(2,1)S(1)}, u32[]{:S(2)}, u32[]{:S(2)}) collective-permute-start(bf16[640,256]{1,0:T(8,128)(2,1)S(1)} %bitcast.9), channel_id=1, source_target_pairs={{0,1},{1,0},{2,3},{3,2},{4,5},{5,4},{6,7},{7,6},{8,9},{9,8},{10,11... | collective-permute-start | bytes 983048 | tf_op jit(solution)/shard_map/ppermute | solution.py:390
  56.5 5.2 %collective-permute-start.2 = (bf16[72,256]{1,0:T(8,128)(2,1)S(1)}, bf16[72,256]{1,0:T(8,128)(2,1)S(1)}, u32[]{:S(2)}, u32[]{:S(2)}) collective-permute-start(bf16[72,256]{1,0:T(8,128)(2,1)S(1)} %get-tuple-element.44.theirs_ref), channel_id=1, source_target_pairs={{0,17},{2,19},{4,21},{6,23},{8,25},{10,27},{12,29},{14,31},{16,1},... | collective-permute-start | bytes 110600 | tf_op jit(solution)/shard_map/ppermute | solution.py:567
  61.7 1.4 %copy-start.4 = (f32[1024]{0:T(1024)S(1)}, f32[1024]{0:T(1024)}, u32[]{:S(2)}) copy-start(f32[1024]{0:T(1024)} %param.15) | copy-start | bytes 12292
  61.7 1.4 %collective-permute-start.3 = (bf16[136,256]{1,0:T(8,128)(2,1)S(1)}, bf16[136,256]{1,0:T(8,128)(2,1)S(1)}, u32[]{:S(2)}, u32[]{:S(2)}) collective-permute-start(bf16[136,256]{1,0:T(8,128)(2,1)S(1)} %slots.1.refs_2_), channel_id=1, source_target_pairs={{0,1},{1,0},{2,3},{3,2},{4,5},{5,4},{6,7},{7,6},{8,9},{9,8},{10,11... | collective-permute-start | bytes 208904 | tf_op jit(solution)/shard_map/ppermute | solution.py:390
  61.9 1.2 %collective-permute-start = (f32[1,128]{1,0:T(1,128)S(1)}, f32[1,128]{1,0:T(1,128)S(1)}, u32[]{:S(2)}, u32[]{:S(2)}) collective-permute-start(f32[1,128]{1,0:T(1,128)S(1)} %get-tuple-element.31.refs_0_), channel_id=1, source_target_pairs={{0,1},{1,0},{2,3},{3,2},{4,5},{5,4},{6,7},{7,6},{8,9},{9,8},{10,11... | collective-permute-start | bytes 1544 | tf_op jit(solution)/shard_map/ppermute | solution.py:390

commit v6 on v5

--- a/solution.py
+++ b/solution.py
@@ -126,8 +126,8 @@
 
 
 def part_held(twist, group, replicas, back=0):
-    half = lax.axis_index("shard") // group
-    return lax.rem(lax.axis_index("replica") + half * twist + (replicas - back), replicas)
+    odd = lax.rem(lax.axis_index("shard") * 2 // group, 2)
+    return lax.rem(lax.axis_index("replica") + odd * twist + (replicas - back), replicas)
 
 
 def layer_kernel(
@@ -320,7 +320,7 @@
     owned_ref[2 * rows :] = jnp.concatenate([gains, padding], axis=0).astype(bf16)
 
 
-def adagrad_kernel(twist, group, replicas, *refs):
+def adagrad_kernel(twist, replicas, *refs):
     wanted_refs, grad_refs = refs[:replicas], refs[replicas : 2 * replicas]
     state_ref, update_ref, state_out_ref, gains_ref = refs[2 * replicas :]
     rows = update_ref.shape[0]
@@ -341,11 +341,13 @@
     wanted = [wanted_ref[...] for wanted_ref in wanted_refs]
     grads = [grad_ref[:slots].astype(f32) for grad_ref in grad_refs]
     if twist:
-        start = lax.axis_index("shard") // group * (slots // 2)
-        lane, row = iota((1, slots), 1), iota((slots, 1), 0)
-        here = (lane >= start) & (lane < start + slots // 2)
+        def even(index):
+            quarter = slots // 4
+            return (index < quarter) | ((index >= 2 * quarter) & (index < 3 * quarter))
+
+        here = even(iota((1, slots), 1))
         wanted = [jnp.where(here, *wanted), jnp.where(here, *wanted[::-1])]
-        here = (row >= start) & (row < start + slots // 2)
+        here = even(iota((slots, 1), 0))
         grads = [jnp.where(here, *grads), jnp.where(here, *grads[::-1])]
     for asked, grad, grad_ref in zip(wanted, grads, grad_refs):
         hit = iota((rows, slots), 0) + first == asked.astype(jnp.int32)
@@ -421,13 +423,16 @@
     group = shards // 2
     share_rows = -(-blocks * width // (replicas * group))
     part_rows = share_rows * group
-    in_half = [list(range(group)), list(range(group, shards))]
-    twist = 1 if replicas == 2 else 0
+    twist = 1 if replicas == 2 and shards % 4 == 0 else 0
     both = ("shard", "replica")
-    place = lambda replica, shard: shard * replicas + replica % replicas
-    lookup_groups = [
-        [place(replica + shard // group * twist, shard) for shard in range(shards)]
-        for replica in range(replicas)
+
+    def members(replica, first, last):
+        turned = [(replica + shard * 4 // shards * twist) % replicas for shard in range(first, last)]
+        return [shard * replicas + turn for shard, turn in zip(range(first, last), turned)]
+
+    lookup_groups = [members(replica, 0, shards) for replica in range(replicas)]
+    half_groups = [
+        members(replica, first, first + group) for replica in range(replicas) for first in (0, group)
     ]
     half_slots = group * capacity
     grad_scale = 1.0 / math.sqrt(tokens * shards * replicas)
@@ -479,7 +484,7 @@
 
     cot = cotangent.reshape(tokens, width)
     lifted_grad, normal, gate_grad, left, *parts = pl.pallas_call(
-        functools.partial(layer_kernel, 0, group),
+        functools.partial(layer_kernel, twist, group),
         out_shape=(
             shape((tokens, w_uvqk.shape[1]), bf16),
             shape((tokens, width + 128), f32),
@@ -495,7 +500,7 @@
     )(small, token_hot, same, slot_rows, cot, w_uvqk, w_out)
     came = hand_on([None] + parts)[1:]
     slot_grad, gain_rows, kept = pl.pallas_call(
-        functools.partial(finish_kernel, 0, group, replicas),
+        functools.partial(finish_kernel, twist, group, replicas),
         out_shape=(
             shape((tokens, width), bf16),
             shape((4, width), f32),
@@ -534,7 +539,7 @@
             axis=1,
         )
     arrived = lax.all_to_all(
-        message, "shard", split_axis=0, concat_axis=0, tiled=True, axis_index_groups=in_half
+        message, both, split_axis=0, concat_axis=0, tiled=True, axis_index_groups=half_groups
     )
     if aligned:
         cross, theirs, mine = pl.pallas_call(
@@ -558,13 +563,8 @@
         cross = total[:share_rows].astype(bf16)
         theirs = jnp.concatenate([theirs, gains, padding], axis=0)
     mirror = [(shard, (shard + group) % shards) for shard in range(shards)]
-    turned_mirror = [
-        (place(replica, shard), place(replica + twist, (shard + group) % shards))
-        for replica in range(replicas)
-        for shard in range(shards)
-    ]
     other = lax.ppermute(cross, "shard", mirror)
-    other_slots = lax.ppermute(theirs, both, turned_mirror)
+    other_slots = lax.ppermute(theirs, "shard", mirror)
     if aligned:
         share = pl.pallas_call(
             functools.partial(share_kernel, grad_scale),
@@ -593,7 +593,7 @@
         owned = jnp.concatenate([by_half, gains.astype(bf16), padding], axis=0)
 
     gathered = lax.all_to_all(
-        share, "shard", split_axis=0, concat_axis=0, tiled=True, axis_index_groups=in_half
+        share, both, split_axis=0, concat_axis=0, tiled=True, axis_index_groups=half_groups
     )
 
     wanted_all = from_all(wanted, replicas)
@@ -601,7 +601,7 @@
     lanes = 128
     block = min(rows_dev, 2048 // replicas)
     row_update, state_new, grad_gains = pl.pallas_call(
-        functools.partial(adagrad_kernel, twist, group, replicas),
+        functools.partial(adagrad_kernel, twist, replicas),
         grid=(rows_dev // block,),
         out_shape=(
             shape((rows_dev, width), f32),
@@ -625,7 +625,7 @@
     grads = ()
     for step, half in enumerate(halves):
         grads = pl.pallas_call(
-            functools.partial(spread_kernel, 0, group, step, replicas),
+            functools.partial(spread_kernel, twist, group, step, replicas),
             out_shape=(shape(w_uvqk.shape, f32), shape(w_out.shape, f32)),
             in_specs=[VMEM] + [pl.BlockSpec(memory_space=pl.ANY)] * len(grads),
             out_specs=(pl.BlockSpec(memory_space=pl.ANY),) * 2,

time: 67 us -> 67.5 us (level)
  waiting for transfers between devices: 10.2 us -> 11.1 us
where the time goes in v6:
time: 67.5 us; the launch traced here: 67.2 us
  blocking collectives  45.3 us (67%)
  waiting for transfers between devices  11.1 us (16%)
  Pallas kernels  6.72 us (10%)
  starting transfers between devices  2.67 us (4%)
  between operations  0.76 us (1%)
  local copies, waits for them, and re-layouts  0.71 us (1%)
    all_to_all x1, blocking collectives, on_device(): lax.all_to_all(asked, both, split_axis=0, concat_axis=0, tiled=True, axis...  14.4 us
    all_to_all x1, blocking collectives, on_device(): lax.all_to_all(message, both, split_axis=0, concat_axis=0, tiled=True, ax...  10.8 us
    all_to_all x1, blocking collectives, on_device(): lax.all_to_all(share, both, split_axis=0, concat_axis=0, tiled=True, axis...  10.5 us
    all_to_all x1, blocking collectives, on_device(): lax.all_to_all(found.reshape(shards, capacity, width), both, split_axis=0...  9.55 us
    ppermute x1, waiting for transfers between devices, on_device(): other_slots = lax.ppermute(theirs, 'shard', mirror)  5.03 us
    ppermute x1, waiting for transfers between devices, on_device(): other = lax.ppermute(cross, 'shard', mirror)  4.61 us
    pallas_call x1, Pallas kernels, on_device(): pl.pallas_call(functools.partial(layer_kernel, twist, group), out_shape=(...  1.83 us
    pallas_call x1, Pallas kernels, on_device(): pl.pallas_call(functools.partial(adagrad_kernel, twist, replicas), grid=(...  1.81 us
  transfers between devices with their start and end apart: 6, of which 4 were waited for; matrix products, arithmetic and copies ran while one was open for 0% of the time, Pallas kernels for 5%

profile of v6, /device:TPU:0, one launch (start us, length us, event | category | flops | bytes accessed | tf_op | source)
XLA Modules:
  0.0 67.2 jit_solution(5137594467863179092)
XLA Ops:
  0.6 0.0 copy-start.6
  0.7 0.6 copy-done.6
  1.3 0.0 copy-done.9
  1.3 0.0 copy-done.5
  1.4 0.0 copy-done.7
  1.4 14.4 %all_to_all.20.ids_ref = s32[16,1,128]{2,1,0:T(1,128)S(1)} all-to-all(s32[16,1,128]{2,1,0:T(1,128)S(1)} %get-tuple-element.29), channel_id=1, replica_groups={{0,2,4,6,9,11,13,15,16,18,20,22,25,27,29,31},{1,3,5,7,8,10,12,14,17,19,..., dimensions={0} | all-to-all | bytes 16384 | tf_op jit(solution)/shard_map/all_to_all | solution.py:459
  15.8 0.0 copy-done
  15.8 0.5 fetch.1
  16.3 0.0 copy-start.2
  16.3 9.5 %all_to_all.21 = bf16[16,8,256]{2,1,0:T(8,128)(2,1)S(1)} all-to-all(bf16[16,8,256]{2,1,0:T(8,128)(2,1)S(1)} %bitcast.12), channel_id=1, replica_groups={{0,2,4,6,9,11,13,15,16,18,20,22,25,27,29,31},{1,3,5,7,8,10,12,14,17,19,..., dimensions={0} | all-to-all | bytes 131072 | tf_op jit(solution)/shard_map/all_to_all | solution.py:476
  25.9 0.0 copy-done.3
  25.9 1.8 %layer.1 = (bf16[128,1024]{1,0:T(8,128)(2,1)S(1)}, f32[128,384]{1,0:T(8,128)S(1)}, f32[1,256]{1,0:T(1,128)S(1)}, bf16[512,128]{1,0:T(8,128)(2,1)S(1)}, bf16[640,256]{1,0:T(8,128)(2,1)S(1)}) custom-call(f32[8,256]{1,0:T(8,128)S(1)} %get-tuple-element.30.small_ref, bf16[128,128]{1,0:T(8,128)(2,1)S(1)} %get-tuple-element.32.token_ref, ...), custom_call_target="tpu_custom_call" | custom-call | flops 268435456 | bytes 1310720 | tf_op jit(solution)/shard_map/layer/pallas_call | solution.py:486
  27.7 0.7 %collective-permute-start.1 = (bf16[640,256]{1,0:T(8,128)(2,1)S(1)}, bf16[640,256]{1,0:T(8,128)(2,1)S(1)}, u32[]{:S(2)}, u32[]{:S(2)}) collective-permute-start(bf16[640,256]{1,0:T(8,128)(2,1)S(1)} %get-tuple-element.42), channel_id=1, source_target_pairs={{0,1},{1,0},{2,3},{3,2},{4,5},{5,4},{6,7},{7,6},{8,9},{9,8},{10,11... | collective-permute-start | bytes 983048 | tf_op jit(solution)/shard_map/ppermute | solution.py:392
  28.5 0.6 finish.1
  29.1 0.6 collective-permute-done.1.refs_1_
  29.7 0.1 pack.1
  29.8 10.8 %all_to_all.22.in_ref = bf16[8,200,128]{2,1,0:T(8,128)(2,1)S(1)} all-to-all(bf16[8,200,128]{2,1,0:T(8,128)(2,1)S(1)} %pack.1), channel_id=1, replica_groups={{0,2,4,6,9,11,13,15},{16,18,20,22,25,27,29,31},{1,3,5,7,8,10,12,14},{17..., dimensions={0} | all-to-all | bytes 819200 | tf_op jit(solution)/shard_map/all_to_all | solution.py:541
  40.6 0.1 cross.1
  40.7 0.8 %collective-permute-start.4 = (bf16[80,256]{1,0:T(8,128)(2,1)S(1)}, bf16[80,256]{1,0:T(8,128)(2,1)S(1)}, u32[]{:S(2)}, u32[]{:S(2)}) collective-permute-start(bf16[80,256]{1,0:T(8,128)(2,1)S(1)} %get-tuple-element.47.mine_ref), channel_id=1, source_target_pairs={{0,16},{2,18},{4,20},{6,22},{8,24},{10,26},{12,28},{14,30},{16,0},... | collective-permute-start | bytes 122888 | tf_op jit(solution)/shard_map/ppermute | solution.py:566
  41.5 4.6 %collective-permute-done.4.other_ref = bf16[80,256]{1,0:T(8,128)(2,1)S(1)} collective-permute-done((bf16[80,256]{1,0:T(8,128)(2,1)S(1)}, bf16[80,256]{1,0:T(8,128)(2,1)S(1)}, u32[]{:S(2)}, u32[]{:S(2)}) %collective-permute-start.4) | collective-permute-done | bytes 40992 | tf_op jit(solution)/shard_map/ppermute | solution.py:566
  46.1 10.5 %all_to_all.23 = bf16[8,80,256]{2,1,0:T(8,128)(2,1)S(1)} all-to-all(bf16[8,80,256]{2,1,0:T(8,128)(2,1)S(1)} %share.1), channel_id=1, replica_groups={{0,2,4,6,9,11,13,15},{16,18,20,22,25,27,29,31},{1,3,5,7,8,10,12,14},{17..., dimensions={0} | all-to-all | bytes 655360 | tf_op jit(solution)/shard_map/all_to_all | solution.py:595
  56.6 0.2 collective-permute-start.5
  56.8 0.4 collective-permute-start.2
  57.1 5.0 %collective-permute-done.2.other_ref = bf16[72,256]{1,0:T(8,128)(2,1)S(1)} collective-permute-done((bf16[72,256]{1,0:T(8,128)(2,1)S(1)}, bf16[72,256]{1,0:T(8,128)(2,1)S(1)}, u32[]{:S(2)}, u32[]{:S(2)}) %collective-permute-start.2) | collective-permute-done | bytes 36896 | tf_op jit(solution)/shard_map/ppermute | solution.py:567
  62.2 0.1 collective-permute-start.3
  62.3 0.5 collective-permute-start
  62.8 0.8 %collective-permute-done.refs_1_ = f32[1,128]{1,0:T(1,128)S(1)} collective-permute-done((f32[1,128]{1,0:T(1,128)S(1)}, f32[1,128]{1,0:T(1,128)S(1)}, u32[]{:S(2)}, u32[]{:S(2)}) %collective-permute-start) | collective-permute-done | bytes 544 | tf_op jit(solution)/shard_map/ppermute | solution.py:392
  63.6 0.0 collective-permute-done.3.refs_3_
  63.6 1.8 %adagrad.1 = (f32[1024,256]{1,0:T(8,128)}, f32[8,1,128]{2,1,0:T(1,128)}, f32[2,256]{1,0:T(2,128)}) custom-call(f32[1,128]{1,0:T(1,128)S(1)} %get-tuple-element.31.refs_0_, f32[1,128]{1,0:T(1,128)S(1)} %collective-permute-done.refs_1_, bf16[136,256]{1,0:T(8,128)(2,1)S(1)} %slots.1.refs_2_, bf16[136,256]{1,0:T(8,128)(2,1)S(1)} %collective-permute-done.3.refs_3_, ...), custom_call_target="tpu_custom_call" | custom-call | flops 134217728 | bytes 1048576 | tf_op jit(solution)/shard_map/adagrad/pallas_call | solution.py:603
  65.4 0.9 %shard_map.137 = (f32[256,1024]{1,0:T(8,128)}, f32[256,256]{1,0:T(8,128)}) custom-call(bf16[640,256]{1,0:T(8,128)(2,1)S(1)} %bitcast.10), custom_call_target="tpu_custom_call" | custom-call | flops 327680 | bytes 983040 | tf_op jit(solution)/shard_map/pallas_call | solution.py:627
  66.3 0.0 collective-permute-done.5.part_ref
  66.3 0.9 %shard_map.138 = (f32[256,1024]{1,0:T(8,128)}, f32[256,256]{1,0:T(8,128)}) custom-call(bf16[640,256]{1,0:T(8,128)(2,1)S(1)} %collective-permute-done.5.part_ref, f32[256,1024]{1,0:T(8,128)} %get-tuple-element.48.refs_0_, f32[256,256]{1,0:T(8,128)} %get-tuple-element.49.refs_1_), custom_call_target="tpu_custom_call", output_to_operand_aliasing={{0}: (1, {}), {1}: (2, {})} | custom-call | flops 327680 | bytes 983040 | tf_op jit(solution)/shard_map/pallas_call | solution.py:627
  (15 shorter events, 0.1 us)
Async XLA Ops:
  0.6 0.7 %copy-start.6 = (f32[256]{0:T(256)S(1)}, f32[256]{0:T(256)}, u32[]{:S(2)}) copy-start(f32[256]{0:T(256)} %param.19) | copy-start | bytes 3076
  0.6 0.7 %copy-start.8 = (s32[1,128]{1,0:T(1,128)S(1)}, s32[1,128]{1,0:T(1,128)}, u32[]{:S(2)}) copy-start(s32[1,128]{1,0:T(1,128)} %slot_ref.1) | copy-start | bytes 1540
  0.7 0.7 copy-start.9
  0.7 0.7 %copy-start.5 = (f32[256]{0:T(256)S(1)}, f32[256]{0:T(256)}, u32[]{:S(2)}) copy-start(f32[256]{0:T(256)} %param.18) | copy-start | bytes 3076
  0.7 0.7 %copy-start.7 = (s32[1,1,128]{2,1,0:T(1,128)S(1)}, s32[1,1,128]{2,1,0:T(1,128)}, u32[]{:S(2)}) copy-start(s32[1,1,128]{2,1,0:T(1,128)} %asked_ref.1) | copy-start | bytes 1540
  1.4 14.5 %copy-start = (f32[1024,256]{1,0:T(8,128)S(1)}, f32[1024,256]{1,0:T(8,128)}, u32[]{:S(2)}) copy-start(f32[1024,256]{1,0:T(8,128)} %table_ref.1) | copy-start | bytes 3145732
  15.8 10.1 %copy-start.1 = (bf16[256,1024]{1,0:T(8,128)(2,1)S(1)}, bf16[256,1024]{1,0:T(8,128)(2,1)}, u32[]{:S(2)}) copy-start(bf16[256,1024]{1,0:T(8,128)(2,1)} %w_ref.3) | copy-start | bytes 1572868
  15.8 10.1 %copy-start.3 = (bf16[256,256]{1,0:T(8,128)(2,1)S(1)}, bf16[256,256]{1,0:T(8,128)(2,1)}, u32[]{:S(2)}) copy-start(bf16[256,256]{1,0:T(8,128)(2,1)} %wo_ref.1) | copy-start | bytes 393220
  16.3 9.6 %copy-start.2 = (bf16[1,128,256]{2,1,0:T(8,128)(2,1)S(1)}, bf16[1,128,256]{2,1,0:T(8,128)(2,1)}, u32[]{:S(2)}) copy-start(bf16[1,128,256]{2,1,0:T(8,128)(2,1)} %param.13) | copy-start | bytes 196612
  27.7 2.0 %collective-permute-start.1 = (bf16[640,256]{1,0:T(8,128)(2,1)S(1)}, bf16[640,256]{1,0:T(8,128)(2,1)S(1)}, u32[]{:S(2)}, u32[]{:S(2)}) collective-permute-start(bf16[640,256]{1,0:T(8,128)(2,1)S(1)} %get-tuple-element.42), channel_id=1, source_target_pairs={{0,1},{1,0},{2,3},{3,2},{4,5},{5,4},{6,7},{7,6},{8,9},{9,8},{10,11... | collective-permute-start | bytes 983048 | tf_op jit(solution)/shard_map/ppermute | solution.py:392
  40.7 5.4 %collective-permute-start.4 = (bf16[80,256]{1,0:T(8,128)(2,1)S(1)}, bf16[80,256]{1,0:T(8,128)(2,1)S(1)}, u32[]{:S(2)}, u32[]{:S(2)}) collective-permute-start(bf16[80,256]{1,0:T(8,128)(2,1)S(1)} %get-tuple-element.47.mine_ref), channel_id=1, source_target_pairs={{0,16},{2,18},{4,20},{6,22},{8,24},{10,26},{12,28},{14,30},{16,0},... | collective-permute-start | bytes 122888 | tf_op jit(solution)/shard_map/ppermute | solution.py:566
  56.6 9.7 %collective-permute-start.5 = (bf16[640,256]{1,0:T(8,128)(2,1)S(1)}, bf16[640,256]{1,0:T(8,128)(2,1)S(1)}, u32[]{:S(2)}, u32[]{:S(2)}) collective-permute-start(bf16[640,256]{1,0:T(8,128)(2,1)S(1)} %bitcast.9), channel_id=1, source_target_pairs={{0,1},{1,0},{2,3},{3,2},{4,5},{5,4},{6,7},{7,6},{8,9},{9,8},{10,11... | collective-permute-start | bytes 983048 | tf_op jit(solution)/shard_map/ppermute | solution.py:392
  56.8 5.4 %collective-permute-start.2 = (bf16[72,256]{1,0:T(8,128)(2,1)S(1)}, bf16[72,256]{1,0:T(8,128)(2,1)S(1)}, u32[]{:S(2)}, u32[]{:S(2)}) collective-permute-start(bf16[72,256]{1,0:T(8,128)(2,1)S(1)} %get-tuple-element.44.theirs_ref), channel_id=1, source_target_pairs={{0,16},{2,18},{4,20},{6,22},{8,24},{10,26},{12,28},{14,30},{16,0},... | collective-permute-start | bytes 110600 | tf_op jit(solution)/shard_map/ppermute | solution.py:567
  62.2 1.4 %copy-start.4 = (f32[1024]{0:T(1024)S(1)}, f32[1024]{0:T(1024)}, u32[]{:S(2)}) copy-start(f32[1024]{0:T(1024)} %param.15) | copy-start | bytes 12292
  62.2 1.4 %collective-permute-start.3 = (bf16[136,256]{1,0:T(8,128)(2,1)S(1)}, bf16[136,256]{1,0:T(8,128)(2,1)S(1)}, u32[]{:S(2)}, u32[]{:S(2)}) collective-permute-start(bf16[136,256]{1,0:T(8,128)(2,1)S(1)} %slots.1.refs_2_), channel_id=1, source_target_pairs={{0,1},{1,0},{2,3},{3,2},{4,5},{5,4},{6,7},{7,6},{8,9},{9,8},{10,11... | collective-permute-start | bytes 208904 | tf_op jit(solution)/shard_map/ppermute | solution.py:392
  62.3 1.3 %collective-permute-start = (f32[1,128]{1,0:T(1,128)S(1)}, f32[1,128]{1,0:T(1,128)S(1)}, u32[]{:S(2)}, u32[]{:S(2)}) collective-permute-start(f32[1,128]{1,0:T(1,128)S(1)} %get-tuple-element.31.refs_0_), channel_id=1, source_target_pairs={{0,1},{1,0},{2,3},{3,2},{4,5},{5,4},{6,7},{7,6},{8,9},{9,8},{10,11... | collective-permute-start | bytes 1544 | tf_op jit(solution)/shard_map/ppermute | solution.py:392
